TPU v7x, 128 devices: a whole 4x4x4 slice. The times are simulated.
128 devices in a mesh: row: 16 (over y, x), col: 8 (over z, core).
Axes of the slice: x: 4, y: 4, z: 4, core: 2. Of those that a mesh axis runs over, the one named last changes fastest.
Arguments:
- tangents: float32 [192, 128, 6144], P('row', None, 'col'), may hold values from -6 to 6
- base_flow: float32 [192, 128, 192], P('row', None, 'col'), may hold values from -0.0625 to 0.0625
- mode_mask: int32 [192, 192], P('row', 'col'), may hold values 0 or 1
- decay_rates: float32 [128], replicated, may hold values from 1 to 100
- to_eigen: float32 [128, 128], replicated, may hold values from -0.5 to 0.5
- from_eigen: float32 [128, 128], replicated, may hold values from -0.5 to 0.5
Outputs:
- vectors: float32 [192, 128, 6144], P('row', None, 'col')
- growth: float32 [32], replicated
Inputs may be any that keep to these rules, and one draw needn't show every extreme that they name: `mode_mask`: 1 keeps a mode pair of the linearized product, 0 removes it.
All inputs are finite; a program needn't handle non-finite values. No bound on the sum of `mode_mask` on one device may be relied on, other than what follows from the above.
Results may differ from a plain program's by a relative error of at most 0.00005.
Values sent between devices are 32-bit elements; how exact they have to be, the bound alone decides.
No kernel may reach another device: no remote copies, remote signals or barrier semaphores. Data moves between devices by JAX's collectives and lax.ppermute only.
A program may use at most 128 MiB of HBM per device.

v0:
```python
import math

import jax
import jax.numpy as jnp
from jax import lax
from jax.sharding import PartitionSpec as P

PRECISE = lax.Precision.HIGHEST
STEP_COEF = 10.0
VISCOSITY = 0.01
ALPHA_X = 0.5
BETA_Z = 1.0


def side_by_side(arrays, axis, split_dim, concat_dim, along):
    widths = [a.shape[along] for a in arrays]
    both = jnp.concatenate(arrays, axis=along)
    out = lax.all_to_all(both, axis, split_axis=split_dim, concat_axis=concat_dim, tiled=True)
    return tuple(jnp.split(out, [sum(widths[:k]) for k in range(1, len(widths))], axis=along))


def total_of_pieces(shard, axis):
    return lax.all_gather(shard, axis).sum(0)


def local_waves(points_count, first_index, length):
    indices = first_index + jnp.arange(length, dtype=jnp.int32)
    middle = points_count // 2
    return jnp.where(indices <= middle, indices, indices - middle).astype(jnp.float32)


def synthesis(points_count):
    points = jnp.arange(points_count, dtype=jnp.int32)[:, None]
    mode_index = jnp.arange(points_count, dtype=jnp.int32)[None, :]
    middle = points_count // 2
    wave_index = jnp.where(mode_index <= middle, mode_index, mode_index - middle)
    turn_count = (points * wave_index % points_count).astype(jnp.float32)
    angles = turn_count * (2.0 * math.pi / points_count)
    return jnp.where(mode_index <= middle, jnp.cos(angles), jnp.sin(angles))


def analysis(points_count):
    mode_index = jnp.arange(points_count, dtype=jnp.int32)
    middle = points_count // 2
    weights = jnp.where(
        (mode_index == 0) | (mode_index == middle),
        jnp.float32(1.0 / points_count),
        jnp.float32(2.0 / points_count),
    )
    return weights[:, None] * synthesis(points_count).T


def derivative_analysis(points_count, wave_scale):
    rows_index = jnp.arange(points_count, dtype=jnp.int32)[:, None]
    cols_index = jnp.arange(points_count, dtype=jnp.int32)[None, :]
    middle = points_count // 2
    rising = (cols_index == rows_index + middle) & (rows_index >= 1) & (rows_index < middle)
    falling = (rows_index == cols_index + middle) & (cols_index >= 1) & (cols_index < middle)
    rows_float = jnp.broadcast_to(rows_index.astype(jnp.float32), (points_count, points_count))
    cols_float = jnp.broadcast_to(cols_index.astype(jnp.float32), (points_count, points_count))
    derivative = jnp.where(rising, rows_float, jnp.float32(0.0)) - jnp.where(
        falling, cols_float, jnp.float32(0.0)
    )
    return -wave_scale * jnp.dot(derivative, analysis(points_count), precision=PRECISE)


def denominators(decay_rates, x_count, z_count, x_start, z_start, x_length, z_length):
    wave_x = ALPHA_X * local_waves(x_count, x_start, x_length)
    wave_z = BETA_Z * local_waves(z_count, z_start, z_length)
    return (
        STEP_COEF
        + VISCOSITY * (wave_x[:, None, None] ** 2 + wave_z[None, None, :] ** 2)
        + decay_rates[None, :, None]
    )


def body(tangents, base_flow, mode_mask, decay_rates, to_eigen, from_eigen):
    x_length, y_count, zv_length = tangents.shape
    z_length = base_flow.shape[2]
    vec_count = zv_length // z_length
    row_devices = lax.axis_size("row")
    col_devices = lax.axis_size("col")
    x_count = x_length * row_devices
    z_count = z_length * col_devices
    x_synthesis = synthesis(x_count)
    z_synthesis = synthesis(z_count)
    x_derivative = derivative_analysis(x_count, ALPHA_X)
    z_analysis = analysis(z_count)
    all_devices = row_devices * col_devices
    plane_count = y_count // all_devices
    stacked = tangents.reshape(x_length, y_count, 1, zv_length)
    speed_stack = base_flow.reshape(x_length, y_count, 1, z_length)
    planes, speed_field = side_by_side((stacked, speed_stack), ("row", "col"), 1, 2, 3)
    x_table = x_synthesis.reshape(x_count, row_devices, x_length)
    z_table = z_synthesis.reshape(z_count, col_devices, z_length)
    planes = planes.reshape(x_length, plane_count, row_devices, col_devices, z_length, vec_count)
    physical = jnp.einsum("myrcnv,prm->ypcnv", planes, x_table, precision=PRECISE)
    physical = jnp.einsum("ypcnv,scn->ypsv", physical, z_table, precision=PRECISE)
    speed_field = speed_field.reshape(x_length, plane_count, row_devices, col_devices, z_length)
    speed_field = jnp.einsum("myrcn,prm->ypcn", speed_field, x_table, precision=PRECISE)
    speed_field = jnp.einsum("ypcn,scn->yps", speed_field, z_table, precision=PRECISE)
    product = physical * speed_field[:, :, :, None]
    returned = jnp.einsum("ypsv,ns->ypnv", product, z_analysis, precision=PRECISE)
    returned = jnp.einsum("ypnv,mp->ymnv", returned, x_derivative, precision=PRECISE)
    returned = returned.reshape(
        plane_count, row_devices, x_length, col_devices, z_length, vec_count
    )
    returned = jnp.transpose(returned, (2, 0, 1, 3, 4, 5)).reshape(
        x_length, plane_count, all_devices, zv_length
    )
    nonlinear = lax.all_to_all(returned, ("row", "col"), split_axis=2, concat_axis=1, tiled=True)
    nonlinear = nonlinear.reshape(x_length, y_count, zv_length)
    x_start = lax.axis_index("row") * x_length
    z_start = lax.axis_index("col") * z_length
    divisor = denominators(decay_rates, x_count, z_count, x_start, z_start, x_length, z_length)
    retained = mode_mask.astype(jnp.float32)[:, None, :, None]
    nonlinear = nonlinear.reshape(x_length, y_count, z_length, vec_count) * retained
    right_side = STEP_COEF * tangents.reshape(x_length, y_count, z_length, vec_count) + nonlinear
    eigen_part = jnp.einsum(
        "ji,mic->mjc", to_eigen, right_side.reshape(x_length, y_count, zv_length), precision=PRECISE
    )
    eigen_part = eigen_part.reshape(x_length, y_count, z_length, vec_count) / divisor[:, :, :, None]
    stepped = jnp.einsum(
        "yj,mjc->myc",
        from_eigen,
        eigen_part.reshape(x_length, y_count, zv_length),
        precision=PRECISE,
    )
    columns = stepped.reshape(x_length * y_count * z_length, vec_count)
    cell_count = x_count * y_count * z_count
    identity = jnp.eye(vec_count, dtype=jnp.float32)
    local_gram = jnp.einsum("cv,cu->vu", columns, columns, precision=PRECISE)
    gram_matrix = total_of_pieces(local_gram, ("row", "col")) / cell_count
    lower_factor = jnp.linalg.cholesky(gram_matrix)
    inverse = jax.scipy.linalg.solve_triangular(lower_factor, identity, lower=True)
    orthonormal = jnp.einsum("cv,uv->cu", columns, inverse, precision=PRECISE)
    growth = jnp.log(jnp.diagonal(lower_factor))
    return (orthonormal.reshape(x_length, y_count, zv_length), growth)


def solution(mesh):
    placed = (P("row", None, "col"), P("row", None, "col"), P("row", "col"), P(), P(), P())
    return jax.shard_map(
        body, mesh=mesh, in_specs=placed, out_specs=(P("row", None, "col"), P()), check_vma=False
    )
```

profile of v0, /device:TPU:1, one launch (start us, length us, event | category | flops | bytes accessed | tf_op | source)
XLA Modules:
  0.0 461.6 jit_solution(4813068991455559650)
XLA Ops:
  0.6 1.2 copy.71
  1.9 2.7 pad_maximum_fusion
  4.6 6.9 %copy.72 = f32[12,128,1,792]{3,2,0,1:T(1,128)} copy(f32[12,128,1,792]{3,1,0,2:T(8,128)S(1)} %pad_maximum_fusion) | data formatting | bytes 9732096 | tf_op jit(solution)/shard_map/concatenate | solution.py:17
  11.5 11.9 %all-to-all-start = ((f32[12,128,1,792]{3,2,0,1:T(1,128)}), f32[12,128,1,792]{3,2,0,1:T(1,128)}, u32[]{:S(2)}, u32[]{:S(2)}) async-start(f32[12,128,1,792]{3,2,0,1:T(1,128)} %copy.72), calls=%async_computation | async-start | bytes 11010048 | tf_op jit(solution)/shard_map/all_to_all | solution.py:18
  23.5 1.3 convolution_multiply_fusion
  24.9 65.9 %all-to-all-done = f32[12,128,1,792]{3,2,0,1:T(1,128)} async-done(((f32[12,128,1,792]{3,2,0,1:T(1,128)}), f32[12,128,1,792]{3,2,0,1:T(1,128)}, u32[]{:S(2)}, u32[]{:S(2)}) %all-to-all-start) | async-done | bytes 4866080 | tf_op jit(solution)/shard_map/all_to_all | solution.py:18
  90.8 3.0 copy.116
  93.9 2.6 split.8
  96.5 12.4 %reshape.260 = f32[12,16,8,24,32]{4,3,2,1,0:T(8,128)} reshape(f32[12,1,128,768]{3,2,0,1:T(8,128)} %split.8) | data formatting | bytes 9437184 | tf_op jit(solution)/shard_map/reshape.8
  108.9 26.0 %copy.74 = f32[12,16,8,24,32]{3,1,0,2,4:T(8,128)} copy(f32[12,16,8,24,32]{4,3,2,1,0:T(8,128)} %reshape.260) | data formatting | bytes 9437184 | tf_op jit(solution)/shard_map/reshape.8
  134.9 2.2 convolution_bitcast_fusion.3
  137.1 46.5 %fusion.23 = f32[192,8,24,32,1]{0,2,4,1,3:T(8,128)S(1)} fusion(f32[12,16,8,24,32]{3,1,0,2,4:T(8,128)} %copy.74, s32[16,12]{0,1:T(8,128)S(1)} %add_select_fusion.3, pred[16,12]{0,1:T(8,128)(4,1)S(1)} %fusion.92), kind=kOutput, calls=%fused_computation.36 | convolution fusion | flops 2718277632 | bytes 9438144 | tf_op jit(solution)/shard_map/myrcnv,prm->ypcnv/dot_general | solution.py:97
  183.6 1.4 convolution_bitcast_fusion.2
  185.0 7.3 %fusion.4 = f32[192,192,32,1]{1,0,3,2:T(8,128)S(1)} fusion(f32[192,8,24,32,1]{0,2,4,1,3:T(8,128)S(1)} %fusion.23, s32[8,24]{1,0:T(8,128)S(1)} %add_select_fusion.4, pred[8,24]{1,0:T(8,128)(4,1)S(1)} %fusion.93), kind=kOutput, calls=%fused_computation.6 | convolution fusion | flops 2718277632 | bytes 9438144 | tf_op jit(solution)/shard_map/ypcnv,scn->ypsv/dot_general | solution.py:98
  192.4 6.6 %fusion.1 = f32[192,192,32]{1,0,2:T(8,128)S(1)} fusion(f32[192,192,32,1]{1,0,3,2:T(8,128)S(1)} %fusion.4, f32[192,192]{0,1:T(8,128)S(1)} %convolution_bitcast_fusion.2, s32[192]{0:T(256)S(1)} %get-tuple-element.4, f32[192]{0:T(256)S(1)} %or_select_fusion, pred[192]{0:T(512)(128)(4,1)S(1)} %get-tuple-element.6), kind=kOutput, calls=%fused_computation.4 | convolution fusion | flops 2719494144 | bytes 9586368 | tf_op jit(solution)/shard_map/ypsv,ns->ypnv/dot_general | solution.py:103
  199.0 17.5 %convolution_bitcast_fusion = f32[12,1,16,8,24,32]{5,2,4,3,0,1:T(8,128)S(1)} fusion(f32[8,24,32,192]{3,1,0,2:T(8,128)S(1)} %bitcast.105, f32[16,12,192,1,1]{2,1,0,4,3:T(8,128)S(1)} %bitcast.110), kind=kOutput, calls=%fused_computation.1 | convolution fusion | flops 2717908992 | bytes 9584640 | tf_op jit(solution)/shard_map/ypnv,mp->ymnv/dot_general | solution.py:104
  216.5 12.1 %copy.99 = f32[12,1,16,8,24,32]{5,4,0,3,2,1:T(8,128)} copy(f32[12,1,16,8,24,32]{5,2,4,3,0,1:T(8,128)S(1)} %convolution_bitcast_fusion) | data formatting | bytes 9437184 | tf_op jit(solution)/shard_map/reshape | solution.py:108
  228.6 15.4 %reshape.286 = f32[12,1,128,768]{3,1,0,2:T(1,128)} reshape(f32[12,1,16,8,24,32]{5,4,0,3,2,1:T(8,128)} %copy.99) | data formatting | bytes 9437184 | tf_op jit(solution)/shard_map/reshape | solution.py:108
  244.1 7.8 %all-to-all-start.1 = ((f32[12,1,128,768]{3,1,0,2:T(1,128)}), f32[12,1,128,768]{3,1,0,2:T(1,128)}, u32[]{:S(2)}, u32[]{:S(2)}) async-start(f32[12,1,128,768]{3,1,0,2:T(1,128)} %reshape.286), calls=%async_computation.1 | async-start | bytes 9437184 | tf_op jit(solution)/shard_map/all_to_all | solution.py:111
  252.4 57.7 %all-to-all-done.1 = f32[12,1,128,768]{3,1,0,2:T(1,128)} async-done(((f32[12,1,128,768]{3,1,0,2:T(1,128)}), f32[12,1,128,768]{3,1,0,2:T(1,128)}, u32[]{:S(2)}, u32[]{:S(2)}) %all-to-all-start.1) | async-done | bytes 4718624 | tf_op jit(solution)/shard_map/all_to_all | solution.py:111
  310.1 10.3 %bitcast_divide_fusion = f32[12,128,768]{1,2,0:T(8,128)S(1)} fusion(f32[12,128,24]{1,2,0:T(8,128)S(1)} %broadcast_add_fusion, f32[128,128]{1,0:T(8,128)S(1)} %copy-done, f32[12,1,128,768]{3,1,0,2:T(1,128)} %all-to-all-done.1, f32[12,128,768]{2,1,0:T(8,128)} %param.6, f32[12,768]{1,0:T(8,128)S(1)} %mul.176), kind=kOutput, calls=%fused_computation.11 | convolution fusion | flops 1816657920 | bytes 14405632 | tf_op jit(solution)/shard_map/ji,mic->mjc/dot_general | solution.py:119
  320.4 5.4 %convolution_bitcast_fusion.1 = f32[12,128,768]{1,2,0:T(8,128)} fusion(f32[12,128,768]{1,2,0:T(8,128)S(1)} %bitcast_divide_fusion, f32[128,128]{1,0:T(8,128)S(1)} %copy-done.1), kind=kOutput, calls=%fused_computation.20 | convolution fusion | flops 1811939328 | bytes 9502720 | tf_op jit(solution)/shard_map/yj,mjc->myc/dot_general | solution.py:123
  325.8 6.1 %copy.84 = f32[12,128,768]{2,1,0:T(8,128)} copy(f32[12,128,768]{1,2,0:T(8,128)} %convolution_bitcast_fusion.1) | data formatting | bytes 9437184 | tf_op jit(solution)/shard_map/yj,mjc->myc/transpose | solution.py:123
  331.9 12.5 %reshape.265 = f32[36864,32]{1,0:T(8,128)} reshape(f32[12,128,768]{2,1,0:T(8,128)} %copy.84) | data formatting | bytes 9437184 | tf_op jit(solution)/shard_map/reshape | solution.py:129
  344.4 38.1 %fusion.119 = f32[32,32]{1,0:T(8,128)S(1)} fusion(f32[36864,32]{1,0:T(8,128)} %reshape.265), kind=kOutput, calls=%fused_computation.162 | convolution fusion | flops 452984832 | bytes 4722688 | tf_op jit(solution)/shard_map/cv,cu->vu/dot_general | solution.py:132
  382.5 36.7 %all-gather = f32[4096,32]{1,0:T(8,128)S(1)} all-gather(f32[32,32]{1,0:T(8,128)S(1)} %fusion.119), channel_id=2, replica_groups=mesh['row'=16,'col'=8] {'row','col'}, dimensions={0}, use_global_device_ids=true | all-gather | bytes 528384 | tf_op jit(solution)/shard_map/all_gather | solution.py:23
  419.5 2.9 cholesky.17
  423.1 0.7 select_bitcast_fusion
  423.8 2.4 custom-call.7
  426.4 20.1 %fusion.120 = f32[36864,32]{1,0:T(8,128)} fusion(f32[36864,32]{1,0:T(8,128)} %reshape.265, f32[32,32]{1,0:T(8,128)S(1)} %fusion.89), kind=kOutput, calls=%fused_computation.163 | convolution fusion | flops 452984832 | bytes 9441280 | tf_op jit(solution)/shard_map/cv,uv->cu/dot_general | solution.py:136
  446.5 13.6 %reshape.266 = f32[12,128,768]{2,1,0:T(8,128)} reshape(f32[36864,32]{1,0:T(8,128)} %fusion.120) | data formatting | bytes 9437184 | tf_op jit(solution)/shard_map/reshape | solution.py:138
  460.2 0.7 gather_fusion
  (36 shorter events, 2.3 us)
Async XLA Ops:
  0.6 309.5 %copy-start = (f32[128,128]{1,0:T(8,128)S(1)}, f32[128,128]{1,0:T(8,128)}, u32[]{:S(2)}) copy-start(f32[128,128]{1,0:T(8,128)} %param.10) | copy-start | bytes 196612
  11.5 79.2 %all-to-all-start = ((f32[12,128,1,792]{3,2,0,1:T(1,128)}), f32[12,128,1,792]{3,2,0,1:T(1,128)}, u32[]{:S(2)}, u32[]{:S(2)}) async-start(f32[12,128,1,792]{3,2,0,1:T(1,128)} %copy.72), calls=%async_computation | async-start | bytes 11010048 | tf_op jit(solution)/shard_map/all_to_all | solution.py:18
  244.0 7.8 %copy-start.2 = (s32[12,24]{1,0:T(8,128)S(1)}, s32[12,24]{1,0:T(8,128)}, u32[]{:S(2)}) copy-start(s32[12,24]{1,0:T(8,128)} %param.8) | copy-start | bytes 3460
  244.0 8.2 %copy-start.3 = (f32[128]{0:T(128)S(1)}, f32[128]{0:T(128)}, u32[]{:S(2)}) copy-start(f32[128]{0:T(128)} %param.9) | copy-start | bytes 1540
  244.1 66.0 %all-to-all-start.1 = ((f32[12,1,128,768]{3,1,0,2:T(1,128)}), f32[12,1,128,768]{3,1,0,2:T(1,128)}, u32[]{:S(2)}, u32[]{:S(2)}) async-start(f32[12,1,128,768]{3,1,0,2:T(1,128)} %reshape.286), calls=%async_computation.1 | async-start | bytes 9437184 | tf_op jit(solution)/shard_map/all_to_all | solution.py:111
  252.4 68.0 %copy-start.1 = (f32[128,128]{1,0:T(8,128)S(1)}, f32[128,128]{1,0:T(8,128)}, u32[]{:S(2)}) copy-start(f32[128,128]{1,0:T(8,128)} %param.11) | copy-start | bytes 196612
where the time goes:
time: 469 us; the launch traced here: 462 us
  matrix products  157 us (33%)
  waiting for transfers between devices  124 us (26%)
  local copies, waits for them, and re-layouts  114 us (24%)
  blocking collectives  36.7 us (8%)
  starting transfers between devices  19.7 us (4%)
  other arithmetic  9.9 us (2%)
    all_to_all x1, waiting for transfers between devices, side_by_side(): lax.all_to_all(both, axis, split_axis=split_dim, concat_axis=concat_dim,...  65.9 us
    all_to_all x1, waiting for transfers between devices, body(): lax.all_to_all(returned, ('row', 'col'), split_axis=2, concat_axis=1, til...  57.7 us
    dot_general x1, matrix products, body(): jnp.einsum('myrcnv,prm->ypcnv', planes, x_table, precision=PRECISE)  46.5 us
    another operation x4, local copies, waits for them, and re-layouts  38.6 us
    dot_general x1, matrix products, body(): local_gram = jnp.einsum('cv,cu->vu', columns, columns, precision=PRECISE)  38.1 us
    all_gather x1, blocking collectives, total_of_pieces(): return lax.all_gather(shard, axis).sum(0)  36.7 us
    reshape x2, local copies, waits for them, and re-layouts, body(): jnp.transpose(returned, (2, 0, 1, 3, 4, 5))  27.5 us
    dot_general x1, matrix products, body(): orthonormal = jnp.einsum('cv,uv->cu', columns, inverse, precision=PRECISE)  20.1 us
  transfers between devices with their start and end apart: 2, of which 2 were waited for; matrix products, arithmetic and copies ran while one was open for 0% of the time, Pallas kernels for 0%

commit v1 on v0

v1 whole, which is shorter than its diff:
```python
import functools

import jax
import jax.numpy as jnp
import numpy as np
from jax import lax
from jax.experimental import pallas as pl
from jax.experimental.pallas import tpu as pltpu
from jax.sharding import PartitionSpec as P

STEP_COEF = 10.0
VISCOSITY = 0.01
ALPHA_X = 0.5
BETA_Z = 1.0
LANES = 128
F32 = jnp.float32
BF16 = jnp.bfloat16
NN = (((1,), (0,)), ((), ()))
NT = (((1,), (1,)), ((), ()))
TN = (((0,), (0,)), ((), ()))


def synthesis(count):
    points = np.arange(count)[:, None]
    modes = np.arange(count)[None, :]
    middle = count // 2
    waves = np.where(modes <= middle, modes, modes - middle)
    angles = (points * waves % count) * (2.0 * np.pi / count)
    return np.where(modes <= middle, np.cos(angles), np.sin(angles))


def analysis(count):
    modes = np.arange(count)
    weights = np.where((modes == 0) | (modes == count // 2), 1.0 / count, 2.0 / count)
    return weights[:, None] * synthesis(count).T


def derivative_analysis(count, scale):
    middle = count // 2
    derivative = np.zeros((count, count))
    for k in range(1, middle):
        derivative[k, middle + k] = k
        derivative[middle + k, k] = -k
    return -scale * (derivative @ analysis(count))


def halves_of_table(table):
    table = np.asarray(table, np.float64)
    high = table.astype(np.float32).astype(jnp.bfloat16)
    low = (table - high.astype(np.float64)).astype(np.float32).astype(jnp.bfloat16)
    return np.stack([high, low])


def split(x):
    high = x.astype(BF16)
    return high, (x - high.astype(F32)).astype(BF16)


def dot(a, b, dims):
    return lax.dot_general(a, b, dims, preferred_element_type=F32)


def dot3(a, b, dims):
    return dot(a[0], b[0], dims) + (dot(a[0], b[1], dims) + dot(a[1], b[0], dims))


def pack_kernel(q_ref, out_ref, *, rows, modes, planes, tiles):
    def step(m, carry):
        for nb in range(tiles):
            out_ref[pl.ds(nb * modes + m, planes, stride=rows), :] = q_ref[
                m, :, nb * LANES : (nb + 1) * LANES
            ]
        return carry

    lax.fori_loop(0, modes, step, 0)


def transform_kernel(
    d_ref, speed_ref, sx_ref, sz_ref, az_ref, g_ref, out_ref, *y_refs,
    rows, modes, row_devices, col_devices, tiles, vecs,
):
    count = modes * row_devices
    hop = col_devices * rows

    def forward_x(t, carry):
        c, nb = t // tiles, t % tiles
        start = c * rows + nb * modes
        pieces = [
            d_ref[pl.ds(start + m, row_devices, stride=hop), :] for m in range(modes)
        ]
        block = jnp.concatenate(pieces, axis=0)
        part = split(block.T)
        mixed = dot3(part, (sx_ref[0], sx_ref[1]), NN)
        at = pl.ds(pl.multiple_of(t * LANES, LANES), LANES)
        for k, y_ref in enumerate(y_refs):
            y_ref[at, :] = mixed[:, k * LANES : (k + 1) * LANES]
        return carry

    lax.fori_loop(0, col_devices * tiles, forward_x, 0)

    def plane(v, carry):
        at = pl.ds(v, count, stride=vecs)
        mixed = jnp.concatenate([y_ref[at, :] for y_ref in y_refs], axis=1)
        physical = dot3((sz_ref[0], sz_ref[1]), split(mixed), NN)
        product = physical * speed_ref[...]
        mixed = dot3((az_ref[0], az_ref[1]), split(product), NN)
        for k, y_ref in enumerate(y_refs):
            y_ref[at, :] = mixed[:, k * LANES : (k + 1) * LANES]
        return carry

    lax.fori_loop(0, vecs, plane, 0)

    def inverse_x(t, carry):
        c, nb = t // tiles, t % tiles
        start = c * rows + nb * modes
        at = pl.ds(pl.multiple_of(t * LANES, LANES), LANES)
        block = split(jnp.concatenate([y_ref[at, :] for y_ref in y_refs], axis=1))
        back = dot3((g_ref[0], g_ref[1]), block, NT)
        for m in range(modes):
            out_ref[pl.ds(start + m, row_devices, stride=hop), :] = back[
                m * row_devices : (m + 1) * row_devices
            ]
        return carry

    lax.fori_loop(0, col_devices * tiles, inverse_x, 0)


def column_kernel(
    nl_ref, q_ref, mask_ref, wave_ref, decay_ref, to_ref, from_ref, stepped_ref, gram_ref,
    *, rows, modes, planes, tiles, vecs, cells,
):
    to_eigen = split(to_ref[...])
    from_eigen = split(from_ref[...])
    decay = jnp.broadcast_to(decay_ref[...], (planes, tiles * LANES))

    def step(m, carry):
        high, cross = carry
        nonlinear = jnp.concatenate(
            [nl_ref[pl.ds(nb * modes + m, planes, stride=rows), :] for nb in range(tiles)],
            axis=1,
        )
        right = STEP_COEF * q_ref[m] + nonlinear * mask_ref[pl.ds(m, 1), :]
        eigen = dot3(to_eigen, split(right), NN)
        eigen = eigen / (wave_ref[pl.ds(m, 1), :] + decay)
        stepped = dot3(from_eigen, split(eigen), NN)
        stepped_ref[m] = stepped
        part = split(stepped)
        stacked = [
            jnp.concatenate([x[:, nb * LANES : (nb + 1) * LANES] for nb in range(tiles)], axis=0)
            for x in part
        ]
        return (
            high + dot(stacked[0], stacked[0], TN),
            cross + dot(stacked[0], stacked[1], TN),
        )

    zero = jnp.zeros((LANES, LANES), F32)
    high, cross = lax.fori_loop(0, modes, step, (zero, zero))
    full = (high + (cross + cross.T)) * (1.0 / cells)
    group = LANES // vecs
    lane = lax.broadcasted_iota(jnp.int32, (vecs, LANES), 1) // vecs
    folded = jnp.zeros((vecs, LANES), F32)
    for k in range(group):
        folded = folded + jnp.where(lane == k, full[k * vecs : (k + 1) * vecs], 0.0)
    folded = folded + pltpu.roll(folded, LANES // 2, 1)
    folded = folded + pltpu.roll(folded, LANES // 4, 1)
    piece = vecs // group
    lane = lax.broadcasted_iota(jnp.int32, (piece, LANES), 1) // vecs
    packed = jnp.zeros((piece, LANES), F32)
    for k in range(group):
        packed = jnp.where(lane == k, folded[k * piece : (k + 1) * piece], packed)
    gram_ref[...] = packed


def finish_kernel(grams_ref, stepped_ref, vectors_ref, growth_ref, w_ref, *, devices, vecs, wide):
    group = LANES // vecs
    piece = vecs // group

    @pl.when(pl.program_id(0) == 0)
    def _():
        packed = jnp.sum(grams_ref[...].reshape(devices, piece, LANES), axis=0)
        gram = jnp.concatenate(
            [pltpu.roll(packed, (LANES - k * vecs) % LANES, 1) for k in range(group)], axis=0
        )
        lane = lax.broadcasted_iota(jnp.int32, (vecs, LANES), 1)
        row = lax.broadcasted_iota(jnp.int32, (vecs, LANES), 0)
        work = jnp.where(lane < vecs, gram, jnp.where(lane == row + vecs, 1.0, 0.0))
        for k in range(vecs - 1):
            pivot_row = work[k : k + 1, :]
            scaled = pivot_row / work[k : k + 1, k : k + 1]
            column = jnp.broadcast_to(work[:, k : k + 1], (vecs, LANES))
            work = work - jnp.where(row > k, column * scaled, 0.0)
        pivots = jnp.sum(jnp.where(lane == row, work, 0.0), axis=1, keepdims=True)
        diagonal = jnp.sqrt(pivots)
        inverse = work / diagonal
        across = jnp.sum(jnp.where(lane == row, diagonal, 0.0), axis=0, keepdims=True)
        growth_ref[...] = jnp.log(jnp.where(lane[:1] < vecs, across, 1.0))
        inverse = jnp.where((lane >= vecs) & (lane < 2 * vecs), inverse, 0.0)
        inverse = inverse + pltpu.roll(inverse, LANES // 2, 1)
        inverse = inverse + pltpu.roll(inverse, LANES // 4, 1)
        repeats = wide // vecs
        tall = jnp.concatenate([inverse] * repeats, axis=0)
        tall = jnp.concatenate([tall] * (wide // LANES), axis=1)
        rows = lax.broadcasted_iota(jnp.int32, (wide, wide), 0) // vecs
        cols = lax.broadcasted_iota(jnp.int32, (wide, wide), 1) // vecs
        w_high, w_low = split(jnp.where(rows == cols, tall, 0.0))
        w_ref[0] = w_high
        w_ref[1] = w_low

    w = (w_ref[0], w_ref[1])
    for k in range(stepped_ref.shape[1] // wide):
        at = slice(k * wide, (k + 1) * wide)
        vectors_ref[:, at] = dot3(split(stepped_ref[:, at]), w, NT)


def vmem():
    return pl.BlockSpec(memory_space=pltpu.VMEM)


def cost(flops, moved):
    return pl.CostEstimate(flops=int(flops), bytes_accessed=int(moved), transcendentals=0)


def waves(count, first, length):
    index = first + jnp.arange(length, dtype=jnp.int32)
    return jnp.where(index <= count // 2, index, index - count // 2).astype(F32)


def body(tangents, base_flow, mode_mask, decay_rates, to_eigen, from_eigen):
    modes, planes, width = tangents.shape
    z_length = base_flow.shape[2]
    vecs = width // z_length
    row_devices, col_devices = lax.axis_size("row"), lax.axis_size("col")
    devices = row_devices * col_devices
    x_count, z_count = modes * row_devices, z_length * col_devices
    tiles = width // LANES
    rows = modes * tiles
    size = tangents.size * 4
    both = ("row", "col")

    order = np.arange(x_count)
    order = (order % row_devices) * modes + order // row_devices
    x_synthesis, z_synthesis = synthesis(x_count), synthesis(z_count)
    points = -(-x_count // LANES) * LANES
    extra = ((0, 0), (0, points - x_count))
    sx = halves_of_table(np.pad(x_synthesis[:, order].T, extra))
    sz = halves_of_table(z_synthesis)
    az = halves_of_table(analysis(z_count))
    gx = halves_of_table(np.pad(derivative_analysis(x_count, ALPHA_X)[order], extra))

    packed = pl.pallas_call(
        functools.partial(pack_kernel, rows=rows, modes=modes, planes=planes, tiles=tiles),
        out_shape=jax.ShapeDtypeStruct((planes * rows, LANES), F32),
        in_specs=[vmem()],
        out_specs=vmem(),
        cost_estimate=cost(0, 2 * size),
        name="pack",
    )(tangents)
    received = lax.all_to_all(packed.reshape(devices, rows, LANES), both, 0, 0, tiled=True)

    base = jnp.transpose(base_flow, (1, 0, 2)).reshape(devices, modes * z_length)
    base = lax.all_to_all(base, both, 0, 0, tiled=True)
    base = base.reshape(row_devices, col_devices, modes, z_length)
    base = jnp.transpose(base, (0, 2, 1, 3)).reshape(x_count, z_count)
    speed = jnp.dot(base, z_synthesis.T.astype(np.float32), precision=lax.Precision.HIGHEST)
    speed = lax.dot_general(
        speed, np.pad(x_synthesis.T, extra).astype(np.float32), TN, precision=lax.Precision.HIGHEST
    )

    flops = 8 * x_count * z_count * (x_count + z_count) * vecs
    returned = pl.pallas_call(
        functools.partial(
            transform_kernel, rows=rows, modes=modes, row_devices=row_devices,
            col_devices=col_devices, tiles=tiles, vecs=vecs,
        ),
        out_shape=jax.ShapeDtypeStruct((devices * rows, LANES), F32),
        in_specs=[vmem()] * 6,
        out_specs=vmem(),
        scratch_shapes=[pltpu.VMEM((z_count * vecs, LANES), F32)] * (points // LANES),
        cost_estimate=cost(flops, 2 * size),
        compiler_params=pltpu.CompilerParams(vmem_limit_bytes=48 * 2**20),
        name="transform",
    )(received.reshape(devices * rows, LANES), speed, sx, sz, az, gx)
    nonlinear = lax.all_to_all(returned.reshape(devices, rows, LANES), both, 0, 0, tiled=True)

    wave_x = ALPHA_X * waves(x_count, lax.axis_index("row") * modes, modes)
    wave_z = BETA_Z * waves(z_count, lax.axis_index("col") * z_length, z_length)
    wave = STEP_COEF + VISCOSITY * (wave_x[:, None] ** 2 + jnp.repeat(wave_z, vecs)[None, :] ** 2)
    mask = jnp.repeat(mode_mask.astype(F32), vecs, axis=1)
    stepped, gram = pl.pallas_call(
        functools.partial(
            column_kernel, rows=rows, modes=modes, planes=planes, tiles=tiles, vecs=vecs,
            cells=x_count * planes * z_count,
        ),
        out_shape=[
            jax.ShapeDtypeStruct(tangents.shape, F32),
            jax.ShapeDtypeStruct((vecs * vecs // LANES, LANES), F32),
        ],
        in_specs=[vmem()] * 7,
        out_specs=[vmem()] * 2,
        cost_estimate=cost(4 * planes * planes * modes * width, 3 * size),
        compiler_params=pltpu.CompilerParams(vmem_limit_bytes=48 * 2**20),
        name="column",
    )(
        nonlinear.reshape(planes * rows, LANES), tangents, mask, wave,
        decay_rates[:, None], to_eigen, from_eigen,
    )

    piece = vecs * vecs // LANES
    grams = lax.all_to_all(
        jnp.broadcast_to(gram[None], (devices, piece, LANES)), both, 0, 0, tiled=True
    ).reshape(devices * piece, LANES)

    height = modes * planes
    block = height // 6
    vectors, growth = pl.pallas_call(
        functools.partial(finish_kernel, devices=devices, vecs=vecs, wide=2 * LANES),
        out_shape=[
            jax.ShapeDtypeStruct((height, width), F32),
            jax.ShapeDtypeStruct((1, LANES), F32),
        ],
        grid=(height // block,),
        in_specs=[
            pl.BlockSpec((devices * piece, LANES), lambda i: (0, 0)),
            pl.BlockSpec((block, width), lambda i: (i, 0)),
        ],
        out_specs=[
            pl.BlockSpec((block, width), lambda i: (i, 0)),
            pl.BlockSpec((1, LANES), lambda i: (0, 0)),
        ],
        scratch_shapes=[pltpu.VMEM((2, 2 * LANES, 2 * LANES), BF16)],
        cost_estimate=cost(2 * height * width * 256, 2 * size),
        name="finish",
    )(grams, stepped.reshape(height, width))
    return vectors.reshape(tangents.shape), growth[0, :vecs]


def solution(mesh):
    placed = (P("row", None, "col"), P("row", None, "col"), P("row", "col"), P(), P(), P())
    return jax.shard_map(
        body, mesh=mesh, in_specs=placed, out_specs=(P("row", None, "col"), P()), check_vma=False
    )
```

time: 469 us -> 269 us (0.57); the launches traced: 462 us -> 268 us
  matrix products: 157 us -> 0.89 us
  local copies, waits for them, and re-layouts: 114 us -> 8.69 us
  Pallas kernels: 0 us -> 92.7 us
  blocking collectives: 36.7 us -> 21.1 us
  other arithmetic: 9.9 us -> 0.56 us
  waiting for transfers between devices: 124 us -> 118 us
  starting transfers between devices: 19.7 us -> 25.2 us
    dot_general x11 -> x2, matrix products: 157 us -> 0.89 us  [the longest x1 0.57 us: body(): jnp.dot(base, z_synthesis.T.astype(np.float32), precision=lax.Precision.H...]
    pallas_call x0 -> x4, Pallas kernels: none -> 92.7 us  [the longest x1 59.6 us: body(): pl.pallas_call(functools.partial(transform_kernel, rows=rows, modes=modes...]
    reshape x5 -> x3, local copies, waits for them, and re-layouts: 54.9 us -> 0.85 us  [the longest x1 0.51 us: body(): base = base.reshape(row_devices, col_devices, modes, z_length)]
    another operation x4 -> x0, local copies, waits for them, and re-layouts: 38.6 us -> none
    all_gather x1 -> x0, blocking collectives: 36.7 us -> none  [total_of_pieces(): return lax.all_gather(shard, axis).sum(0)]
    all_to_all x0 -> x1, blocking collectives: none -> 21.1 us  [body(): lax.all_to_all(jnp.broadcast_to(gram[None], (devices, piece, LANES)), bot...]
    concatenate x1 -> x0, local copies, waits for them, and re-layouts: 6.93 us -> none  [side_by_side(): both = jnp.concatenate(arrays, axis=along)]
    another operation x5 -> x0, other arithmetic: 6.68 us -> none  [the longest x3 3.59 us: body(): lower_factor = jnp.linalg.cholesky(gram_matrix)]
  transfers between devices with their start and end apart: 2 -> 3, of which waited for: 2 -> 3; matrix products, arithmetic and copies ran while one was open for 0% -> 1% of each run, Pallas kernels for 0% -> 2%
where the time goes in v1:
time: 269 us; the launch traced here: 268 us
  waiting for transfers between devices  118 us (44%)
  Pallas kernels  92.7 us (34%)
  starting transfers between devices  25.2 us (9%)
  blocking collectives  21.1 us (8%)
  local copies, waits for them, and re-layouts  8.69 us (3%)
    pallas_call x1, Pallas kernels, body(): pl.pallas_call(functools.partial(transform_kernel, rows=rows, modes=modes...  59.6 us
    all_to_all x1, waiting for transfers between devices, body(): lax.all_to_all(returned.reshape(devices, rows, LANES), both, 0, 0, tiled=...  57.6 us
    all_to_all x1, waiting for transfers between devices, body(): lax.all_to_all(packed.reshape(devices, rows, LANES), both, 0, 0, tiled=True)  55.8 us
    all_to_all x1, blocking collectives, body(): lax.all_to_all(jnp.broadcast_to(gram[None], (devices, piece, LANES)), bot...  21.1 us
    pallas_call x1, Pallas kernels, body(): pl.pallas_call(functools.partial(column_kernel, rows=rows, modes=modes, p...  17.2 us
    all_to_all x1, starting transfers between devices, body(): base = lax.all_to_all(base, both, 0, 0, tiled=True)  11.5 us
    pallas_call x1, Pallas kernels, body(): pl.pallas_call(functools.partial(finish_kernel, devices=devices, vecs=vec...  10.2 us
    all_to_all x1, starting transfers between devices, body(): lax.all_to_all(returned.reshape(devices, rows, LANES), both, 0, 0, tiled=...  8.15 us
  transfers between devices with their start and end apart: 3, of which 3 were waited for; matrix products, arithmetic and copies ran while one was open for 1% of the time, Pallas kernels for 2%

profile of v1, /device:TPU:1, one launch (start us, length us, event | category | flops | bytes accessed | tf_op | source)
XLA Modules:
  0.0 268.0 jit_solution(12473435046638528686)
XLA Ops:
  0.6 1.7 copy.21
  2.3 11.5 %all-to-all-start.1 = ((f32[128,1,288]{2,1,0:T(1,128)}), f32[128,1,288]{2,1,0:T(1,128)S(1)}, u32[]{:S(2)}, u32[]{:S(2)}) async-start(f32[128,1,288]{2,1,0:T(1,128)} %copy.21), calls=%async_computation.1 | async-start | bytes 393216 | tf_op jit(solution)/shard_map/all_to_all | solution.py:262
  13.8 5.7 %pack.1 = f32[9216,128]{1,0:T(8,128)} custom-call(f32[12,128,768]{2,1,0:T(8,128)} %q_ref.3), custom_call_target="tpu_custom_call" | custom-call | bytes 9437184 | tf_op jit(solution)/shard_map/pack/pallas_call | solution.py:251
  19.6 4.6 %all-to-all-done.1 = f32[128,1,288]{2,1,0:T(1,128)S(1)} async-done(((f32[128,1,288]{2,1,0:T(1,128)}), f32[128,1,288]{2,1,0:T(1,128)S(1)}, u32[]{:S(2)}, u32[]{:S(2)}) %all-to-all-start.1) | async-done | bytes 147488 | tf_op jit(solution)/shard_map/all_to_all | solution.py:262
  24.2 5.6 %all-to-all-start = ((f32[128,72,128]{2,1,0:T(8,128)}), f32[128,72,128]{2,1,0:T(8,128)}, u32[]{:S(2)}, u32[]{:S(2)}) async-start(f32[128,72,128]{2,1,0:T(8,128)} %bitcast.22), calls=%async_computation | async-start | bytes 9437184 | tf_op jit(solution)/shard_map/all_to_all | solution.py:259
  29.8 0.0 copy-start.8
  29.8 0.0 copy-start.4
  29.8 0.0 copy-start.5
  29.8 0.0 copy-start.6
  29.8 0.0 copy-start.7
  29.8 0.5 reduce
  30.3 0.5 reshape.61
  30.8 0.3 copy.22
  31.1 0.2 reshape.62
  31.3 0.6 fusion.5
  31.9 0.3 fusion.6.speed_ref
  32.3 55.8 %all-to-all-done = f32[128,72,128]{2,1,0:T(8,128)} async-done(((f32[128,72,128]{2,1,0:T(8,128)}), f32[128,72,128]{2,1,0:T(8,128)}, u32[]{:S(2)}, u32[]{:S(2)}) %all-to-all-start) | async-done | bytes 4718624 | tf_op jit(solution)/shard_map/all_to_all | solution.py:259
  88.1 59.6 %transform.1 = f32[9216,128]{1,0:T(8,128)S(1)} custom-call(f32[9216,128]{1,0:T(8,128)} %bitcast.1.d_ref, f32[192,256]{1,0:T(8,128)S(1)} %fusion.6.speed_ref, bf16[2,192,256]{2,1,0:T(8,128)(2,1)S(1)} %copy-done.7, bf16[2,192,192]{2,1,0:T(8,128)(2,1)S(1)} %copy-done.6, bf16[2,192,192]{2,1,0:T(8,128)(2,1)S(1)} %copy-done.5, bf16[2,192,256]{2,1,0:T(8,128)(2,1)S(1)} %copy-done.4), custom_call_target="tpu_custom_call" | custom-call | flops 3623878656 | bytes 9437184 | tf_op jit(solution)/shard_map/transform/pallas_call | solution.py:271
  147.7 2.2 copy-done.1
  149.9 8.2 %all-to-all-start.2 = ((f32[128,72,128]{2,1,0:T(8,128)}), f32[128,72,128]{2,1,0:T(8,128)}, u32[]{:S(2)}, u32[]{:S(2)}) async-start(f32[128,72,128]{2,1,0:T(8,128)} %bitcast.21), calls=%async_computation.2 | async-start | bytes 9437184 | tf_op jit(solution)/shard_map/all_to_all | solution.py:284
  158.1 0.1 broadcast_in_dim.17
  158.2 0.1 integer_pow.22
  158.3 0.1 copy.23.decay_ref
  158.4 0.1 broadcast_in_dim.16
  158.5 0.1 reshape.65.mask_ref
  158.6 0.1 multiply_add_fusion.wave_ref
  158.7 57.6 %all-to-all-done.2 = f32[128,72,128]{2,1,0:T(8,128)} async-done(((f32[128,72,128]{2,1,0:T(8,128)}), f32[128,72,128]{2,1,0:T(8,128)}, u32[]{:S(2)}, u32[]{:S(2)}) %all-to-all-start.2) | async-done | bytes 4718624 | tf_op jit(solution)/shard_map/all_to_all | solution.py:284
  216.3 17.2 %column.1 = (f32[12,128,768]{2,1,0:T(8,128)S(1)}, f32[8,128]{1,0:T(8,128)S(1)}) custom-call(f32[9216,128]{1,0:T(8,128)} %bitcast.6.nl_ref, f32[12,128,768]{2,1,0:T(8,128)} %q_ref.3, f32[12,768]{1,0:T(8,128)S(1)} %reshape.65.mask_ref, f32[12,768]{1,0:T(8,128)S(1)} %multiply_add_fusion.wave_ref, f32[128,1]{1,0:T(8,128)S(1)} %copy.23.decay_ref, ...), custom_call_target="tpu_custom_call" | custom-call | flops 603979776 | bytes 14155776 | tf_op jit(solution)/shard_map/column/pallas_call | solution.py:290
  233.5 2.1 copy-done
  235.7 21.1 %all_to_all.24 = f32[128,8,128]{2,1,0:T(8,128)} all-to-all(f32[128,8,128]{2,1,0:T(8,128)S(1)} %broadcast_in_dim.19), channel_id=1, replica_groups=mesh['row'=16,'col'=8] {'row','col'}, dimensions={0} | all-to-all | bytes 1048576 | tf_op jit(solution)/shard_map/all_to_all | solution.py:310
  256.8 10.2 %finish.1 = (f32[1536,768]{1,0:T(8,128)}, f32[1,128]{1,0:T(1,128)}) custom-call(f32[1024,128]{1,0:T(8,128)} %bitcast.24, f32[1536,768]{1,0:T(8,128)} %bitcast.20), custom_call_target="tpu_custom_call" | custom-call | flops 603979776 | bytes 9437184 | tf_op jit(solution)/shard_map/finish/pallas_call | solution.py:316
  266.9 1.1 slice_bitcast_fusion
  (21 shorter events, 0.1 us)
Async XLA Ops:
  2.3 21.8 %all-to-all-start.1 = ((f32[128,1,288]{2,1,0:T(1,128)}), f32[128,1,288]{2,1,0:T(1,128)S(1)}, u32[]{:S(2)}, u32[]{:S(2)}) async-start(f32[128,1,288]{2,1,0:T(1,128)} %copy.21), calls=%async_computation.1 | async-start | bytes 393216 | tf_op jit(solution)/shard_map/all_to_all | solution.py:262
  24.2 7.2 %copy-start.9 = (f32[192,192]{1,0:T(8,128)S(1)}, f32[192,192]{1,0:T(8,128)}, u32[]{:S(2)}) copy-start(f32[192,192]{1,0:T(8,128)} %constant.37.clone) | copy-start | bytes 442372
  24.2 63.9 %all-to-all-start = ((f32[128,72,128]{2,1,0:T(8,128)}), f32[128,72,128]{2,1,0:T(8,128)}, u32[]{:S(2)}, u32[]{:S(2)}) async-start(f32[128,72,128]{2,1,0:T(8,128)} %bitcast.22), calls=%async_computation | async-start | bytes 9437184 | tf_op jit(solution)/shard_map/all_to_all | solution.py:259
  29.8 2.2 copy-start.8
  29.8 58.3 %copy-start.4 = (bf16[2,192,256]{2,1,0:T(8,128)(2,1)S(1)}, bf16[2,192,256]{2,1,0:T(8,128)(2,1)}, u32[]{:S(2)}) copy-start(bf16[2,192,256]{2,1,0:T(8,128)(2,1)} %constant.42.clone.g_ref) | copy-start | bytes 589828
  29.8 58.3 %copy-start.5 = (bf16[2,192,192]{2,1,0:T(8,128)(2,1)S(1)}, bf16[2,192,192]{2,1,0:T(8,128)(2,1)}, u32[]{:S(2)}) copy-start(bf16[2,192,192]{2,1,0:T(8,128)(2,1)} %constant.41.clone.az_ref) | copy-start | bytes 442372
  29.8 58.3 %copy-start.6 = (bf16[2,192,192]{2,1,0:T(8,128)(2,1)S(1)}, bf16[2,192,192]{2,1,0:T(8,128)(2,1)}, u32[]{:S(2)}) copy-start(bf16[2,192,192]{2,1,0:T(8,128)(2,1)} %constant.40.clone.sz_ref) | copy-start | bytes 442372
  29.8 58.3 %copy-start.7 = (bf16[2,192,256]{2,1,0:T(8,128)(2,1)S(1)}, bf16[2,192,256]{2,1,0:T(8,128)(2,1)}, u32[]{:S(2)}) copy-start(bf16[2,192,256]{2,1,0:T(8,128)(2,1)} %constant.39.clone.sx_ref) | copy-start | bytes 589828
  147.7 2.2 copy-start.1
  149.9 8.2 %copy-start.10 = (s32[12,24]{1,0:T(8,128)S(1)}, s32[12,24]{1,0:T(8,128)}, u32[]{:S(2)}) copy-start(s32[12,24]{1,0:T(8,128)} %param.14) | copy-start | bytes 3460
  149.9 8.4 %copy-start.11 = (f32[128]{0:T(128)S(1)}, f32[128]{0:T(128)}, u32[]{:S(2)}) copy-start(f32[128]{0:T(128)} %param.15) | copy-start | bytes 1540
  149.9 66.4 %copy-start.2 = (f32[128,128]{1,0:T(8,128)S(1)}, f32[128,128]{1,0:T(8,128)}, u32[]{:S(2)}) copy-start(f32[128,128]{1,0:T(8,128)} %to_ref.1) | copy-start | bytes 196612
  149.9 66.4 %copy-start.3 = (f32[128,128]{1,0:T(8,128)S(1)}, f32[128,128]{1,0:T(8,128)}, u32[]{:S(2)}) copy-start(f32[128,128]{1,0:T(8,128)} %from_ref.1) | copy-start | bytes 196612
  149.9 66.4 %all-to-all-start.2 = ((f32[128,72,128]{2,1,0:T(8,128)}), f32[128,72,128]{2,1,0:T(8,128)}, u32[]{:S(2)}, u32[]{:S(2)}) async-start(f32[128,72,128]{2,1,0:T(8,128)} %bitcast.21), calls=%async_computation.2 | async-start | bytes 9437184 | tf_op jit(solution)/shard_map/all_to_all | solution.py:284
  233.5 2.1 copy-start

commit v2 on v1

v2 whole, which is shorter than its diff:
```python
import functools

import jax
import jax.numpy as jnp
import numpy as np
from jax import lax
from jax.experimental import pallas as pl
from jax.experimental.pallas import tpu as pltpu
from jax.sharding import PartitionSpec as P

STEP_COEF = 10.0
VISCOSITY = 0.01
ALPHA_X = 0.5
BETA_Z = 1.0
LANES = 128
F32 = jnp.float32
BF16 = jnp.bfloat16
NN = (((1,), (0,)), ((), ()))
NT = (((1,), (1,)), ((), ()))
TN = (((0,), (0,)), ((), ()))


def synthesis(count):
    points = np.arange(count)[:, None]
    modes = np.arange(count)[None, :]
    middle = count // 2
    waves = np.where(modes <= middle, modes, modes - middle)
    angles = (points * waves % count) * (2.0 * np.pi / count)
    return np.where(modes <= middle, np.cos(angles), np.sin(angles))


def analysis(count):
    modes = np.arange(count)
    weights = np.where((modes == 0) | (modes == count // 2), 1.0 / count, 2.0 / count)
    return weights[:, None] * synthesis(count).T


def derivative_analysis(count, scale):
    middle = count // 2
    derivative = np.zeros((count, count))
    for k in range(1, middle):
        derivative[k, middle + k] = k
        derivative[middle + k, k] = -k
    return -scale * (derivative @ analysis(count))


def halves_of_table(table):
    table = np.asarray(table, np.float64)
    high = table.astype(np.float32).astype(jnp.bfloat16)
    low = (table - high.astype(np.float64)).astype(np.float32).astype(jnp.bfloat16)
    return np.stack([high, low])


def split(x):
    high = x.astype(BF16)
    return high, (x - high.astype(F32)).astype(BF16)


def dot(a, b, dims):
    return lax.dot_general(a, b, dims, preferred_element_type=F32)


def dot3(a, b, dims):
    return dot(a[0], b[0], dims) + (dot(a[0], b[1], dims) + dot(a[1], b[0], dims))


def pack_kernel(q_ref, base_ref, out_ref, *, modes, planes, tiles, extra, step_modes):
    stride = modes * tiles + extra

    @pl.when(pl.program_id(0) == 0)
    def _():
        part = base_ref.shape[0] // extra
        fill = jnp.zeros((LANES - part, planes), F32)
        for k in range(extra):
            block = jnp.concatenate([base_ref[k * part : (k + 1) * part, :], fill], axis=0)
            out_ref[pl.ds(modes * tiles + k, planes, stride=stride), :] = block.T

    for k in range(step_modes):
        m = pl.program_id(0) * step_modes + k
        for nb in range(tiles):
            out_ref[pl.ds(nb * modes + m, planes, stride=stride), :] = q_ref[
                k, :, nb * LANES : (nb + 1) * LANES
            ]


def transform_kernel(
    d_ref, sx_ref, sz_ref, az_ref, g_ref, out_ref, speed_ref, *scratch,
    modes, row_devices, col_devices, tiles, extra, vecs,
):
    halves = len(scratch) // 2
    y_refs, z_refs = scratch[:halves], scratch[halves:]
    rows = modes * tiles
    stride = rows + extra
    hop = col_devices * stride
    x_count = modes * row_devices
    height = tiles * LANES

    turned = []
    for k in range(extra):
        block = jnp.concatenate(
            [
                d_ref[pl.ds(c * stride + rows + k, row_devices, stride=hop), :]
                for c in range(col_devices)
            ],
            axis=0,
        )
        turned.append(block.T)
    z_length = sz_ref.shape[2] // col_devices
    slot = lax.broadcasted_iota(jnp.int32, (z_length, LANES), 1) // row_devices
    slots = LANES // row_devices
    share = modes // extra
    sheets = []
    for c in range(col_devices):
        parts = [jnp.zeros((z_length, LANES), F32) for _ in range(halves)]
        for m in range(modes):
            piece = turned[m // share][(m % share) * z_length : (m % share + 1) * z_length]
            shift = ((m % slots - c) * row_devices) % LANES
            piece = pltpu.roll(piece, shift, 1) if shift else piece
            parts[m // slots] = jnp.where(slot == m % slots, piece, parts[m // slots])
        sheets.append(jnp.concatenate(parts, axis=1))
    base = jnp.concatenate(sheets, axis=0)[:, :x_count]
    half_way = dot3(split(base), (sx_ref[0], sx_ref[1]), NN)
    speed_ref[...] = dot3((sz_ref[0], sz_ref[1]), split(half_way), NN)

    def forward_x(c, carry):
        parts = []
        for nb in range(tiles):
            start = c * stride + nb * modes
            block = jnp.concatenate(
                [d_ref[pl.ds(start + m, row_devices, stride=hop), :] for m in range(modes)],
                axis=0,
            )
            parts.append(block.T)
        mixed = dot3(split(jnp.concatenate(parts, axis=0)), (sx_ref[0], sx_ref[1]), NN)
        at = pl.ds(pl.multiple_of(c * height, height), height)
        for k, y_ref in enumerate(y_refs):
            y_ref[at, :] = mixed[:, k * LANES : (k + 1) * LANES]
        return carry

    lax.fori_loop(0, col_devices, forward_x, 0, unroll=4)

    def plane(i, carry):
        for j in range(4):
            at = pl.ds(i * 4 + j, y_refs[0].shape[0] // vecs, stride=vecs)
            mixed = jnp.concatenate([y_ref[at, :] for y_ref in y_refs], axis=1)
            physical = dot3((sz_ref[0], sz_ref[1]), split(mixed), NN)
            product = physical * speed_ref[...]
            mixed = dot3((az_ref[0], az_ref[1]), split(product), NN)
            for k, z_ref in enumerate(z_refs):
                z_ref[at, :] = mixed[:, k * LANES : (k + 1) * LANES]
        return carry

    lax.fori_loop(0, vecs // 4, plane, 0, unroll=2)

    batch = 3

    def inverse_x(i, carry):
        at = pl.ds(pl.multiple_of(i * (batch * LANES), LANES), batch * LANES)
        block = split(jnp.concatenate([z_ref[at, :] for z_ref in z_refs], axis=1))
        back = dot3((g_ref[0], g_ref[1]), block, NT)
        c, group = i // (tiles // batch), i % (tiles // batch)
        for nb in range(batch):
            start = c * stride + (group * batch + nb) * modes
            for m in range(modes):
                out_ref[pl.ds(start + m, row_devices, stride=hop), :] = back[
                    m * row_devices : (m + 1) * row_devices, nb * LANES : (nb + 1) * LANES
                ]
        return carry

    stride = rows
    hop = col_devices * stride
    lax.fori_loop(0, col_devices * tiles // batch, inverse_x, 0, unroll=4)


def column_kernel(
    nl_ref, q_ref, mask_ref, decay_ref, to_ref, from_ref, stepped_ref, gram_ref,
    mask_s, wave_s, decay_s, high_s, cross_s,
    *, modes, planes, tiles, vecs, step_modes, x_count, z_count, z_length,
):
    width = tiles * LANES

    @pl.when(pl.program_id(0) == 0)
    def _():
        lane = lax.broadcasted_iota(jnp.int32, (z_length, width), 1) // vecs
        row = lax.broadcasted_iota(jnp.int32, (z_length, width), 0)
        spread = jnp.where(lane == row, 1.0, 0.0).astype(BF16)
        mask_s[...] = dot(mask_ref[...].astype(F32).astype(BF16), spread, NN)
        n = lax.broadcasted_iota(jnp.int32, (modes, width), 1) // vecs
        n = n + lax.axis_index("col") * z_length
        m = lax.broadcasted_iota(jnp.int32, (modes, width), 0)
        m = m + lax.axis_index("row") * modes
        wave_x = jnp.where(m <= x_count // 2, m, m - x_count // 2).astype(F32) * ALPHA_X
        wave_z = jnp.where(n <= z_count // 2, n, n - z_count // 2).astype(F32) * BETA_Z
        wave_s[...] = STEP_COEF + VISCOSITY * (wave_x * wave_x + wave_z * wave_z)
        decay_s[...] = jnp.broadcast_to(decay_ref[...], (LANES, planes)).T
        high_s[...] = jnp.zeros_like(high_s)
        cross_s[...] = jnp.zeros_like(cross_s)

    to_eigen = split(to_ref[...])
    from_eigen = split(from_ref[...])
    decay = jnp.concatenate([decay_s[...]] * tiles, axis=1)
    high, cross = high_s[...], cross_s[...]
    for k in range(step_modes):
        m = pl.program_id(0) * step_modes + k
        nonlinear = jnp.concatenate(
            [
                nl_ref[pl.ds(nb * modes + m, planes, stride=tiles * modes), :]
                for nb in range(tiles)
            ],
            axis=1,
        )
        right = STEP_COEF * q_ref[k] + nonlinear * mask_s[pl.ds(m, 1), :]
        eigen = dot3(to_eigen, split(right), NN)
        eigen = eigen / (wave_s[pl.ds(m, 1), :] + decay)
        stepped = dot3(from_eigen, split(eigen), NN)
        stepped_ref[pl.ds(pl.multiple_of(m * planes, planes), planes), :] = stepped
        stacked = [
            jnp.concatenate([x[:, nb * LANES : (nb + 1) * LANES] for nb in range(tiles)], axis=0)
            for x in split(stepped)
        ]
        high = high + dot(stacked[0], stacked[0], TN)
        cross = cross + dot(stacked[0], stacked[1], TN)
    high_s[...] = high
    cross_s[...] = cross

    @pl.when(pl.program_id(0) == pl.num_programs(0) - 1)
    def _():
        full = (high + (cross + cross.T)) * (1.0 / (x_count * planes * z_count))
        group = LANES // vecs
        lane = lax.broadcasted_iota(jnp.int32, (vecs, LANES), 1) // vecs
        folded = jnp.zeros((vecs, LANES), F32)
        for k in range(group):
            folded = folded + jnp.where(lane == k, full[k * vecs : (k + 1) * vecs], 0.0)
        folded = folded + pltpu.roll(folded, LANES // 2, 1)
        folded = folded + pltpu.roll(folded, LANES // 4, 1)
        piece = vecs // group
        lane = lax.broadcasted_iota(jnp.int32, (piece, LANES), 1) // vecs
        packed = jnp.zeros((piece, LANES), F32)
        for k in range(group):
            packed = jnp.where(lane == k, folded[k * piece : (k + 1) * piece], packed)
        gram_ref[...] = jnp.broadcast_to(packed[None], gram_ref.shape)


def finish_kernel(grams_ref, stepped_ref, vectors_ref, growth_ref, w_ref, *, devices, vecs, wide):
    group = LANES // vecs
    piece = vecs // group

    @pl.when(pl.program_id(0) == 0)
    def _():
        packed = jnp.sum(grams_ref[...].reshape(devices, piece, LANES), axis=0)
        gram = jnp.concatenate(
            [pltpu.roll(packed, (LANES - k * vecs) % LANES, 1) for k in range(group)], axis=0
        )
        lane = lax.broadcasted_iota(jnp.int32, (vecs, LANES), 1)
        row = lax.broadcasted_iota(jnp.int32, (vecs, LANES), 0)
        work = jnp.where(lane < vecs, gram, jnp.where(lane == row + vecs, 1.0, 0.0))
        for k in range(vecs - 1):
            pivot_row = work[k : k + 1, :]
            scaled = pivot_row / work[k : k + 1, k : k + 1]
            column = jnp.broadcast_to(work[:, k : k + 1], (vecs, LANES))
            work = work - jnp.where(row > k, column * scaled, 0.0)
        pivots = jnp.sum(jnp.where(lane == row, work, 0.0), axis=1, keepdims=True)
        diagonal = jnp.sqrt(pivots)
        inverse = work / diagonal
        across = jnp.sum(jnp.where(lane == row, diagonal, 0.0), axis=0, keepdims=True)
        growth_ref[...] = jnp.log(across[:, :vecs])
        inverse = jnp.where((lane >= vecs) & (lane < 2 * vecs), inverse, 0.0)
        inverse = inverse + pltpu.roll(inverse, LANES // 2, 1)
        inverse = inverse + pltpu.roll(inverse, LANES // 4, 1)
        repeats = wide // vecs
        tall = jnp.concatenate([inverse] * repeats, axis=0)
        tall = jnp.concatenate([tall] * (wide // LANES), axis=1)
        rows = lax.broadcasted_iota(jnp.int32, (wide, wide), 0) // vecs
        cols = lax.broadcasted_iota(jnp.int32, (wide, wide), 1) // vecs
        w_high, w_low = split(jnp.where(rows == cols, tall, 0.0))
        w_ref[0] = w_high
        w_ref[1] = w_low

    w = (w_ref[0], w_ref[1])
    block = vectors_ref.shape[0]
    rows = pl.ds(pl.multiple_of(pl.program_id(0) * block, block), block)
    for k in range(vectors_ref.shape[1] // wide):
        at = slice(k * wide, (k + 1) * wide)
        vectors_ref[:, at] = dot3(split(stepped_ref[rows, at]), w, NT)


def vmem():
    return pl.BlockSpec(memory_space=pltpu.VMEM)


def cost(flops, moved):
    return pl.CostEstimate(flops=int(flops), bytes_accessed=int(moved), transcendentals=0)


def body(tangents, base_flow, mode_mask, decay_rates, to_eigen, from_eigen):
    modes, planes, width = tangents.shape
    z_length = base_flow.shape[2]
    vecs = width // z_length
    row_devices, col_devices = lax.axis_size("row"), lax.axis_size("col")
    devices = row_devices * col_devices
    x_count, z_count = modes * row_devices, z_length * col_devices
    tiles = width // LANES
    rows = modes * tiles
    extra = -(-modes * z_length // LANES)
    size = tangents.size * 4
    both = ("row", "col")
    big = pltpu.CompilerParams(vmem_limit_bytes=40 * 2**20)
    small = pltpu.CompilerParams(vmem_limit_bytes=24 * 2**20)

    order = np.arange(x_count)
    order = (order % row_devices) * modes + order // row_devices
    halves = -(-x_count // LANES)
    fill = ((0, 0), (0, halves * LANES - x_count))
    sx = halves_of_table(np.pad(synthesis(x_count)[:, order].T, fill))
    sz = halves_of_table(synthesis(z_count))
    az = halves_of_table(analysis(z_count))
    gx = halves_of_table(np.pad(derivative_analysis(x_count, ALPHA_X)[order], fill))

    steps = 4
    base = jnp.transpose(base_flow, (0, 2, 1)).reshape(modes * z_length, planes)
    packed = pl.pallas_call(
        functools.partial(
            pack_kernel, modes=modes, planes=planes, tiles=tiles, extra=extra,
            step_modes=modes // steps,
        ),
        out_shape=jax.ShapeDtypeStruct((planes * (rows + extra), LANES), F32),
        grid=(steps,),
        in_specs=[
            pl.BlockSpec((modes // steps, planes, width), lambda i: (i, 0, 0)),
            pl.BlockSpec(base.shape, lambda i: (0, 0)),
        ],
        out_specs=vmem(),
        cost_estimate=cost(10**9, 2 * size),
        compiler_params=small,
        name="pack",
    )(tangents, base)
    received = lax.all_to_all(
        packed.reshape(devices, rows + extra, 1, LANES), both, 0, 0, tiled=True
    ).reshape(packed.shape)

    returned = pl.pallas_call(
        functools.partial(
            transform_kernel, modes=modes, row_devices=row_devices,
            col_devices=col_devices, tiles=tiles, extra=extra, vecs=vecs,
        ),
        out_shape=jax.ShapeDtypeStruct((devices * rows, LANES), F32),
        in_specs=[vmem()] * 5,
        out_specs=vmem(),
        scratch_shapes=[pltpu.VMEM((z_count, halves * LANES), F32)]
        + [pltpu.VMEM((z_count * vecs, LANES), F32)] * (2 * halves),
        cost_estimate=cost(2 * 10**10, 2 * size),
        compiler_params=big,
        name="transform",
    )(received, sx, sz, az, gx)
    nonlinear = lax.all_to_all(
        returned.reshape(devices, rows, LANES), both, 0, 0, tiled=True
    ).reshape(returned.shape)

    piece = vecs * vecs // LANES
    height = modes * planes
    stepped, grams = pl.pallas_call(
        functools.partial(
            column_kernel, modes=modes, planes=planes, tiles=tiles, vecs=vecs,
            step_modes=modes // steps, x_count=x_count, z_count=z_count, z_length=z_length,
        ),
        out_shape=[
            jax.ShapeDtypeStruct((height, width), F32),
            jax.ShapeDtypeStruct((devices, piece, LANES), F32),
        ],
        grid=(steps,),
        in_specs=[
            vmem(),
            pl.BlockSpec((modes // steps, planes, width), lambda i: (i, 0, 0)),
        ]
        + [vmem()] * 4,
        out_specs=[vmem()] * 2,
        scratch_shapes=[
            pltpu.VMEM((modes, width), F32),
            pltpu.VMEM((modes, width), F32),
            pltpu.VMEM((planes, LANES), F32),
            pltpu.VMEM((LANES, LANES), F32),
            pltpu.VMEM((LANES, LANES), F32),
        ],
        cost_estimate=cost(10**10, 3 * size),
        compiler_params=big,
        name="column",
    )(nonlinear, tangents, mode_mask, decay_rates[None, :], to_eigen, from_eigen)
    grams = lax.all_to_all(grams, both, 0, 0, tiled=True).reshape(devices * piece, LANES)

    block = height // 6
    vectors, growth = pl.pallas_call(
        functools.partial(finish_kernel, devices=devices, vecs=vecs, wide=2 * LANES),
        out_shape=[
            jax.ShapeDtypeStruct((height, width), F32),
            jax.ShapeDtypeStruct((1, vecs), F32),
        ],
        grid=(height // block,),
        in_specs=[vmem()] * 2,
        out_specs=[
            pl.BlockSpec((block, width), lambda i: (i, 0)),
            pl.BlockSpec((1, vecs), lambda i: (0, 0)),
        ],
        scratch_shapes=[pltpu.VMEM((2, 2 * LANES, 2 * LANES), BF16)],
        cost_estimate=cost(2 * height * width * 256, 2 * size),
        compiler_params=small,
        name="finish",
    )(grams, stepped)
    return vectors.reshape(tangents.shape), growth[0]


def solution(mesh):
    placed = (P("row", None, "col"), P("row", None, "col"), P("row", "col"), P(), P(), P())
    return jax.shard_map(
        body, mesh=mesh, in_specs=placed, out_specs=(P("row", None, "col"), P()), check_vma=False
    )
```

time: 269 us -> 204 us (0.76)
  blocking collectives: 21.1 us -> 153 us
  waiting for transfers between devices: 118 us -> 0 us
  Pallas kernels: 92.7 us -> 46.6 us
  starting transfers between devices: 25.2 us -> 0 us
  local copies, waits for them, and re-layouts: 8.69 us -> 3.29 us
    all_to_all x1 -> x3, blocking collectives: 21.1 us -> 153 us  [the longest x1 71.8 us: body(): lax.all_to_all(packed.reshape(devices, rows + extra, 1, LANES), both, 0,...]
    all_to_all x3 -> x0, waiting for transfers between devices: 118 us -> none  [the longest x1 57.6 us: body(): lax.all_to_all(returned.reshape(devices, rows, LANES), both, 0, 0, tiled=...]
    pallas_call x3, Pallas kernels: 82.5 us -> 38.9 us  [the longest x1 24.9 us: body(): pl.pallas_call(functools.partial(transform_kernel, modes=modes, row_devic...]
    all_to_all x3 -> x0, starting transfers between devices: 25.2 us -> none  [the longest x1 11.5 us: body(): base = lax.all_to_all(base, both, 0, 0, tiled=True)]
  transfers between devices with their start and end apart: 3 -> 0, of which waited for: 3 -> 0; matrix products, arithmetic and copies ran while one was open for 1% -> 0% of each run, Pallas kernels for 2% -> 0%
where the time goes in v2:
time: 204 us; the launch traced here: 203 us
  blocking collectives  153 us (75%)
  Pallas kernels  46.6 us (23%)
  local copies, waits for them, and re-layouts  3.29 us (2%)
    all_to_all x1, blocking collectives, body(): lax.all_to_all(packed.reshape(devices, rows + extra, 1, LANES), both, 0,...  71.8 us
    all_to_all x1, blocking collectives, body(): lax.all_to_all(returned.reshape(devices, rows, LANES), both, 0, 0, tiled=...  62.9 us
    pallas_call x1, Pallas kernels, body(): pl.pallas_call(functools.partial(transform_kernel, modes=modes, row_devic...  24.9 us
    all_to_all x1, blocking collectives, body(): lax.all_to_all(grams, both, 0, 0, tiled=True)  17.9 us
    pallas_call x1, Pallas kernels, body(): pl.pallas_call(functools.partial(column_kernel, modes=modes, planes=plane...  13.5 us
    pallas_call x1, Pallas kernels, body(): pl.pallas_call(functools.partial(finish_kernel, devices=devices, vecs=vec...  7.64 us

profile of v2, /device:TPU:1, one launch (start us, length us, event | category | flops | bytes accessed | tf_op | source)
XLA Modules:
  0.0 203.3 jit_solution(9057268297786248100)
XLA Ops:
  0.6 0.0 copy-start
  0.6 2.3 %copy-done = f32[12,128,768]{2,1,0:T(8,128)S(1)} copy-done((f32[12,128,768]{2,1,0:T(8,128)S(1)}, f32[12,128,768]{2,1,0:T(8,128)}, u32[]{:S(2)}) %copy-start) | copy-done | bytes 4718616
  3.0 0.0 copy-start.1
  3.0 0.9 copy-done.1
  3.9 0.5 pack.1
  4.4 0.0 copy-start.6
  4.4 0.0 copy-start.7
  4.4 0.0 copy-start.8
  4.4 0.0 copy-start.9
  4.4 71.8 %all_to_all.15 = f32[128,75,1,128]{3,2,1,0:T(1,128)S(1)} all-to-all(f32[128,75,1,128]{3,2,1,0:T(1,128)S(1)} %bitcast.11), channel_id=1, replica_groups=mesh['row'=16,'col'=8] {'row','col'}, dimensions={0} | all-to-all | bytes 9830400 | tf_op jit(solution)/shard_map/all_to_all | solution.py:337
  76.2 0.0 copy-done.6
  76.2 0.0 copy-done.7
  76.2 0.0 copy-done.8
  76.2 0.0 copy-done.9
  76.3 24.9 %transform.1 = f32[9216,128]{1,0:T(8,128)S(1)} custom-call(f32[9600,128]{1,0:T(8,128)S(1)} %bitcast.12, bf16[2,192,256]{2,1,0:T(8,128)(2,1)S(1)} %copy-done.9, bf16[2,192,192]{2,1,0:T(8,128)(2,1)S(1)} %copy-done.8, bf16[2,192,192]{2,1,0:T(8,128)(2,1)S(1)} %copy-done.7, bf16[2,192,256]{2,1,0:T(8,128)(2,1)S(1)} %copy-done.6), custom_call_target="tpu_custom_call" | custom-call | flops 20000000000 | bytes 9437184 | tf_op jit(solution)/shard_map/transform/pallas_call | solution.py:341
  101.2 0.0 copy-start.2
  101.2 0.0 copy-start.3
  101.2 0.0 copy-start.4
  101.2 0.0 copy-start.5
  101.2 62.9 %all_to_all.16 = f32[128,72,128]{2,1,0:T(8,128)S(1)} all-to-all(f32[128,72,128]{2,1,0:T(8,128)S(1)} %bitcast.13), channel_id=1, replica_groups=mesh['row'=16,'col'=8] {'row','col'}, dimensions={0} | all-to-all | bytes 9437184 | tf_op jit(solution)/shard_map/all_to_all | solution.py:355
  164.1 0.0 copy-done.2
  164.1 0.0 copy-done.3
  164.1 0.0 copy-done.4
  164.1 0.0 copy-done.5
  164.1 13.5 %column.1 = (f32[1536,768]{1,0:T(8,128)S(1)}, f32[128,8,128]{2,1,0:T(8,128)S(1)}) custom-call(f32[9216,128]{1,0:T(8,128)S(1)} %bitcast.14, f32[12,128,768]{2,1,0:T(8,128)} %q_ref.3, s32[12,24]{1,0:T(8,128)S(1)} %copy-done.4, f32[1,128]{1,0:T(1,128)S(1)} %bitcast.17, f32[128,128]{1,0:T(8,128)S(1)} %copy-done.2, f32[128,128]{1,0:T(8,128)S(1)} %copy-done.3), custom_call_target="tpu_custom_call" | custom-call | flops 10000000000 | bytes 14155776 | tf_op jit(solution)/shard_map/column/pallas_call | solution.py:361
  177.7 17.9 %all_to_all.17 = f32[128,8,128]{2,1,0:T(8,128)S(1)} all-to-all(f32[128,8,128]{2,1,0:T(8,128)S(1)} %get-tuple-element.6), channel_id=1, replica_groups=mesh['row'=16,'col'=8] {'row','col'}, dimensions={0} | all-to-all | bytes 1048576 | tf_op jit(solution)/shard_map/all_to_all | solution.py:388
  195.6 7.6 %finish.1 = (f32[1536,768]{1,0:T(8,128)}, f32[1,32]{1,0:T(1,128)}) custom-call(f32[1024,128]{1,0:T(8,128)S(1)} %bitcast.15, f32[1536,768]{1,0:T(8,128)S(1)} %get-tuple-element.7.stepped_ref), custom_call_target="tpu_custom_call" | custom-call | flops 603979776 | bytes 9437184 | tf_op jit(solution)/shard_map/finish/pallas_call | solution.py:391
Async XLA Ops:
  0.6 2.3 %copy-start = (f32[12,128,768]{2,1,0:T(8,128)S(1)}, f32[12,128,768]{2,1,0:T(8,128)}, u32[]{:S(2)}) copy-start(f32[12,128,768]{2,1,0:T(8,128)} %q_ref.3) | copy-start | bytes 14155780
  3.0 0.9 copy-start.1
  4.4 71.9 %copy-start.6 = (bf16[2,192,256]{2,1,0:T(8,128)(2,1)S(1)}, bf16[2,192,256]{2,1,0:T(8,128)(2,1)}, u32[]{:S(2)}) copy-start(bf16[2,192,256]{2,1,0:T(8,128)(2,1)} %constant.11.clone.g_ref) | copy-start | bytes 589828
  4.4 71.8 %copy-start.7 = (bf16[2,192,192]{2,1,0:T(8,128)(2,1)S(1)}, bf16[2,192,192]{2,1,0:T(8,128)(2,1)}, u32[]{:S(2)}) copy-start(bf16[2,192,192]{2,1,0:T(8,128)(2,1)} %constant.10.clone.az_ref) | copy-start | bytes 442372
  4.4 71.8 %copy-start.8 = (bf16[2,192,192]{2,1,0:T(8,128)(2,1)S(1)}, bf16[2,192,192]{2,1,0:T(8,128)(2,1)}, u32[]{:S(2)}) copy-start(bf16[2,192,192]{2,1,0:T(8,128)(2,1)} %constant.9.clone.sz_ref) | copy-start | bytes 442372
  4.4 71.8 %copy-start.9 = (bf16[2,192,256]{2,1,0:T(8,128)(2,1)S(1)}, bf16[2,192,256]{2,1,0:T(8,128)(2,1)}, u32[]{:S(2)}) copy-start(bf16[2,192,256]{2,1,0:T(8,128)(2,1)} %constant.8.clone.sx_ref) | copy-start | bytes 589828
  101.2 62.9 %copy-start.2 = (f32[128,128]{1,0:T(8,128)S(1)}, f32[128,128]{1,0:T(8,128)}, u32[]{:S(2)}) copy-start(f32[128,128]{1,0:T(8,128)} %to_ref.1) | copy-start | bytes 196612
  101.2 62.9 %copy-start.3 = (f32[128,128]{1,0:T(8,128)S(1)}, f32[128,128]{1,0:T(8,128)}, u32[]{:S(2)}) copy-start(f32[128,128]{1,0:T(8,128)} %from_ref.1) | copy-start | bytes 196612
  101.2 62.9 %copy-start.4 = (s32[12,24]{1,0:T(8,128)S(1)}, s32[12,24]{1,0:T(8,128)}, u32[]{:S(2)}) copy-start(s32[12,24]{1,0:T(8,128)} %mask_ref.1) | copy-start | bytes 3460
  101.2 62.9 %copy-start.5 = (f32[128]{0:T(128)S(1)}, f32[128]{0:T(128)}, u32[]{:S(2)}) copy-start(f32[128]{0:T(128)} %param.13) | copy-start | bytes 1540

commit v3 on v2

--- a/solution.py
+++ b/solution.py
@@ -64,6 +64,18 @@
     return dot(a[0], b[0], dims) + (dot(a[0], b[1], dims) + dot(a[1], b[0], dims))
 
 
+def stacked_dot(table, x):
+    high, low = split(x)
+    return dot(table, jnp.concatenate([high, high], axis=0), NN) + dot(
+        table[:, : x.shape[0]], low, NN
+    )
+
+
+def table_dot(table_ref, x):
+    high, low = split(x)
+    return dot(table_ref[...], jnp.concatenate([high, high, low], axis=0), NN)
+
+
 def pack_kernel(q_ref, base_ref, out_ref, *, modes, planes, tiles, extra, step_modes):
     stride = modes * tiles + extra
 
@@ -91,21 +103,16 @@
     y_refs, z_refs = scratch[:halves], scratch[halves:]
     rows = modes * tiles
     stride = rows + extra
-    hop = col_devices * stride
     x_count = modes * row_devices
-    height = tiles * LANES
+    z_count = sz_ref.shape[0]
+    z_length = z_count // col_devices
+    pitch = y_refs[0].shape[0] // vecs
+    per_tile = LANES // vecs
 
     turned = []
     for k in range(extra):
-        block = jnp.concatenate(
-            [
-                d_ref[pl.ds(c * stride + rows + k, row_devices, stride=hop), :]
-                for c in range(col_devices)
-            ],
-            axis=0,
-        )
+        block = d_ref[pl.ds(rows + k, row_devices * col_devices, stride=stride), :]
         turned.append(block.T)
-    z_length = sz_ref.shape[2] // col_devices
     slot = lax.broadcasted_iota(jnp.int32, (z_length, LANES), 1) // row_devices
     slots = LANES // row_devices
     share = modes // extra
@@ -119,33 +126,35 @@
             parts[m // slots] = jnp.where(slot == m % slots, piece, parts[m // slots])
         sheets.append(jnp.concatenate(parts, axis=1))
     base = jnp.concatenate(sheets, axis=0)[:, :x_count]
-    half_way = dot3(split(base), (sx_ref[0], sx_ref[1]), NN)
-    speed_ref[...] = dot3((sz_ref[0], sz_ref[1]), split(half_way), NN)
+    sx = (sx_ref[:x_count], sx_ref[2 * x_count :])
+    speed_ref[...] = table_dot(sz_ref, dot3(split(base), sx, NN))
 
     def forward_x(c, carry):
         parts = []
         for nb in range(tiles):
-            start = c * stride + nb * modes
+            start = c * (row_devices * stride) + nb * modes
             block = jnp.concatenate(
-                [d_ref[pl.ds(start + m, row_devices, stride=hop), :] for m in range(modes)],
+                [d_ref[pl.ds(start + m, row_devices, stride=stride), :] for m in range(modes)],
                 axis=0,
             )
-            parts.append(block.T)
-        mixed = dot3(split(jnp.concatenate(parts, axis=0)), (sx_ref[0], sx_ref[1]), NN)
-        at = pl.ds(pl.multiple_of(c * height, height), height)
-        for k, y_ref in enumerate(y_refs):
-            y_ref[at, :] = mixed[:, k * LANES : (k + 1) * LANES]
+            block = jnp.concatenate(split(block), axis=0).T
+            parts.append(jnp.concatenate([block, block[:, :x_count]], axis=1))
+        mixed = dot(jnp.concatenate(parts, axis=0), sx_ref[...], NN)
+        for n in range(z_length):
+            for k, y_ref in enumerate(y_refs):
+                y_ref[pl.ds(c * z_length + n, vecs, stride=pitch), :] = mixed[
+                    n * vecs : (n + 1) * vecs, k * LANES : (k + 1) * LANES
+                ]
         return carry
 
     lax.fori_loop(0, col_devices, forward_x, 0, unroll=4)
 
     def plane(i, carry):
         for j in range(4):
-            at = pl.ds(i * 4 + j, y_refs[0].shape[0] // vecs, stride=vecs)
+            at = pl.ds(pl.multiple_of((i * 4 + j) * pitch, 8), z_count)
             mixed = jnp.concatenate([y_ref[at, :] for y_ref in y_refs], axis=1)
-            physical = dot3((sz_ref[0], sz_ref[1]), split(mixed), NN)
-            product = physical * speed_ref[...]
-            mixed = dot3((az_ref[0], az_ref[1]), split(product), NN)
+            product = table_dot(sz_ref, mixed) * speed_ref[...]
+            mixed = table_dot(az_ref, product)
             for k, z_ref in enumerate(z_refs):
                 z_ref[at, :] = mixed[:, k * LANES : (k + 1) * LANES]
         return carry
@@ -155,26 +164,33 @@
     batch = 3
 
     def inverse_x(i, carry):
-        at = pl.ds(pl.multiple_of(i * (batch * LANES), LANES), batch * LANES)
-        block = split(jnp.concatenate([z_ref[at, :] for z_ref in z_refs], axis=1))
-        back = dot3((g_ref[0], g_ref[1]), block, NT)
         c, group = i // (tiles // batch), i % (tiles // batch)
+        first = c * z_length + group * (batch * per_tile)
+        block = jnp.concatenate(
+            [
+                jnp.concatenate(
+                    [z_ref[pl.ds(first + n, vecs, stride=pitch), :] for z_ref in z_refs], axis=1
+                )
+                for n in range(batch * per_tile)
+            ],
+            axis=0,
+        )
+        high, low = split(block)
+        back = dot(g_ref[...], jnp.concatenate([high, high, low], axis=1), NT)
         for nb in range(batch):
-            start = c * stride + (group * batch + nb) * modes
+            start = c * (row_devices * rows) + (group * batch + nb) * modes
             for m in range(modes):
-                out_ref[pl.ds(start + m, row_devices, stride=hop), :] = back[
+                out_ref[pl.ds(start + m, row_devices, stride=rows), :] = back[
                     m * row_devices : (m + 1) * row_devices, nb * LANES : (nb + 1) * LANES
                 ]
         return carry
 
-    stride = rows
-    hop = col_devices * stride
     lax.fori_loop(0, col_devices * tiles // batch, inverse_x, 0, unroll=4)
 
 
 def column_kernel(
     nl_ref, q_ref, mask_ref, decay_ref, to_ref, from_ref, stepped_ref, gram_ref,
-    mask_s, wave_s, decay_s, high_s, cross_s,
+    mask_s, wave_s, decay_s, gram_s,
     *, modes, planes, tiles, vecs, step_modes, x_count, z_count, z_length,
 ):
     width = tiles * LANES
@@ -193,13 +209,12 @@
         wave_z = jnp.where(n <= z_count // 2, n, n - z_count // 2).astype(F32) * BETA_Z
         wave_s[...] = STEP_COEF + VISCOSITY * (wave_x * wave_x + wave_z * wave_z)
         decay_s[...] = jnp.broadcast_to(decay_ref[...], (LANES, planes)).T
-        high_s[...] = jnp.zeros_like(high_s)
-        cross_s[...] = jnp.zeros_like(cross_s)
-
-    to_eigen = split(to_ref[...])
-    from_eigen = split(from_ref[...])
+        gram_s[...] = jnp.zeros_like(gram_s)
+
+    to_eigen = jnp.concatenate(split(to_ref[...]), axis=1)
+    from_eigen = jnp.concatenate(split(from_ref[...]), axis=1)
     decay = jnp.concatenate([decay_s[...]] * tiles, axis=1)
-    high, cross = high_s[...], cross_s[...]
+    gram = gram_s[...]
     for k in range(step_modes):
         m = pl.program_id(0) * step_modes + k
         nonlinear = jnp.concatenate(
@@ -210,21 +225,21 @@
             axis=1,
         )
         right = STEP_COEF * q_ref[k] + nonlinear * mask_s[pl.ds(m, 1), :]
-        eigen = dot3(to_eigen, split(right), NN)
+        eigen = stacked_dot(to_eigen, right)
         eigen = eigen / (wave_s[pl.ds(m, 1), :] + decay)
-        stepped = dot3(from_eigen, split(eigen), NN)
+        stepped = stacked_dot(from_eigen, eigen)
         stepped_ref[pl.ds(pl.multiple_of(m * planes, planes), planes), :] = stepped
-        stacked = [
-            jnp.concatenate([x[:, nb * LANES : (nb + 1) * LANES] for nb in range(tiles)], axis=0)
-            for x in split(stepped)
-        ]
-        high = high + dot(stacked[0], stacked[0], TN)
-        cross = cross + dot(stacked[0], stacked[1], TN)
-    high_s[...] = high
-    cross_s[...] = cross
+        columns = [stepped[:, nb * LANES : (nb + 1) * LANES] for nb in range(tiles)]
+        left = jnp.concatenate([x.T.astype(BF16) for x in columns], axis=1)
+        right = jnp.concatenate(
+            [jnp.concatenate(split(x), axis=1) for x in columns], axis=0
+        )
+        gram = gram + dot(left, right, NN)
+    gram_s[...] = gram
 
     @pl.when(pl.program_id(0) == pl.num_programs(0) - 1)
     def _():
+        high, cross = gram[:, :LANES], gram[:, LANES:]
         full = (high + (cross + cross.T)) * (1.0 / (x_count * planes * z_count))
         group = LANES // vecs
         lane = lax.broadcasted_iota(jnp.int32, (vecs, LANES), 1) // vecs
@@ -303,7 +318,8 @@
     rows = modes * tiles
     extra = -(-modes * z_length // LANES)
     size = tangents.size * 4
-    both = ("row", "col")
+    both = ("col", "row")
+    pitch = 8 * (z_count // 8 + 1 - z_count // 8 % 2)
     big = pltpu.CompilerParams(vmem_limit_bytes=40 * 2**20)
     small = pltpu.CompilerParams(vmem_limit_bytes=24 * 2**20)
 
@@ -311,10 +327,19 @@
     order = (order % row_devices) * modes + order // row_devices
     halves = -(-x_count // LANES)
     fill = ((0, 0), (0, halves * LANES - x_count))
-    sx = halves_of_table(np.pad(synthesis(x_count)[:, order].T, fill))
-    sz = halves_of_table(synthesis(z_count))
-    az = halves_of_table(analysis(z_count))
-    gx = halves_of_table(np.pad(derivative_analysis(x_count, ALPHA_X)[order], fill))
+    sx_high, sx_low = halves_of_table(np.pad(synthesis(x_count)[:, order].T, fill))
+    sx = np.concatenate([sx_high, sx_high, sx_low], axis=0)
+    sz, az, gx = (
+        np.concatenate([high, low, high], axis=1)
+        for high, low in map(
+            halves_of_table,
+            (
+                synthesis(z_count),
+                analysis(z_count),
+                np.pad(derivative_analysis(x_count, ALPHA_X)[order], fill),
+            ),
+        )
+    )
 
     steps = 4
     base = jnp.transpose(base_flow, (0, 2, 1)).reshape(modes * z_length, planes)
@@ -347,7 +372,7 @@
         in_specs=[vmem()] * 5,
         out_specs=vmem(),
         scratch_shapes=[pltpu.VMEM((z_count, halves * LANES), F32)]
-        + [pltpu.VMEM((z_count * vecs, LANES), F32)] * (2 * halves),
+        + [pltpu.VMEM((pitch * vecs, LANES), F32)] * (2 * halves),
         cost_estimate=cost(2 * 10**10, 2 * size),
         compiler_params=big,
         name="transform",
@@ -361,16 +386,16 @@
     stepped, grams = pl.pallas_call(
         functools.partial(
             column_kernel, modes=modes, planes=planes, tiles=tiles, vecs=vecs,
-            step_modes=modes // steps, x_count=x_count, z_count=z_count, z_length=z_length,
+            step_modes=modes // 2, x_count=x_count, z_count=z_count, z_length=z_length,
         ),
         out_shape=[
             jax.ShapeDtypeStruct((height, width), F32),
             jax.ShapeDtypeStruct((devices, piece, LANES), F32),
         ],
-        grid=(steps,),
+        grid=(2,),
         in_specs=[
             vmem(),
-            pl.BlockSpec((modes // steps, planes, width), lambda i: (i, 0, 0)),
+            pl.BlockSpec((modes // 2, planes, width), lambda i: (i, 0, 0)),
         ]
         + [vmem()] * 4,
         out_specs=[vmem()] * 2,
@@ -378,8 +403,7 @@
             pltpu.VMEM((modes, width), F32),
             pltpu.VMEM((modes, width), F32),
             pltpu.VMEM((planes, LANES), F32),
-            pltpu.VMEM((LANES, LANES), F32),
-            pltpu.VMEM((LANES, LANES), F32),
+            pltpu.VMEM((LANES, 2 * LANES), F32),
         ],
         cost_estimate=cost(10**10, 3 * size),
         compiler_params=big,
@@ -387,7 +411,7 @@
     )(nonlinear, tangents, mode_mask, decay_rates[None, :], to_eigen, from_eigen)
     grams = lax.all_to_all(grams, both, 0, 0, tiled=True).reshape(devices * piece, LANES)
 
-    block = height // 6
+    block = height // 3
     vectors, growth = pl.pallas_call(
         functools.partial(finish_kernel, devices=devices, vecs=vecs, wide=2 * LANES),
         out_shape=[

time: 204 us -> 188 us (0.922)
  Pallas kernels: 46.6 us -> 30.5 us
    pallas_call x1, Pallas kernels: 24.9 us -> 15.5 us  [body(): pl.pallas_call(functools.partial(transform_kernel, modes=modes, row_devic...]
    pallas_call x1, Pallas kernels: 13.5 us -> 7.65 us  [body(): pl.pallas_call(functools.partial(column_kernel, modes=modes, planes=plane...]
where the time goes in v3:
time: 188 us; the launch traced here: 187 us
  blocking collectives  153 us (81%)
  Pallas kernels  30.5 us (16%)
  local copies, waits for them, and re-layouts  3.29 us (2%)
    all_to_all x1, blocking collectives, body(): lax.all_to_all(packed.reshape(devices, rows + extra, 1, LANES), both, 0,...  72.1 us
    all_to_all x1, blocking collectives, body(): lax.all_to_all(returned.reshape(devices, rows, LANES), both, 0, 0, tiled=...  62.8 us
    all_to_all x1, blocking collectives, body(): lax.all_to_all(grams, both, 0, 0, tiled=True)  17.9 us
    pallas_call x1, Pallas kernels, body(): pl.pallas_call(functools.partial(transform_kernel, modes=modes, row_devic...  15.5 us
    pallas_call x1, Pallas kernels, body(): pl.pallas_call(functools.partial(column_kernel, modes=modes, planes=plane...  7.65 us
    pallas_call x1, Pallas kernels, body(): pl.pallas_call(functools.partial(finish_kernel, devices=devices, vecs=vec...  6.84 us

profile of v3, /device:TPU:1, one launch (start us, length us, event | category | flops | bytes accessed | tf_op | source)
XLA Modules:
  0.0 187.4 jit_solution(8949141993359629493)
XLA Ops:
  0.6 0.0 copy-start
  0.6 2.3 %copy-done = f32[12,128,768]{2,1,0:T(8,128)S(1)} copy-done((f32[12,128,768]{2,1,0:T(8,128)S(1)}, f32[12,128,768]{2,1,0:T(8,128)}, u32[]{:S(2)}) %copy-start) | copy-done | bytes 4718616
  3.0 0.0 copy-start.1
  3.0 0.9 copy-done.1
  3.9 0.5 pack.1
  4.4 0.0 copy-start.6
  4.4 0.0 copy-start.7
  4.4 0.0 copy-start.8
  4.4 0.0 copy-start.9
  4.4 72.1 %all_to_all.15 = f32[128,75,1,128]{3,2,1,0:T(1,128)S(1)} all-to-all(f32[128,75,1,128]{3,2,1,0:T(1,128)S(1)} %bitcast.11), channel_id=1, replica_groups=mesh['row'=16,'col'=8] {'col','row'}, dimensions={0} | all-to-all | bytes 9830400 | tf_op jit(solution)/shard_map/all_to_all | solution.py:362
  76.6 0.0 copy-done.6
  76.6 0.0 copy-done.7
  76.6 0.0 copy-done.8
  76.6 0.0 copy-done.9
  76.6 15.5 %transform.1 = f32[9216,128]{1,0:T(8,128)S(1)} custom-call(f32[9600,128]{1,0:T(8,128)S(1)} %bitcast.12, bf16[576,256]{1,0:T(8,128)(2,1)S(1)} %copy-done.7, bf16[192,576]{1,0:T(8,128)(2,1)S(1)} %copy-done.9, bf16[192,576]{1,0:T(8,128)(2,1)S(1)} %copy-done.8, bf16[192,768]{1,0:T(8,128)(2,1)S(1)} %copy-done.6), custom_call_target="tpu_custom_call" | custom-call | flops 20000000000 | bytes 9437184 | tf_op jit(solution)/shard_map/transform/pallas_call | solution.py:366
  92.1 0.0 copy-start.2
  92.1 0.0 copy-start.3
  92.1 0.0 copy-start.4
  92.1 0.0 copy-start.5
  92.1 62.8 %all_to_all.16 = f32[128,72,128]{2,1,0:T(8,128)S(1)} all-to-all(f32[128,72,128]{2,1,0:T(8,128)S(1)} %bitcast.13), channel_id=1, replica_groups=mesh['row'=16,'col'=8] {'col','row'}, dimensions={0} | all-to-all | bytes 9437184 | tf_op jit(solution)/shard_map/all_to_all | solution.py:380
  155.0 0.0 copy-done.2
  155.0 0.0 copy-done.3
  155.0 0.0 copy-done.4
  155.0 0.0 copy-done.5
  155.0 7.6 %column.1 = (f32[1536,768]{1,0:T(8,128)S(1)}, f32[128,8,128]{2,1,0:T(8,128)S(1)}) custom-call(f32[9216,128]{1,0:T(8,128)S(1)} %bitcast.14, f32[12,128,768]{2,1,0:T(8,128)} %q_ref.3, s32[12,24]{1,0:T(8,128)S(1)} %copy-done.4, f32[1,128]{1,0:T(1,128)S(1)} %bitcast.17, f32[128,128]{1,0:T(8,128)S(1)} %copy-done.2, f32[128,128]{1,0:T(8,128)S(1)} %copy-done.3), custom_call_target="tpu_custom_call" | custom-call | flops 10000000000 | bytes 14155776 | tf_op jit(solution)/shard_map/column/pallas_call | solution.py:386
  162.7 17.9 %all_to_all.17 = f32[128,8,128]{2,1,0:T(8,128)S(1)} all-to-all(f32[128,8,128]{2,1,0:T(8,128)S(1)} %get-tuple-element.6), channel_id=1, replica_groups=mesh['row'=16,'col'=8] {'col','row'}, dimensions={0} | all-to-all | bytes 1048576 | tf_op jit(solution)/shard_map/all_to_all | solution.py:412
  180.6 6.8 %finish.1 = (f32[1536,768]{1,0:T(8,128)}, f32[1,32]{1,0:T(1,128)}) custom-call(f32[1024,128]{1,0:T(8,128)S(1)} %bitcast.15, f32[1536,768]{1,0:T(8,128)S(1)} %get-tuple-element.7.stepped_ref), custom_call_target="tpu_custom_call" | custom-call | flops 603979776 | bytes 9437184 | tf_op jit(solution)/shard_map/finish/pallas_call | solution.py:415
Async XLA Ops:
  0.6 2.3 %copy-start = (f32[12,128,768]{2,1,0:T(8,128)S(1)}, f32[12,128,768]{2,1,0:T(8,128)}, u32[]{:S(2)}) copy-start(f32[12,128,768]{2,1,0:T(8,128)} %q_ref.3) | copy-start | bytes 14155780
  3.0 0.9 copy-start.1
  4.4 72.2 %copy-start.6 = (bf16[192,768]{1,0:T(8,128)(2,1)S(1)}, bf16[192,768]{1,0:T(8,128)(2,1)}, u32[]{:S(2)}) copy-start(bf16[192,768]{1,0:T(8,128)(2,1)} %constant.11.clone.g_ref) | copy-start | bytes 884740
  4.4 72.2 %copy-start.7 = (bf16[576,256]{1,0:T(8,128)(2,1)S(1)}, bf16[576,256]{1,0:T(8,128)(2,1)}, u32[]{:S(2)}) copy-start(bf16[576,256]{1,0:T(8,128)(2,1)} %constant.8.clone.sx_ref) | copy-start | bytes 884740
  4.4 72.2 %copy-start.8 = (bf16[192,576]{1,0:T(8,128)(2,1)S(1)}, bf16[192,576]{1,0:T(8,128)(2,1)}, u32[]{:S(2)}) copy-start(bf16[192,576]{1,0:T(8,128)(2,1)} %constant.10.clone.az_ref) | copy-start | bytes 663556
  4.4 72.1 %copy-start.9 = (bf16[192,576]{1,0:T(8,128)(2,1)S(1)}, bf16[192,576]{1,0:T(8,128)(2,1)}, u32[]{:S(2)}) copy-start(bf16[192,576]{1,0:T(8,128)(2,1)} %constant.9.clone.sz_ref) | copy-start | bytes 663556
  92.1 62.9 %copy-start.2 = (f32[128,128]{1,0:T(8,128)S(1)}, f32[128,128]{1,0:T(8,128)}, u32[]{:S(2)}) copy-start(f32[128,128]{1,0:T(8,128)} %to_ref.1) | copy-start | bytes 196612
  92.1 62.9 %copy-start.3 = (f32[128,128]{1,0:T(8,128)S(1)}, f32[128,128]{1,0:T(8,128)}, u32[]{:S(2)}) copy-start(f32[128,128]{1,0:T(8,128)} %from_ref.1) | copy-start | bytes 196612
  92.1 62.9 %copy-start.4 = (s32[12,24]{1,0:T(8,128)S(1)}, s32[12,24]{1,0:T(8,128)}, u32[]{:S(2)}) copy-start(s32[12,24]{1,0:T(8,128)} %mask_ref.1) | copy-start | bytes 3460
  92.1 62.9 %copy-start.5 = (f32[128]{0:T(128)S(1)}, f32[128]{0:T(128)}, u32[]{:S(2)}) copy-start(f32[128]{0:T(128)} %param.13) | copy-start | bytes 1540

commit v4 on v3

--- a/solution.py
+++ b/solution.py
@@ -76,22 +76,24 @@
     return dot(table_ref[...], jnp.concatenate([high, high, low], axis=0), NN)
 
 
-def pack_kernel(q_ref, base_ref, out_ref, *, modes, planes, tiles, extra, step_modes):
+def pack_kernel(q_ref, base_ref, out_ref, q_s, base_s, sems, *, modes, planes, tiles, extra):
     stride = modes * tiles + extra
-
-    @pl.when(pl.program_id(0) == 0)
-    def _():
-        part = base_ref.shape[0] // extra
-        fill = jnp.zeros((LANES - part, planes), F32)
-        for k in range(extra):
-            block = jnp.concatenate([base_ref[k * part : (k + 1) * part, :], fill], axis=0)
-            out_ref[pl.ds(modes * tiles + k, planes, stride=stride), :] = block.T
-
-    for k in range(step_modes):
-        m = pl.program_id(0) * step_modes + k
+    copies = [pltpu.make_async_copy(q_ref.at[m], q_s.at[m], sems.at[m]) for m in range(modes)]
+    base_copy = pltpu.make_async_copy(base_ref, base_s, sems.at[modes])
+    base_copy.start()
+    for copy in copies:
+        copy.start()
+    base_copy.wait()
+    part = base_s.shape[0] // extra
+    fill = jnp.zeros((LANES - part, planes), F32)
+    for k in range(extra):
+        block = jnp.concatenate([base_s[k * part : (k + 1) * part, :], fill], axis=0)
+        out_ref[pl.ds(modes * tiles + k, planes, stride=stride), :] = block.T
+    for m, copy in enumerate(copies):
+        copy.wait()
         for nb in range(tiles):
-            out_ref[pl.ds(nb * modes + m, planes, stride=stride), :] = q_ref[
-                k, :, nb * LANES : (nb + 1) * LANES
+            out_ref[pl.ds(nb * modes + m, planes, stride=stride), :] = q_s[
+                m, :, nb * LANES : (nb + 1) * LANES
             ]
 
 
@@ -147,45 +149,69 @@
                 ]
         return carry
 
-    lax.fori_loop(0, col_devices, forward_x, 0, unroll=4)
+    lax.fori_loop(0, col_devices, forward_x, 0, unroll=8)
+
+    y_low, y_high = y_refs
+    z_low, z_high = z_refs
+    first = lax.broadcasted_iota(jnp.int32, (z_count, LANES), 1) < LANES // 2
+    batch = 8
 
     def plane(i, carry):
-        for j in range(4):
-            at = pl.ds(pl.multiple_of((i * 4 + j) * pitch, 8), z_count)
-            mixed = jnp.concatenate([y_ref[at, :] for y_ref in y_refs], axis=1)
-            product = table_dot(sz_ref, mixed) * speed_ref[...]
-            mixed = table_dot(az_ref, product)
-            for k, z_ref in enumerate(z_refs):
-                z_ref[at, :] = mixed[:, k * LANES : (k + 1) * LANES]
+        ats = [
+            pl.ds(pl.multiple_of((i * batch + j) * pitch, 8), z_count) for j in range(batch)
+        ]
+        mixed = jnp.concatenate(
+            [y_low[at, :] for at in ats]
+            + [
+                jnp.where(first, y_high[ats[j], :], y_high[ats[j + 1], :])
+                for j in range(0, batch, 2)
+            ],
+            axis=1,
+        )
+        speed = jnp.concatenate(
+            [speed_ref[:, :LANES]] * batch + [speed_ref[:, LANES:]] * (batch // 2), axis=1
+        )
+        mixed = table_dot(az_ref, table_dot(sz_ref, mixed) * speed)
+        for j, at in enumerate(ats):
+            k = batch + j // 2
+            z_low[at, :] = mixed[:, j * LANES : (j + 1) * LANES]
+            z_high[at, :] = mixed[:, k * LANES : (k + 1) * LANES]
         return carry
 
-    lax.fori_loop(0, vecs // 4, plane, 0, unroll=2)
-
-    batch = 3
-
-    def inverse_x(i, carry):
-        c, group = i // (tiles // batch), i % (tiles // batch)
-        first = c * z_length + group * (batch * per_tile)
+    lax.fori_loop(0, vecs // batch, plane, 0, unroll=2)
+
+    rows_of = lax.broadcasted_iota(jnp.int32, (vecs, LANES), 0)
+    lanes_of = lax.broadcasted_iota(jnp.int32, (vecs, LANES), 1)
+    mine = (rows_of % 2) == (lanes_of // (LANES // 2))
+
+    def inverse_x(c, carry):
         block = jnp.concatenate(
             [
                 jnp.concatenate(
-                    [z_ref[pl.ds(first + n, vecs, stride=pitch), :] for z_ref in z_refs], axis=1
+                    [
+                        z_low[pl.ds(c * z_length + n, vecs, stride=pitch), :],
+                        jnp.where(
+                            mine, z_high[pl.ds(c * z_length + n, vecs, stride=pitch), :], 0.0
+                        ),
+                    ],
+                    axis=1,
                 )
-                for n in range(batch * per_tile)
+                for n in range(z_length)
             ],
             axis=0,
         )
         high, low = split(block)
-        back = dot(g_ref[...], jnp.concatenate([high, high, low], axis=1), NT)
-        for nb in range(batch):
-            start = c * (row_devices * rows) + (group * batch + nb) * modes
+        both = dot(g_ref[...], high, NT)
+        back = both[:x_count] + (both[x_count:] + dot(g_ref[:x_count], low, NT))
+        for nb in range(tiles):
+            start = c * (row_devices * rows) + nb * modes
             for m in range(modes):
                 out_ref[pl.ds(start + m, row_devices, stride=rows), :] = back[
                     m * row_devices : (m + 1) * row_devices, nb * LANES : (nb + 1) * LANES
                 ]
         return carry
 
-    lax.fori_loop(0, col_devices * tiles // batch, inverse_x, 0, unroll=4)
+    lax.fori_loop(0, col_devices, inverse_x, 0, unroll=8)
 
 
 def column_kernel(
@@ -224,7 +250,7 @@
             ],
             axis=1,
         )
-        right = STEP_COEF * q_ref[k] + nonlinear * mask_s[pl.ds(m, 1), :]
+        right = STEP_COEF * q_ref[m] + nonlinear * mask_s[pl.ds(m, 1), :]
         eigen = stacked_dot(to_eigen, right)
         eigen = eigen / (wave_s[pl.ds(m, 1), :] + decay)
         stepped = stacked_dot(from_eigen, eigen)
@@ -256,7 +282,7 @@
         gram_ref[...] = jnp.broadcast_to(packed[None], gram_ref.shape)
 
 
-def finish_kernel(grams_ref, stepped_ref, vectors_ref, growth_ref, w_ref, *, devices, vecs, wide):
+def finish_kernel(grams_ref, stepped_ref, vectors_ref, growth_ref, w_ref, *, devices, vecs, panel):
     group = LANES // vecs
     piece = vecs // group
 
@@ -269,11 +295,18 @@
         lane = lax.broadcasted_iota(jnp.int32, (vecs, LANES), 1)
         row = lax.broadcasted_iota(jnp.int32, (vecs, LANES), 0)
         work = jnp.where(lane < vecs, gram, jnp.where(lane == row + vecs, 1.0, 0.0))
-        for k in range(vecs - 1):
-            pivot_row = work[k : k + 1, :]
-            scaled = pivot_row / work[k : k + 1, k : k + 1]
-            column = jnp.broadcast_to(work[:, k : k + 1], (vecs, LANES))
-            work = work - jnp.where(row > k, column * scaled, 0.0)
+        for first in range(0, vecs, panel):
+            own = range(first, first + panel)
+            columns = [jnp.broadcast_to(work[:, k : k + 1], (vecs, LANES)) for k in own]
+            lines = [work[k : k + 1, :] for k in own]
+            for j, k in enumerate(own):
+                pivot = columns[j][k : k + 1]
+                column = jnp.where(row > k, columns[j], 0.0)
+                scaled = lines[j] / pivot
+                for i in range(j + 1, panel):
+                    columns[i] = columns[i] - column * (columns[i][k : k + 1] / pivot)
+                    lines[i] = lines[i] - columns[j][first + i : first + i + 1] * scaled
+                work = work - column * scaled
         pivots = jnp.sum(jnp.where(lane == row, work, 0.0), axis=1, keepdims=True)
         diagonal = jnp.sqrt(pivots)
         inverse = work / diagonal
@@ -282,21 +315,25 @@
         inverse = jnp.where((lane >= vecs) & (lane < 2 * vecs), inverse, 0.0)
         inverse = inverse + pltpu.roll(inverse, LANES // 2, 1)
         inverse = inverse + pltpu.roll(inverse, LANES // 4, 1)
-        repeats = wide // vecs
-        tall = jnp.concatenate([inverse] * repeats, axis=0)
-        tall = jnp.concatenate([tall] * (wide // LANES), axis=1)
-        rows = lax.broadcasted_iota(jnp.int32, (wide, wide), 0) // vecs
-        cols = lax.broadcasted_iota(jnp.int32, (wide, wide), 1) // vecs
-        w_high, w_low = split(jnp.where(rows == cols, tall, 0.0))
-        w_ref[0] = w_high
-        w_ref[1] = w_low
-
-    w = (w_ref[0], w_ref[1])
+        high, low = split(
+            jnp.concatenate(
+                [jnp.where(lane // vecs == k, inverse, 0.0) for k in range(group)], axis=0
+            )
+        )
+        w_ref[...] = jnp.concatenate(
+            [
+                jnp.concatenate([high, high], axis=1),
+                jnp.concatenate([low, jnp.zeros_like(low)], axis=1),
+            ],
+            axis=0,
+        )
+
     block = vectors_ref.shape[0]
     rows = pl.ds(pl.multiple_of(pl.program_id(0) * block, block), block)
-    for k in range(vectors_ref.shape[1] // wide):
-        at = slice(k * wide, (k + 1) * wide)
-        vectors_ref[:, at] = dot3(split(stepped_ref[rows, at]), w, NT)
+    for k in range(vectors_ref.shape[1] // LANES):
+        at = slice(k * LANES, (k + 1) * LANES)
+        both = dot(jnp.concatenate(split(stepped_ref[rows, at]), axis=1), w_ref[...], NT)
+        vectors_ref[:, at] = both[:, :LANES] + both[:, LANES:]
 
 
 def vmem():
@@ -326,37 +363,32 @@
     order = np.arange(x_count)
     order = (order % row_devices) * modes + order // row_devices
     halves = -(-x_count // LANES)
-    fill = ((0, 0), (0, halves * LANES - x_count))
-    sx_high, sx_low = halves_of_table(np.pad(synthesis(x_count)[:, order].T, fill))
+    points = np.arange(halves * LANES)
+    points = np.where(points < x_count, points, points - (halves * LANES - x_count))
+    sx_high, sx_low = halves_of_table(synthesis(x_count)[points][:, order].T)
     sx = np.concatenate([sx_high, sx_high, sx_low], axis=0)
-    sz, az, gx = (
+    sz, az = (
         np.concatenate([high, low, high], axis=1)
-        for high, low in map(
-            halves_of_table,
-            (
-                synthesis(z_count),
-                analysis(z_count),
-                np.pad(derivative_analysis(x_count, ALPHA_X)[order], fill),
-            ),
-        )
+        for high, low in map(halves_of_table, (synthesis(z_count), analysis(z_count)))
     )
-
-    steps = 4
+    gx = np.concatenate(
+        halves_of_table(derivative_analysis(x_count, ALPHA_X)[order][:, points]), axis=0
+    )
+
+    steps = 2
     base = jnp.transpose(base_flow, (0, 2, 1)).reshape(modes * z_length, planes)
     packed = pl.pallas_call(
-        functools.partial(
-            pack_kernel, modes=modes, planes=planes, tiles=tiles, extra=extra,
-            step_modes=modes // steps,
-        ),
+        functools.partial(pack_kernel, modes=modes, planes=planes, tiles=tiles, extra=extra),
         out_shape=jax.ShapeDtypeStruct((planes * (rows + extra), LANES), F32),
-        grid=(steps,),
-        in_specs=[
-            pl.BlockSpec((modes // steps, planes, width), lambda i: (i, 0, 0)),
-            pl.BlockSpec(base.shape, lambda i: (0, 0)),
+        in_specs=[pl.BlockSpec(memory_space=pltpu.HBM)] * 2,
+        out_specs=vmem(),
+        scratch_shapes=[
+            pltpu.VMEM(tangents.shape, F32),
+            pltpu.VMEM(base.shape, F32),
+            pltpu.SemaphoreType.DMA((modes + 1,)),
         ],
-        out_specs=vmem(),
         cost_estimate=cost(10**9, 2 * size),
-        compiler_params=small,
+        compiler_params=pltpu.CompilerParams(vmem_limit_bytes=44 * 2**20),
         name="pack",
     )(tangents, base)
     received = lax.all_to_all(
@@ -386,18 +418,14 @@
     stepped, grams = pl.pallas_call(
         functools.partial(
             column_kernel, modes=modes, planes=planes, tiles=tiles, vecs=vecs,
-            step_modes=modes // 2, x_count=x_count, z_count=z_count, z_length=z_length,
+            step_modes=modes // steps, x_count=x_count, z_count=z_count, z_length=z_length,
         ),
         out_shape=[
             jax.ShapeDtypeStruct((height, width), F32),
             jax.ShapeDtypeStruct((devices, piece, LANES), F32),
         ],
-        grid=(2,),
-        in_specs=[
-            vmem(),
-            pl.BlockSpec((modes // 2, planes, width), lambda i: (i, 0, 0)),
-        ]
-        + [vmem()] * 4,
+        grid=(steps,),
+        in_specs=[vmem()] * 6,
         out_specs=[vmem()] * 2,
         scratch_shapes=[
             pltpu.VMEM((modes, width), F32),
@@ -406,14 +434,14 @@
             pltpu.VMEM((LANES, 2 * LANES), F32),
         ],
         cost_estimate=cost(10**10, 3 * size),
-        compiler_params=big,
+        compiler_params=small,
         name="column",
     )(nonlinear, tangents, mode_mask, decay_rates[None, :], to_eigen, from_eigen)
     grams = lax.all_to_all(grams, both, 0, 0, tiled=True).reshape(devices * piece, LANES)
 
     block = height // 3
     vectors, growth = pl.pallas_call(
-        functools.partial(finish_kernel, devices=devices, vecs=vecs, wide=2 * LANES),
+        functools.partial(finish_kernel, devices=devices, vecs=vecs, panel=8),
         out_shape=[
             jax.ShapeDtypeStruct((height, width), F32),
             jax.ShapeDtypeStruct((1, vecs), F32),
@@ -424,7 +452,7 @@
             pl.BlockSpec((block, width), lambda i: (i, 0)),
             pl.BlockSpec((1, vecs), lambda i: (0, 0)),
         ],
-        scratch_shapes=[pltpu.VMEM((2, 2 * LANES, 2 * LANES), BF16)],
+        scratch_shapes=[pltpu.VMEM((2 * LANES, 2 * LANES), BF16)],
         cost_estimate=cost(2 * height * width * 256, 2 * size),
         compiler_params=small,
         name="finish",

time: 188 us -> 181 us (0.963)
  Pallas kernels: 30.5 us -> 24.1 us
    pallas_call x1, Pallas kernels: 15.5 us -> 10.5 us  [body(): pl.pallas_call(functools.partial(transform_kernel, modes=modes, row_devic...]
    pallas_call x1, Pallas kernels: 0.49 us -> 2.96 us  [body(): pl.pallas_call(functools.partial(pack_kernel, modes=modes, planes=planes,...]
    pallas_call x1, Pallas kernels: 6.84 us -> 4.64 us  [body(): pl.pallas_call(functools.partial(finish_kernel, devices=devices, vecs=vec...]
where the time goes in v4:
time: 181 us
  blocking collectives  153 us (85%)
  Pallas kernels  24.1 us (13%)
  local copies, waits for them, and re-layouts  3.31 us (2%)
    all_to_all x1, blocking collectives, body(): lax.all_to_all(packed.reshape(devices, rows + extra, 1, LANES), both, 0,...  72.1 us
    all_to_all x1, blocking collectives, body(): lax.all_to_all(returned.reshape(devices, rows, LANES), both, 0, 0, tiled=...  62.8 us
    all_to_all x1, blocking collectives, body(): lax.all_to_all(grams, both, 0, 0, tiled=True)  17.9 us
    pallas_call x1, Pallas kernels, body(): pl.pallas_call(functools.partial(transform_kernel, modes=modes, row_devic...  10.5 us
    pallas_call x1, Pallas kernels, body(): pl.pallas_call(functools.partial(column_kernel, modes=modes, planes=plane...  5.97 us
    pallas_call x1, Pallas kernels, body(): pl.pallas_call(functools.partial(finish_kernel, devices=devices, vecs=vec...  4.64 us

profile of v4, /device:TPU:1, one launch (start us, length us, event | category | flops | bytes accessed | tf_op | source)
XLA Modules:
  0.0 181.0 jit_solution(8728685924044834996)
XLA Ops:
  0.6 0.0 copy-start
  0.6 2.3 %copy-done = f32[12,128,768]{2,1,0:T(8,128)S(1)} copy-done((f32[12,128,768]{2,1,0:T(8,128)S(1)}, f32[12,128,768]{2,1,0:T(8,128)}, u32[]{:S(2)}) %copy-start) | copy-done | bytes 4718616
  3.0 0.0 copy-start.1
  3.0 0.9 copy-done.1
  3.9 3.0 %pack.1 = f32[9600,128]{1,0:T(8,128)S(1)} custom-call(f32[12,128,768]{2,1,0:T(8,128)S(1)} %copy-done, f32[288,128]{1,0:T(8,128)S(1)} %bitcast.18), custom_call_target="tpu_custom_call" | custom-call | flops 1000000000 | bytes 9437184 | tf_op jit(solution)/shard_map/pack/pallas_call | solution.py:380
  6.9 0.0 copy-start.6
  6.9 0.0 copy-start.7
  6.9 0.0 copy-start.8
  6.9 0.0 copy-start.9
  6.9 0.0 slice-start
  6.9 72.1 %all_to_all.15 = f32[128,75,1,128]{3,2,1,0:T(1,128)S(1)} all-to-all(f32[128,75,1,128]{3,2,1,0:T(1,128)S(1)} %bitcast.11), channel_id=1, replica_groups=mesh['row'=16,'col'=8] {'col','row'}, dimensions={0} | all-to-all | bytes 9830400 | tf_op jit(solution)/shard_map/all_to_all | solution.py:394
  79.0 0.0 copy-done.6
  79.0 0.0 copy-done.7
  79.0 0.0 copy-done.8
  79.0 0.0 copy-done.9
  79.1 0.0 slice-start.1
  79.1 10.5 %transform.1 = f32[9216,128]{1,0:T(8,128)S(1)} custom-call(f32[9600,128]{1,0:T(8,128)S(1)} %bitcast.12, bf16[576,256]{1,0:T(8,128)(2,1)S(1)} %copy-done.6, bf16[192,576]{1,0:T(8,128)(2,1)S(1)} %copy-done.8, bf16[192,576]{1,0:T(8,128)(2,1)S(1)} %copy-done.7, bf16[384,256]{1,0:T(8,128)(2,1)S(1)} %copy-done.9), custom_call_target="tpu_custom_call" | custom-call | flops 20000000000 | bytes 9437184 | tf_op jit(solution)/shard_map/transform/pallas_call | solution.py:398
  89.6 0.0 copy-start.2
  89.6 0.0 copy-start.3
  89.6 0.0 copy-start.4
  89.6 0.0 copy-start.5
  89.6 62.8 %all_to_all.16 = f32[128,72,128]{2,1,0:T(8,128)S(1)} all-to-all(f32[128,72,128]{2,1,0:T(8,128)S(1)} %bitcast.15), channel_id=1, replica_groups=mesh['row'=16,'col'=8] {'col','row'}, dimensions={0} | all-to-all | bytes 9437184 | tf_op jit(solution)/shard_map/all_to_all | solution.py:412
  152.5 0.0 slice-done
  152.5 0.0 slice-done.1
  152.5 0.0 copy-done.2
  152.5 0.0 copy-done.3
  152.5 0.0 copy-done.4
  152.5 0.0 copy-done.5
  152.5 6.0 %column.1 = (f32[1536,768]{1,0:T(8,128)S(1)}, f32[128,8,128]{2,1,0:T(8,128)S(1)}) custom-call(f32[9216,128]{1,0:T(8,128)S(1)} %bitcast.16, f32[12,128,768]{2,1,0:T(8,128)S(1)} %bitcast.14, s32[12,24]{1,0:T(8,128)S(1)} %copy-done.4, f32[1,128]{1,0:T(1,128)S(1)} %bitcast.19, f32[128,128]{1,0:T(8,128)S(1)} %copy-done.2, f32[128,128]{1,0:T(8,128)S(1)} %copy-done.3), custom_call_target="tpu_custom_call" | custom-call | flops 10000000000 | bytes 14155776 | tf_op jit(solution)/shard_map/column/pallas_call | solution.py:418
  158.5 17.9 %all_to_all.17 = f32[128,8,128]{2,1,0:T(8,128)S(1)} all-to-all(f32[128,8,128]{2,1,0:T(8,128)S(1)} %get-tuple-element.6), channel_id=1, replica_groups=mesh['row'=16,'col'=8] {'col','row'}, dimensions={0} | all-to-all | bytes 1048576 | tf_op jit(solution)/shard_map/all_to_all | solution.py:440
  176.4 4.6 %finish.1 = (f32[1536,768]{1,0:T(8,128)}, f32[1,32]{1,0:T(1,128)}) custom-call(f32[1024,128]{1,0:T(8,128)S(1)} %bitcast.17, f32[1536,768]{1,0:T(8,128)S(1)} %get-tuple-element.7.stepped_ref), custom_call_target="tpu_custom_call" | custom-call | flops 603979776 | bytes 9437184 | tf_op jit(solution)/shard_map/finish/pallas_call | solution.py:443
  (1 shorter events, 0.0 us)
Async XLA Ops:
  0.6 2.3 %copy-start = (f32[12,128,768]{2,1,0:T(8,128)S(1)}, f32[12,128,768]{2,1,0:T(8,128)}, u32[]{:S(2)}) copy-start(f32[12,128,768]{2,1,0:T(8,128)} %q_ref.3) | copy-start | bytes 14155780
  3.0 0.9 copy-start.1
  6.9 72.2 %copy-start.6 = (bf16[576,256]{1,0:T(8,128)(2,1)S(1)}, bf16[576,256]{1,0:T(8,128)(2,1)}, u32[]{:S(2)}) copy-start(bf16[576,256]{1,0:T(8,128)(2,1)} %constant.8.clone.sx_ref) | copy-start | bytes 884740
  6.9 72.2 %copy-start.7 = (bf16[192,576]{1,0:T(8,128)(2,1)S(1)}, bf16[192,576]{1,0:T(8,128)(2,1)}, u32[]{:S(2)}) copy-start(bf16[192,576]{1,0:T(8,128)(2,1)} %constant.10.clone.az_ref) | copy-start | bytes 663556
  6.9 72.2 %copy-start.8 = (bf16[192,576]{1,0:T(8,128)(2,1)S(1)}, bf16[192,576]{1,0:T(8,128)(2,1)}, u32[]{:S(2)}) copy-start(bf16[192,576]{1,0:T(8,128)(2,1)} %constant.9.clone.sz_ref) | copy-start | bytes 663556
  6.9 72.2 %copy-start.9 = (bf16[384,256]{1,0:T(8,128)(2,1)S(1)}, bf16[384,256]{1,0:T(8,128)(2,1)}, u32[]{:S(2)}) copy-start(bf16[384,256]{1,0:T(8,128)(2,1)} %constant.11.clone.g_ref) | copy-start | bytes 589828
  6.9 145.6 %slice-start = ((s8[4718592]{0:T(1024)(128)(4,1)}), s8[524288]{0:T(1024)(128)(4,1)S(1)}, s32[]{:S(2)}) async-start(s8[4718592]{0:T(1024)(128)(4,1)} %bitcast.13), calls=%async_computation.3 | async-start | bytes 1048576
  79.1 73.4 %slice-start.1 = ((s8[4718592]{0:T(1024)(128)(4,1)}), s8[4194304]{0:T(1024)(128)(4,1)S(1)}, s32[]{:S(2)}) async-start(s8[4718592]{0:T(1024)(128)(4,1)} %bitcast.13), calls=%async_computation.4 | async-start | bytes 8388608
  89.6 62.9 %copy-start.2 = (f32[128,128]{1,0:T(8,128)S(1)}, f32[128,128]{1,0:T(8,128)}, u32[]{:S(2)}) copy-start(f32[128,128]{1,0:T(8,128)} %to_ref.1) | copy-start | bytes 196612
  89.6 62.9 %copy-start.3 = (f32[128,128]{1,0:T(8,128)S(1)}, f32[128,128]{1,0:T(8,128)}, u32[]{:S(2)}) copy-start(f32[128,128]{1,0:T(8,128)} %from_ref.1) | copy-start | bytes 196612
  89.6 62.9 %copy-start.4 = (s32[12,24]{1,0:T(8,128)S(1)}, s32[12,24]{1,0:T(8,128)}, u32[]{:S(2)}) copy-start(s32[12,24]{1,0:T(8,128)} %mask_ref.1) | copy-start | bytes 3460
  89.6 62.9 %copy-start.5 = (f32[128]{0:T(128)S(1)}, f32[128]{0:T(128)}, u32[]{:S(2)}) copy-start(f32[128]{0:T(128)} %param.13) | copy-start | bytes 1540

commit v5 on v4

--- a/solution.py
+++ b/solution.py
@@ -76,23 +76,16 @@
     return dot(table_ref[...], jnp.concatenate([high, high, low], axis=0), NN)
 
 
-def pack_kernel(q_ref, base_ref, out_ref, q_s, base_s, sems, *, modes, planes, tiles, extra):
+def pack_kernel(q_ref, base_ref, out_ref, *, modes, planes, tiles, extra):
     stride = modes * tiles + extra
-    copies = [pltpu.make_async_copy(q_ref.at[m], q_s.at[m], sems.at[m]) for m in range(modes)]
-    base_copy = pltpu.make_async_copy(base_ref, base_s, sems.at[modes])
-    base_copy.start()
-    for copy in copies:
-        copy.start()
-    base_copy.wait()
-    part = base_s.shape[0] // extra
+    part = base_ref.shape[0] // extra
     fill = jnp.zeros((LANES - part, planes), F32)
     for k in range(extra):
-        block = jnp.concatenate([base_s[k * part : (k + 1) * part, :], fill], axis=0)
+        block = jnp.concatenate([base_ref[k * part : (k + 1) * part, :], fill], axis=0)
         out_ref[pl.ds(modes * tiles + k, planes, stride=stride), :] = block.T
-    for m, copy in enumerate(copies):
-        copy.wait()
+    for m in range(modes):
         for nb in range(tiles):
-            out_ref[pl.ds(nb * modes + m, planes, stride=stride), :] = q_s[
+            out_ref[pl.ds(nb * modes + m, planes, stride=stride), :] = q_ref[
                 m, :, nb * LANES : (nb + 1) * LANES
             ]
 
@@ -375,20 +368,15 @@
         halves_of_table(derivative_analysis(x_count, ALPHA_X)[order][:, points]), axis=0
     )
 
-    steps = 2
+    steps = 1
     base = jnp.transpose(base_flow, (0, 2, 1)).reshape(modes * z_length, planes)
     packed = pl.pallas_call(
         functools.partial(pack_kernel, modes=modes, planes=planes, tiles=tiles, extra=extra),
         out_shape=jax.ShapeDtypeStruct((planes * (rows + extra), LANES), F32),
-        in_specs=[pl.BlockSpec(memory_space=pltpu.HBM)] * 2,
+        in_specs=[vmem()] * 2,
         out_specs=vmem(),
-        scratch_shapes=[
-            pltpu.VMEM(tangents.shape, F32),
-            pltpu.VMEM(base.shape, F32),
-            pltpu.SemaphoreType.DMA((modes + 1,)),
-        ],
         cost_estimate=cost(10**9, 2 * size),
-        compiler_params=pltpu.CompilerParams(vmem_limit_bytes=44 * 2**20),
+        compiler_params=small,
         name="pack",
     )(tangents, base)
     received = lax.all_to_all(
@@ -439,7 +427,7 @@
     )(nonlinear, tangents, mode_mask, decay_rates[None, :], to_eigen, from_eigen)
     grams = lax.all_to_all(grams, both, 0, 0, tiled=True).reshape(devices * piece, LANES)
 
-    block = height // 3
+    block = height // 2
     vectors, growth = pl.pallas_call(
         functools.partial(finish_kernel, devices=devices, vecs=vecs, panel=8),
         out_shape=[

time: 181 us -> 178 us (0.983)
  Pallas kernels: 24.1 us -> 20.7 us
    pallas_call x1, Pallas kernels: 2.96 us -> 0.32 us  [body(): pl.pallas_call(functools.partial(pack_kernel, modes=modes, planes=planes,...]
where the time goes in v5:
time: 178 us
  blocking collectives  153 us (86%)
  Pallas kernels  20.7 us (12%)
  local copies, waits for them, and re-layouts  3.31 us (2%)
    all_to_all x1, blocking collectives, body(): lax.all_to_all(packed.reshape(devices, rows + extra, 1, LANES), both, 0,...  72.1 us
    all_to_all x1, blocking collectives, body(): lax.all_to_all(returned.reshape(devices, rows, LANES), both, 0, 0, tiled=...  62.8 us
    all_to_all x1, blocking collectives, body(): lax.all_to_all(grams, both, 0, 0, tiled=True)  17.9 us
    pallas_call x1, Pallas kernels, body(): pl.pallas_call(functools.partial(transform_kernel, modes=modes, row_devic...  10.5 us
    pallas_call x1, Pallas kernels, body(): pl.pallas_call(functools.partial(column_kernel, modes=modes, planes=plane...  5.77 us
    pallas_call x1, Pallas kernels, body(): pl.pallas_call(functools.partial(finish_kernel, devices=devices, vecs=vec...  4.13 us

profile of v5, /device:TPU:1, one launch (start us, length us, event | category | flops | bytes accessed | tf_op | source)
XLA Modules:
  0.0 177.7 jit_solution(8397202009289702285)
XLA Ops:
  0.6 0.0 copy-start
  0.6 2.3 %copy-done = f32[12,128,768]{2,1,0:T(8,128)S(1)} copy-done((f32[12,128,768]{2,1,0:T(8,128)S(1)}, f32[12,128,768]{2,1,0:T(8,128)}, u32[]{:S(2)}) %copy-start) | copy-done | bytes 4718616
  3.0 0.0 copy-start.1
  3.0 0.9 copy-done.1
  3.9 0.3 pack.1
  4.2 0.0 copy-start.6
  4.2 0.0 copy-start.7
  4.2 0.0 copy-start.8
  4.2 0.0 copy-start.9
  4.3 0.0 slice-start
  4.3 72.1 %all_to_all.15 = f32[128,75,1,128]{3,2,1,0:T(1,128)S(1)} all-to-all(f32[128,75,1,128]{3,2,1,0:T(1,128)S(1)} %bitcast.11), channel_id=1, replica_groups=mesh['row'=16,'col'=8] {'col','row'}, dimensions={0} | all-to-all | bytes 9830400 | tf_op jit(solution)/shard_map/all_to_all | solution.py:382
  76.4 0.0 copy-done.6
  76.4 0.0 copy-done.7
  76.4 0.0 copy-done.8
  76.4 0.0 copy-done.9
  76.4 0.0 slice-start.1
  76.4 10.5 %transform.1 = f32[9216,128]{1,0:T(8,128)S(1)} custom-call(f32[9600,128]{1,0:T(8,128)S(1)} %bitcast.12, bf16[576,256]{1,0:T(8,128)(2,1)S(1)} %copy-done.6, bf16[192,576]{1,0:T(8,128)(2,1)S(1)} %copy-done.8, bf16[192,576]{1,0:T(8,128)(2,1)S(1)} %copy-done.7, bf16[384,256]{1,0:T(8,128)(2,1)S(1)} %copy-done.9), custom_call_target="tpu_custom_call" | custom-call | flops 20000000000 | bytes 9437184 | tf_op jit(solution)/shard_map/transform/pallas_call | solution.py:386
  86.9 0.0 copy-start.2
  86.9 0.0 copy-start.3
  87.0 0.0 copy-start.4
  87.0 0.0 copy-start.5
  87.0 62.8 %all_to_all.16 = f32[128,72,128]{2,1,0:T(8,128)S(1)} all-to-all(f32[128,72,128]{2,1,0:T(8,128)S(1)} %bitcast.15), channel_id=1, replica_groups=mesh['row'=16,'col'=8] {'col','row'}, dimensions={0} | all-to-all | bytes 9437184 | tf_op jit(solution)/shard_map/all_to_all | solution.py:400
  149.8 0.0 slice-done
  149.8 0.0 slice-done.1
  149.8 0.0 copy-done.2
  149.8 0.0 copy-done.3
  149.8 0.0 copy-done.4
  149.8 0.0 copy-done.5
  149.9 5.8 %column.1 = (f32[1536,768]{1,0:T(8,128)S(1)}, f32[128,8,128]{2,1,0:T(8,128)S(1)}) custom-call(f32[9216,128]{1,0:T(8,128)S(1)} %bitcast.16, f32[12,128,768]{2,1,0:T(8,128)S(1)} %bitcast.14, s32[12,24]{1,0:T(8,128)S(1)} %copy-done.4, f32[1,128]{1,0:T(1,128)S(1)} %bitcast.19, f32[128,128]{1,0:T(8,128)S(1)} %copy-done.2, f32[128,128]{1,0:T(8,128)S(1)} %copy-done.3), custom_call_target="tpu_custom_call" | custom-call | flops 10000000000 | bytes 14155776 | tf_op jit(solution)/shard_map/column/pallas_call | solution.py:406
  155.6 17.9 %all_to_all.17 = f32[128,8,128]{2,1,0:T(8,128)S(1)} all-to-all(f32[128,8,128]{2,1,0:T(8,128)S(1)} %get-tuple-element.6), channel_id=1, replica_groups=mesh['row'=16,'col'=8] {'col','row'}, dimensions={0} | all-to-all | bytes 1048576 | tf_op jit(solution)/shard_map/all_to_all | solution.py:428
  173.6 4.1 %finish.1 = (f32[1536,768]{1,0:T(8,128)}, f32[1,32]{1,0:T(1,128)}) custom-call(f32[1024,128]{1,0:T(8,128)S(1)} %bitcast.17, f32[1536,768]{1,0:T(8,128)S(1)} %get-tuple-element.7.stepped_ref), custom_call_target="tpu_custom_call" | custom-call | flops 603979776 | bytes 9437184 | tf_op jit(solution)/shard_map/finish/pallas_call | solution.py:431
  (1 shorter events, 0.0 us)
Async XLA Ops:
  0.6 2.3 %copy-start = (f32[12,128,768]{2,1,0:T(8,128)S(1)}, f32[12,128,768]{2,1,0:T(8,128)}, u32[]{:S(2)}) copy-start(f32[12,128,768]{2,1,0:T(8,128)} %q_ref.3) | copy-start | bytes 14155780
  3.0 0.9 copy-start.1
  4.2 72.2 %copy-start.6 = (bf16[576,256]{1,0:T(8,128)(2,1)S(1)}, bf16[576,256]{1,0:T(8,128)(2,1)}, u32[]{:S(2)}) copy-start(bf16[576,256]{1,0:T(8,128)(2,1)} %constant.8.clone.sx_ref) | copy-start | bytes 884740
  4.2 72.2 %copy-start.7 = (bf16[192,576]{1,0:T(8,128)(2,1)S(1)}, bf16[192,576]{1,0:T(8,128)(2,1)}, u32[]{:S(2)}) copy-start(bf16[192,576]{1,0:T(8,128)(2,1)} %constant.10.clone.az_ref) | copy-start | bytes 663556
  4.2 72.2 %copy-start.8 = (bf16[192,576]{1,0:T(8,128)(2,1)S(1)}, bf16[192,576]{1,0:T(8,128)(2,1)}, u32[]{:S(2)}) copy-start(bf16[192,576]{1,0:T(8,128)(2,1)} %constant.9.clone.sz_ref) | copy-start | bytes 663556
  4.2 72.2 %copy-start.9 = (bf16[384,256]{1,0:T(8,128)(2,1)S(1)}, bf16[384,256]{1,0:T(8,128)(2,1)}, u32[]{:S(2)}) copy-start(bf16[384,256]{1,0:T(8,128)(2,1)} %constant.11.clone.g_ref) | copy-start | bytes 589828
  4.3 145.6 %slice-start = ((s8[4718592]{0:T(1024)(128)(4,1)}), s8[4194304]{0:T(1024)(128)(4,1)S(1)}, s32[]{:S(2)}) async-start(s8[4718592]{0:T(1024)(128)(4,1)} %bitcast.13), calls=%async_computation.3 | async-start | bytes 8388608
  76.4 73.4 %slice-start.1 = ((s8[4718592]{0:T(1024)(128)(4,1)}), s8[524288]{0:T(1024)(128)(4,1)S(1)}, s32[]{:S(2)}) async-start(s8[4718592]{0:T(1024)(128)(4,1)} %bitcast.13), calls=%async_computation.4 | async-start | bytes 1048576
  86.9 62.9 %copy-start.2 = (f32[128,128]{1,0:T(8,128)S(1)}, f32[128,128]{1,0:T(8,128)}, u32[]{:S(2)}) copy-start(f32[128,128]{1,0:T(8,128)} %to_ref.1) | copy-start | bytes 196612
  86.9 62.9 %copy-start.3 = (f32[128,128]{1,0:T(8,128)S(1)}, f32[128,128]{1,0:T(8,128)}, u32[]{:S(2)}) copy-start(f32[128,128]{1,0:T(8,128)} %from_ref.1) | copy-start | bytes 196612
  87.0 62.9 %copy-start.4 = (s32[12,24]{1,0:T(8,128)S(1)}, s32[12,24]{1,0:T(8,128)}, u32[]{:S(2)}) copy-start(s32[12,24]{1,0:T(8,128)} %mask_ref.1) | copy-start | bytes 3460
  87.0 62.9 %copy-start.5 = (f32[128]{0:T(128)S(1)}, f32[128]{0:T(128)}, u32[]{:S(2)}) copy-start(f32[128]{0:T(128)} %param.13) | copy-start | bytes 1540

commit v6 on v5

--- a/solution.py
+++ b/solution.py
@@ -267,24 +267,48 @@
             folded = folded + jnp.where(lane == k, full[k * vecs : (k + 1) * vecs], 0.0)
         folded = folded + pltpu.roll(folded, LANES // 2, 1)
         folded = folded + pltpu.roll(folded, LANES // 4, 1)
-        piece = vecs // group
-        lane = lax.broadcasted_iota(jnp.int32, (piece, LANES), 1) // vecs
+        half = vecs // 2
+        lane = lax.broadcasted_iota(jnp.int32, (half, LANES), 1)
+        row = lax.broadcasted_iota(jnp.int32, (half, LANES), 0)
+        top, shifted = folded[:half], pltpu.roll(folded[half:], LANES - half, 1)
+        square = jnp.where((lane % vecs < half) & (lane % vecs < row), shifted, top)
+        piece = half // group
+        spread = lane[:piece] // vecs
         packed = jnp.zeros((piece, LANES), F32)
         for k in range(group):
-            packed = jnp.where(lane == k, folded[k * piece : (k + 1) * piece], packed)
-        gram_ref[...] = jnp.broadcast_to(packed[None], gram_ref.shape)
+            packed = jnp.where(spread == k, square[k * piece : (k + 1) * piece], packed)
+        diagonal = jnp.sum(jnp.where(lane % vecs == row, shifted, 0.0), axis=0, keepdims=True)
+        sent = [packed[k : k + 1] for k in range(piece)] + [diagonal]
+        for k, line in enumerate(sent):
+            gram_ref[pl.ds(k, planes, stride=len(sent)), :] = jnp.broadcast_to(
+                line, (planes, LANES)
+            )
 
 
 def finish_kernel(grams_ref, stepped_ref, vectors_ref, growth_ref, w_ref, *, devices, vecs, panel):
     group = LANES // vecs
-    piece = vecs // group
+    half = vecs // 2
+    piece = half // group
 
     @pl.when(pl.program_id(0) == 0)
     def _():
-        packed = jnp.sum(grams_ref[...].reshape(devices, piece, LANES), axis=0)
-        gram = jnp.concatenate(
+        lines = [
+            jnp.sum(
+                grams_ref[pl.ds(k, devices, stride=piece + 1), :], axis=0, keepdims=True
+            )
+            for k in range(piece + 1)
+        ]
+        packed = jnp.concatenate(lines[:piece], axis=0)
+        square = jnp.concatenate(
             [pltpu.roll(packed, (LANES - k * vecs) % LANES, 1) for k in range(group)], axis=0
         )
+        turned = jnp.concatenate([square, jnp.zeros((LANES - half, LANES), F32)], axis=0).T
+        lane = lax.broadcasted_iota(jnp.int32, (half, LANES), 1)
+        row = lax.broadcasted_iota(jnp.int32, (half, LANES), 0)
+        top = jnp.where((lane < half) & (lane < row), turned[:half], square)
+        right = jnp.where(lane < row, square, jnp.where(lane == row, lines[piece], turned[:half]))
+        bottom = jnp.where(lane < half, turned[half:vecs], pltpu.roll(right, half, 1))
+        gram = jnp.concatenate([top, bottom], axis=0)
         lane = lax.broadcasted_iota(jnp.int32, (vecs, LANES), 1)
         row = lax.broadcasted_iota(jnp.int32, (vecs, LANES), 0)
         work = jnp.where(lane < vecs, gram, jnp.where(lane == row + vecs, 1.0, 0.0))
@@ -401,7 +425,7 @@
         returned.reshape(devices, rows, LANES), both, 0, 0, tiled=True
     ).reshape(returned.shape)
 
-    piece = vecs * vecs // LANES
+    lines = vecs * vecs // (2 * LANES) + 1
     height = modes * planes
     stepped, grams = pl.pallas_call(
         functools.partial(
@@ -410,7 +434,7 @@
         ),
         out_shape=[
             jax.ShapeDtypeStruct((height, width), F32),
-            jax.ShapeDtypeStruct((devices, piece, LANES), F32),
+            jax.ShapeDtypeStruct((devices * lines, LANES), F32),
         ],
         grid=(steps,),
         in_specs=[vmem()] * 6,
@@ -425,7 +449,9 @@
         compiler_params=small,
         name="column",
     )(nonlinear, tangents, mode_mask, decay_rates[None, :], to_eigen, from_eigen)
-    grams = lax.all_to_all(grams, both, 0, 0, tiled=True).reshape(devices * piece, LANES)
+    grams = lax.all_to_all(
+        grams.reshape(devices, lines, 1, LANES), both, 0, 0, tiled=True
+    ).reshape(grams.shape)
 
     block = height // 2
     vectors, growth = pl.pallas_call(

time: 178 us -> 176 us (0.989)
  blocking collectives: 153 us -> 151 us
    all_to_all x1, blocking collectives: 17.9 us -> 15.9 us  [body(): lax.all_to_all(grams.reshape(devices, lines, 1, LANES), both, 0, 0, tiled...]
where the time goes in v6:
time: 176 us
  blocking collectives  151 us (86%)
  Pallas kernels  20.8 us (12%)
  local copies, waits for them, and re-layouts  3.31 us (2%)
    all_to_all x1, blocking collectives, body(): lax.all_to_all(packed.reshape(devices, rows + extra, 1, LANES), both, 0,...  72.1 us
    all_to_all x1, blocking collectives, body(): lax.all_to_all(returned.reshape(devices, rows, LANES), both, 0, 0, tiled=...  62.8 us
    all_to_all x1, blocking collectives, body(): lax.all_to_all(grams.reshape(devices, lines, 1, LANES), both, 0, 0, tiled...  15.9 us
    pallas_call x1, Pallas kernels, body(): pl.pallas_call(functools.partial(transform_kernel, modes=modes, row_devic...  10.5 us
    pallas_call x1, Pallas kernels, body(): pl.pallas_call(functools.partial(column_kernel, modes=modes, planes=plane...  5.82 us
    pallas_call x1, Pallas kernels, body(): pl.pallas_call(functools.partial(finish_kernel, devices=devices, vecs=vec...  4.15 us

profile of v6, /device:TPU:1, one launch (start us, length us, event | category | flops | bytes accessed | tf_op | source)
XLA Modules:
  0.0 175.8 jit_solution(3116068372417941123)
XLA Ops:
  0.6 0.0 copy-start
  0.6 2.3 %copy-done = f32[12,128,768]{2,1,0:T(8,128)S(1)} copy-done((f32[12,128,768]{2,1,0:T(8,128)S(1)}, f32[12,128,768]{2,1,0:T(8,128)}, u32[]{:S(2)}) %copy-start) | copy-done | bytes 4718616
  3.0 0.0 copy-start.1
  3.0 0.9 copy-done.1
  3.9 0.3 pack.1
  4.2 0.0 copy-start.6
  4.2 0.0 copy-start.7
  4.2 0.0 copy-start.8
  4.2 0.0 copy-start.9
  4.3 0.0 slice-start
  4.3 72.1 %all_to_all.15 = f32[128,75,1,128]{3,2,1,0:T(1,128)S(1)} all-to-all(f32[128,75,1,128]{3,2,1,0:T(1,128)S(1)} %bitcast.12), channel_id=1, replica_groups=mesh['row'=16,'col'=8] {'col','row'}, dimensions={0} | all-to-all | bytes 9830400 | tf_op jit(solution)/shard_map/all_to_all | solution.py:406
  76.4 0.0 copy-done.6
  76.4 0.0 copy-done.7
  76.4 0.0 copy-done.8
  76.4 0.0 copy-done.9
  76.4 0.0 slice-start.1
  76.4 10.5 %transform.1 = f32[9216,128]{1,0:T(8,128)S(1)} custom-call(f32[9600,128]{1,0:T(8,128)S(1)} %bitcast.13, bf16[576,256]{1,0:T(8,128)(2,1)S(1)} %copy-done.6, bf16[192,576]{1,0:T(8,128)(2,1)S(1)} %copy-done.8, bf16[192,576]{1,0:T(8,128)(2,1)S(1)} %copy-done.7, bf16[384,256]{1,0:T(8,128)(2,1)S(1)} %copy-done.9), custom_call_target="tpu_custom_call" | custom-call | flops 20000000000 | bytes 9437184 | tf_op jit(solution)/shard_map/transform/pallas_call | solution.py:410
  86.9 0.0 copy-start.2
  86.9 0.0 copy-start.3
  87.0 0.0 copy-start.4
  87.0 0.0 copy-start.5
  87.0 62.8 %all_to_all.16 = f32[128,72,128]{2,1,0:T(8,128)S(1)} all-to-all(f32[128,72,128]{2,1,0:T(8,128)S(1)} %bitcast.16), channel_id=1, replica_groups=mesh['row'=16,'col'=8] {'col','row'}, dimensions={0} | all-to-all | bytes 9437184 | tf_op jit(solution)/shard_map/all_to_all | solution.py:424
  149.8 0.0 slice-done
  149.8 0.0 slice-done.1
  149.8 0.0 copy-done.2
  149.8 0.0 copy-done.3
  149.8 0.0 copy-done.4
  149.8 0.0 copy-done.5
  149.9 5.8 %column.1 = (f32[1536,768]{1,0:T(8,128)S(1)}, f32[640,128]{1,0:T(8,128)S(1)}) custom-call(f32[9216,128]{1,0:T(8,128)S(1)} %bitcast.17, f32[12,128,768]{2,1,0:T(8,128)S(1)} %bitcast.15, s32[12,24]{1,0:T(8,128)S(1)} %copy-done.4, f32[1,128]{1,0:T(1,128)S(1)} %bitcast.21, f32[128,128]{1,0:T(8,128)S(1)} %copy-done.2, f32[128,128]{1,0:T(8,128)S(1)} %copy-done.3), custom_call_target="tpu_custom_call" | custom-call | flops 10000000000 | bytes 14155776 | tf_op jit(solution)/shard_map/column/pallas_call | solution.py:430
  155.7 15.9 %all_to_all.17 = f32[128,5,1,128]{3,2,1,0:T(1,128)S(1)} all-to-all(f32[128,5,1,128]{3,2,1,0:T(1,128)S(1)} %bitcast.19), channel_id=1, replica_groups=mesh['row'=16,'col'=8] {'col','row'}, dimensions={0} | all-to-all | bytes 655360 | tf_op jit(solution)/shard_map/all_to_all | solution.py:452
  171.6 4.1 %finish.1 = (f32[1536,768]{1,0:T(8,128)}, f32[1,32]{1,0:T(1,128)}) custom-call(f32[640,128]{1,0:T(8,128)S(1)} %bitcast.18, f32[1536,768]{1,0:T(8,128)S(1)} %get-tuple-element.7.stepped_ref), custom_call_target="tpu_custom_call" | custom-call | flops 603979776 | bytes 9437184 | tf_op jit(solution)/shard_map/finish/pallas_call | solution.py:457
  (1 shorter events, 0.0 us)
Async XLA Ops:
  0.6 2.3 %copy-start = (f32[12,128,768]{2,1,0:T(8,128)S(1)}, f32[12,128,768]{2,1,0:T(8,128)}, u32[]{:S(2)}) copy-start(f32[12,128,768]{2,1,0:T(8,128)} %q_ref.3) | copy-start | bytes 14155780
  3.0 0.9 copy-start.1
  4.2 72.2 %copy-start.6 = (bf16[576,256]{1,0:T(8,128)(2,1)S(1)}, bf16[576,256]{1,0:T(8,128)(2,1)}, u32[]{:S(2)}) copy-start(bf16[576,256]{1,0:T(8,128)(2,1)} %constant.8.clone.sx_ref) | copy-start | bytes 884740
  4.2 72.2 %copy-start.7 = (bf16[192,576]{1,0:T(8,128)(2,1)S(1)}, bf16[192,576]{1,0:T(8,128)(2,1)}, u32[]{:S(2)}) copy-start(bf16[192,576]{1,0:T(8,128)(2,1)} %constant.10.clone.az_ref) | copy-start | bytes 663556
  4.2 72.2 %copy-start.8 = (bf16[192,576]{1,0:T(8,128)(2,1)S(1)}, bf16[192,576]{1,0:T(8,128)(2,1)}, u32[]{:S(2)}) copy-start(bf16[192,576]{1,0:T(8,128)(2,1)} %constant.9.clone.sz_ref) | copy-start | bytes 663556
  4.2 72.2 %copy-start.9 = (bf16[384,256]{1,0:T(8,128)(2,1)S(1)}, bf16[384,256]{1,0:T(8,128)(2,1)}, u32[]{:S(2)}) copy-start(bf16[384,256]{1,0:T(8,128)(2,1)} %constant.11.clone.g_ref) | copy-start | bytes 589828
  4.3 145.6 %slice-start = ((s8[4718592]{0:T(1024)(128)(4,1)}), s8[4194304]{0:T(1024)(128)(4,1)S(1)}, s32[]{:S(2)}) async-start(s8[4718592]{0:T(1024)(128)(4,1)} %bitcast.14), calls=%async_computation.3 | async-start | bytes 8388608
  76.4 73.4 %slice-start.1 = ((s8[4718592]{0:T(1024)(128)(4,1)}), s8[524288]{0:T(1024)(128)(4,1)S(1)}, s32[]{:S(2)}) async-start(s8[4718592]{0:T(1024)(128)(4,1)} %bitcast.14), calls=%async_computation.4 | async-start | bytes 1048576
  86.9 62.9 %copy-start.2 = (f32[128,128]{1,0:T(8,128)S(1)}, f32[128,128]{1,0:T(8,128)}, u32[]{:S(2)}) copy-start(f32[128,128]{1,0:T(8,128)} %to_ref.1) | copy-start | bytes 196612
  86.9 62.9 %copy-start.3 = (f32[128,128]{1,0:T(8,128)S(1)}, f32[128,128]{1,0:T(8,128)}, u32[]{:S(2)}) copy-start(f32[128,128]{1,0:T(8,128)} %from_ref.1) | copy-start | bytes 196612
  87.0 62.9 %copy-start.4 = (s32[12,24]{1,0:T(8,128)S(1)}, s32[12,24]{1,0:T(8,128)}, u32[]{:S(2)}) copy-start(s32[12,24]{1,0:T(8,128)} %mask_ref.1) | copy-start | bytes 3460
  87.0 62.9 %copy-start.5 = (f32[128]{0:T(128)S(1)}, f32[128]{0:T(128)}, u32[]{:S(2)}) copy-start(f32[128]{0:T(128)} %param.13) | copy-start | bytes 1540

commit v7 on v6

--- a/solution.py
+++ b/solution.py
@@ -71,9 +71,38 @@
     )
 
 
-def table_dot(table_ref, x):
+def tripled(table):
+    high, low = halves_of_table(table)
+    return np.concatenate([high, low, high], axis=1)
+
+
+def table_dot(table_ref, high, low):
+    return dot(table_ref[...], jnp.concatenate([high, high, low], axis=0), NN)
+
+
+def parity_tables(count):
+    middle = count // 2
+    wide, tall = middle + 16, middle + 8
+    to_points, to_modes = synthesis(count), analysis(count)
+    weights = np.where(np.arange(middle + 1) % middle == 0, 1.0, 2.0)
+    even_points = np.zeros((wide, wide))
+    even_points[: middle + 1, : middle + 1] = to_points[: middle + 1, : middle + 1]
+    odd_points = np.zeros((middle, middle))
+    odd_points[1:, 1:] = to_points[1:middle, middle + 1 :]
+    even_modes = np.zeros((tall, wide))
+    even_modes[: middle + 1, : middle + 1] = to_modes[: middle + 1, : middle + 1] * weights
+    odd_modes = np.zeros((middle, middle))
+    odd_modes[1:, 1:] = 2.0 * to_modes[middle + 1 :, 1:middle]
+    return [tripled(t) for t in (even_points, odd_points, even_modes, odd_modes)]
+
+
+def to_parity_points(even_ref, odd_ref, x):
     high, low = split(x)
-    return dot(table_ref[...], jnp.concatenate([high, high, low], axis=0), NN)
+    wide, middle = even_ref.shape[0], odd_ref.shape[0]
+    return (
+        table_dot(even_ref, high[:wide], low[:wide]),
+        table_dot(odd_ref, high[middle:], low[middle:]),
+    )
 
 
 def pack_kernel(q_ref, base_ref, out_ref, *, modes, planes, tiles, extra):
@@ -91,7 +120,8 @@
 
 
 def transform_kernel(
-    d_ref, sx_ref, sz_ref, az_ref, g_ref, out_ref, speed_ref, *scratch,
+    d_ref, sx_ref, even_p_ref, odd_p_ref, even_m_ref, odd_m_ref, g_ref, out_ref, speed_ref,
+    *scratch,
     modes, row_devices, col_devices, tiles, extra, vecs,
 ):
     halves = len(scratch) // 2
@@ -99,7 +129,8 @@
     rows = modes * tiles
     stride = rows + extra
     x_count = modes * row_devices
-    z_count = sz_ref.shape[0]
+    wide, tall, middle = even_p_ref.shape[0], even_m_ref.shape[0], odd_p_ref.shape[0]
+    z_count = 2 * middle
     z_length = z_count // col_devices
     pitch = y_refs[0].shape[0] // vecs
     per_tile = LANES // vecs
@@ -122,7 +153,9 @@
         sheets.append(jnp.concatenate(parts, axis=1))
     base = jnp.concatenate(sheets, axis=0)[:, :x_count]
     sx = (sx_ref[:x_count], sx_ref[2 * x_count :])
-    speed_ref[...] = table_dot(sz_ref, dot3(split(base), sx, NN))
+    even, odd = to_parity_points(even_p_ref, odd_p_ref, dot3(split(base), sx, NN))
+    speed_ref[:wide] = even
+    speed_ref[wide:] = odd
 
     def forward_x(c, carry):
         parts = []
@@ -164,14 +197,28 @@
         speed = jnp.concatenate(
             [speed_ref[:, :LANES]] * batch + [speed_ref[:, LANES:]] * (batch // 2), axis=1
         )
-        mixed = table_dot(az_ref, table_dot(sz_ref, mixed) * speed)
+        even, odd = to_parity_points(even_p_ref, odd_p_ref, mixed)
+        even_speed, odd_speed = speed[:wide], speed[wide:]
+        cross = even[:middle] * odd_speed + odd * even_speed[:middle]
+        even = even * even_speed
+        even = jnp.concatenate([even[:middle] + odd * odd_speed, even[middle:]], axis=0)
+        even = table_dot(even_m_ref, *split(even))
+        odd = table_dot(odd_m_ref, *split(cross))
+        mixed = jnp.concatenate(
+            [
+                even[:middle],
+                even[middle:] + odd[: tall - middle],
+                odd[tall - middle :],
+            ],
+            axis=0,
+        )
         for j, at in enumerate(ats):
             k = batch + j // 2
             z_low[at, :] = mixed[:, j * LANES : (j + 1) * LANES]
             z_high[at, :] = mixed[:, k * LANES : (k + 1) * LANES]
         return carry
 
-    lax.fori_loop(0, vecs // batch, plane, 0, unroll=2)
+    lax.fori_loop(0, vecs // batch, plane, 0, unroll=4)
 
     rows_of = lax.broadcasted_iota(jnp.int32, (vecs, LANES), 0)
     lanes_of = lax.broadcasted_iota(jnp.int32, (vecs, LANES), 1)
@@ -384,10 +431,7 @@
     points = np.where(points < x_count, points, points - (halves * LANES - x_count))
     sx_high, sx_low = halves_of_table(synthesis(x_count)[points][:, order].T)
     sx = np.concatenate([sx_high, sx_high, sx_low], axis=0)
-    sz, az = (
-        np.concatenate([high, low, high], axis=1)
-        for high, low in map(halves_of_table, (synthesis(z_count), analysis(z_count)))
-    )
+    line_tables = parity_tables(z_count)
     gx = np.concatenate(
         halves_of_table(derivative_analysis(x_count, ALPHA_X)[order][:, points]), axis=0
     )
@@ -413,14 +457,14 @@
             col_devices=col_devices, tiles=tiles, extra=extra, vecs=vecs,
         ),
         out_shape=jax.ShapeDtypeStruct((devices * rows, LANES), F32),
-        in_specs=[vmem()] * 5,
+        in_specs=[vmem()] * 7,
         out_specs=vmem(),
-        scratch_shapes=[pltpu.VMEM((z_count, halves * LANES), F32)]
+        scratch_shapes=[pltpu.VMEM((z_count + 16, halves * LANES), F32)]
         + [pltpu.VMEM((pitch * vecs, LANES), F32)] * (2 * halves),
         cost_estimate=cost(2 * 10**10, 2 * size),
         compiler_params=big,
         name="transform",
-    )(received, sx, sz, az, gx)
+    )(received, sx, *line_tables, gx)
     nonlinear = lax.all_to_all(
         returned.reshape(devices, rows, LANES), both, 0, 0, tiled=True
     ).reshape(returned.shape)

time: 176 us -> 176 us (level)
  no operation moved by 1% of the time
where the time goes in v7:
time: 176 us; the launch traced here: 175 us
  blocking collectives  151 us (86%)
  Pallas kernels  20.3 us (12%)
  local copies, waits for them, and re-layouts  3.32 us (2%)
    all_to_all x1, blocking collectives, body(): lax.all_to_all(packed.reshape(devices, rows + extra, 1, LANES), both, 0,...  72.1 us
    all_to_all x1, blocking collectives, body(): lax.all_to_all(returned.reshape(devices, rows, LANES), both, 0, 0, tiled=...  62.8 us
    all_to_all x1, blocking collectives, body(): lax.all_to_all(grams.reshape(devices, lines, 1, LANES), both, 0, 0, tiled...  15.9 us
    pallas_call x1, Pallas kernels, body(): pl.pallas_call(functools.partial(transform_kernel, modes=modes, row_devic...  9.94 us
    pallas_call x1, Pallas kernels, body(): pl.pallas_call(functools.partial(column_kernel, modes=modes, planes=plane...  5.92 us
    pallas_call x1, Pallas kernels, body(): pl.pallas_call(functools.partial(finish_kernel, devices=devices, vecs=vec...  4.15 us

profile of v7, /device:TPU:1, one launch (start us, length us, event | category | flops | bytes accessed | tf_op | source)
XLA Modules:
  0.0 175.4 jit_solution(1544113240169609866)
XLA Ops:
  0.6 0.0 copy-start
  0.6 2.3 %copy-done = f32[12,128,768]{2,1,0:T(8,128)S(1)} copy-done((f32[12,128,768]{2,1,0:T(8,128)S(1)}, f32[12,128,768]{2,1,0:T(8,128)}, u32[]{:S(2)}) %copy-start) | copy-done | bytes 4718616
  3.0 0.9 copy-done.1
  3.9 0.3 pack.1
  4.2 0.0 copy-start.6
  4.2 0.0 copy-start.7
  4.2 0.0 copy-start.8
  4.2 0.0 copy-start.9
  4.3 0.0 copy-start.10
  4.3 0.0 copy-start.11
  4.3 0.0 slice-start
  4.3 72.1 %all_to_all.15 = f32[128,75,1,128]{3,2,1,0:T(1,128)S(1)} all-to-all(f32[128,75,1,128]{3,2,1,0:T(1,128)S(1)} %bitcast.12), channel_id=1, replica_groups=mesh['row'=16,'col'=8] {'col','row'}, dimensions={0} | all-to-all | bytes 9830400 | tf_op jit(solution)/shard_map/all_to_all | solution.py:450
  76.4 0.0 copy-done.6
  76.4 0.0 copy-done.7
  76.4 0.0 copy-done.8
  76.4 0.0 copy-done.9
  76.4 0.0 copy-done.10
  76.5 0.0 copy-done.11
  76.5 0.0 slice-start.1
  76.5 9.9 %transform.1 = f32[9216,128]{1,0:T(8,128)S(1)} custom-call(f32[9600,128]{1,0:T(8,128)S(1)} %bitcast.13, bf16[576,256]{1,0:T(8,128)(2,1)S(1)} %copy-done.6, bf16[112,336]{1,0:T(8,128)(2,1)S(1)} %copy-done.8, bf16[96,288]{1,0:T(8,128)(2,1)S(1)} %copy-done.11, bf16[104,336]{1,0:T(8,128)(2,1)S(1)} %copy-done.9, bf16[96,288]{1,0:T(8,128)(2,1)S(1)} %copy-done.10, ...), custom_call_target="tpu_custom_call" | custom-call | flops 20000000000 | bytes 9437184 | tf_op jit(solution)/shard_map/transform/pallas_call | solution.py:454
  86.4 0.0 copy-start.2
  86.4 0.0 copy-start.3
  86.4 0.0 copy-start.4
  86.5 0.0 copy-start.5
  86.5 62.8 %all_to_all.16 = f32[128,72,128]{2,1,0:T(8,128)S(1)} all-to-all(f32[128,72,128]{2,1,0:T(8,128)S(1)} %bitcast.16), channel_id=1, replica_groups=mesh['row'=16,'col'=8] {'col','row'}, dimensions={0} | all-to-all | bytes 9437184 | tf_op jit(solution)/shard_map/all_to_all | solution.py:468
  149.3 0.0 slice-done
  149.3 0.0 slice-done.1
  149.3 0.0 copy-done.2
  149.3 0.0 copy-done.3
  149.4 5.9 %column.1 = (f32[1536,768]{1,0:T(8,128)S(1)}, f32[640,128]{1,0:T(8,128)S(1)}) custom-call(f32[9216,128]{1,0:T(8,128)S(1)} %bitcast.17, f32[12,128,768]{2,1,0:T(8,128)S(1)} %bitcast.15, s32[12,24]{1,0:T(8,128)S(1)} %copy-done.4, f32[1,128]{1,0:T(1,128)S(1)} %bitcast.21, f32[128,128]{1,0:T(8,128)S(1)} %copy-done.2, f32[128,128]{1,0:T(8,128)S(1)} %copy-done.3), custom_call_target="tpu_custom_call" | custom-call | flops 10000000000 | bytes 14155776 | tf_op jit(solution)/shard_map/column/pallas_call | solution.py:474
  155.3 15.9 %all_to_all.17 = f32[128,5,1,128]{3,2,1,0:T(1,128)S(1)} all-to-all(f32[128,5,1,128]{3,2,1,0:T(1,128)S(1)} %bitcast.19), channel_id=1, replica_groups=mesh['row'=16,'col'=8] {'col','row'}, dimensions={0} | all-to-all | bytes 655360 | tf_op jit(solution)/shard_map/all_to_all | solution.py:496
  171.2 4.1 %finish.1 = (f32[1536,768]{1,0:T(8,128)}, f32[1,32]{1,0:T(1,128)}) custom-call(f32[640,128]{1,0:T(8,128)S(1)} %bitcast.18, f32[1536,768]{1,0:T(8,128)S(1)} %get-tuple-element.7.stepped_ref), custom_call_target="tpu_custom_call" | custom-call | flops 603979776 | bytes 9437184 | tf_op jit(solution)/shard_map/finish/pallas_call | solution.py:501
  (4 shorter events, 0.0 us)
Async XLA Ops:
  0.6 2.3 %copy-start = (f32[12,128,768]{2,1,0:T(8,128)S(1)}, f32[12,128,768]{2,1,0:T(8,128)}, u32[]{:S(2)}) copy-start(f32[12,128,768]{2,1,0:T(8,128)} %q_ref.3) | copy-start | bytes 14155780
  3.0 0.9 copy-start.1
  4.2 72.2 %copy-start.6 = (bf16[576,256]{1,0:T(8,128)(2,1)S(1)}, bf16[576,256]{1,0:T(8,128)(2,1)}, u32[]{:S(2)}) copy-start(bf16[576,256]{1,0:T(8,128)(2,1)} %constant.12.clone.sx_ref) | copy-start | bytes 884740
  4.2 72.2 %copy-start.7 = (bf16[384,256]{1,0:T(8,128)(2,1)S(1)}, bf16[384,256]{1,0:T(8,128)(2,1)}, u32[]{:S(2)}) copy-start(bf16[384,256]{1,0:T(8,128)(2,1)} %constant.17.clone.g_ref) | copy-start | bytes 589828
  4.2 72.2 %copy-start.8 = (bf16[112,336]{1,0:T(8,128)(2,1)S(1)}, bf16[112,336]{1,0:T(8,128)(2,1)}, u32[]{:S(2)}) copy-start(bf16[112,336]{1,0:T(8,128)(2,1)} %constant.13.clone.even_p_ref) | copy-start | bytes 225796
  4.2 72.2 %copy-start.9 = (bf16[104,336]{1,0:T(8,128)(2,1)S(1)}, bf16[104,336]{1,0:T(8,128)(2,1)}, u32[]{:S(2)}) copy-start(bf16[104,336]{1,0:T(8,128)(2,1)} %constant.15.clone.even_m_ref) | copy-start | bytes 209668
  4.3 72.2 %copy-start.10 = (bf16[96,288]{1,0:T(8,128)(2,1)S(1)}, bf16[96,288]{1,0:T(8,128)(2,1)}, u32[]{:S(2)}) copy-start(bf16[96,288]{1,0:T(8,128)(2,1)} %constant.16.clone.odd_m_ref) | copy-start | bytes 165892
  4.3 72.2 %copy-start.11 = (bf16[96,288]{1,0:T(8,128)(2,1)S(1)}, bf16[96,288]{1,0:T(8,128)(2,1)}, u32[]{:S(2)}) copy-start(bf16[96,288]{1,0:T(8,128)(2,1)} %constant.14.clone.odd_p_ref) | copy-start | bytes 165892
  4.3 145.0 %slice-start = ((s8[4718592]{0:T(1024)(128)(4,1)}), s8[4194304]{0:T(1024)(128)(4,1)S(1)}, s32[]{:S(2)}) async-start(s8[4718592]{0:T(1024)(128)(4,1)} %bitcast.14), calls=%async_computation.3 | async-start | bytes 8388608
  76.5 72.8 %slice-start.1 = ((s8[4718592]{0:T(1024)(128)(4,1)}), s8[524288]{0:T(1024)(128)(4,1)S(1)}, s32[]{:S(2)}) async-start(s8[4718592]{0:T(1024)(128)(4,1)} %bitcast.14), calls=%async_computation.4 | async-start | bytes 1048576
  86.4 62.9 %copy-start.2 = (f32[128,128]{1,0:T(8,128)S(1)}, f32[128,128]{1,0:T(8,128)}, u32[]{:S(2)}) copy-start(f32[128,128]{1,0:T(8,128)} %to_ref.1) | copy-start | bytes 196612
  86.4 62.9 %copy-start.3 = (f32[128,128]{1,0:T(8,128)S(1)}, f32[128,128]{1,0:T(8,128)}, u32[]{:S(2)}) copy-start(f32[128,128]{1,0:T(8,128)} %from_ref.1) | copy-start | bytes 196612
  86.4 62.9 %copy-start.4 = (s32[12,24]{1,0:T(8,128)S(1)}, s32[12,24]{1,0:T(8,128)}, u32[]{:S(2)}) copy-start(s32[12,24]{1,0:T(8,128)} %mask_ref.1) | copy-start | bytes 3460
  86.5 62.9 %copy-start.5 = (f32[128]{0:T(128)S(1)}, f32[128]{0:T(128)}, u32[]{:S(2)}) copy-start(f32[128]{0:T(128)} %param.15) | copy-start | bytes 1540

commit v8 on v7

--- a/solution.py
+++ b/solution.py
@@ -105,7 +105,9 @@
     )
 
 
-def pack_kernel(q_ref, base_ref, out_ref, *, modes, planes, tiles, extra):
+def pack_kernel(base_ref, *refs, modes, planes, tiles, extra):
+    q_refs, out_ref = refs[:-1], refs[-1]
+    share = modes // len(q_refs)
     stride = modes * tiles + extra
     part = base_ref.shape[0] // extra
     fill = jnp.zeros((LANES - part, planes), F32)
@@ -114,8 +116,8 @@
         out_ref[pl.ds(modes * tiles + k, planes, stride=stride), :] = block.T
     for m in range(modes):
         for nb in range(tiles):
-            out_ref[pl.ds(nb * modes + m, planes, stride=stride), :] = q_ref[
-                m, :, nb * LANES : (nb + 1) * LANES
+            out_ref[pl.ds(nb * modes + m, planes, stride=stride), :] = q_refs[m // share][
+                m % share, :, nb * LANES : (nb + 1) * LANES
             ]
 
 
@@ -441,12 +443,12 @@
     packed = pl.pallas_call(
         functools.partial(pack_kernel, modes=modes, planes=planes, tiles=tiles, extra=extra),
         out_shape=jax.ShapeDtypeStruct((planes * (rows + extra), LANES), F32),
-        in_specs=[vmem()] * 2,
+        in_specs=[vmem()] * 3,
         out_specs=vmem(),
         cost_estimate=cost(10**9, 2 * size),
         compiler_params=small,
         name="pack",
-    )(tangents, base)
+    )(base, tangents[: modes // 2], tangents[modes // 2 :])
     received = lax.all_to_all(
         packed.reshape(devices, rows + extra, 1, LANES), both, 0, 0, tiled=True
     ).reshape(packed.shape)

time: 176 us -> 175 us (level)
    unnamed x28 -> x26, local copies, waits for them, and re-layouts: 3.32 us -> 0.09 us
    slice x0 -> x1, local copies, waits for them, and re-layouts: none -> 2.96 us  [body(): tangents[modes // 2:]]
where the time goes in v8:
time: 175 us
  blocking collectives  151 us (86%)
  Pallas kernels  20.4 us (12%)
  local copies, waits for them, and re-layouts  3.05 us (2%)
    all_to_all x1, blocking collectives, body(): lax.all_to_all(packed.reshape(devices, rows + extra, 1, LANES), both, 0,...  72.1 us
    all_to_all x1, blocking collectives, body(): lax.all_to_all(returned.reshape(devices, rows, LANES), both, 0, 0, tiled=...  62.8 us
    all_to_all x1, blocking collectives, body(): lax.all_to_all(grams.reshape(devices, lines, 1, LANES), both, 0, 0, tiled...  15.9 us
    pallas_call x1, Pallas kernels, body(): pl.pallas_call(functools.partial(transform_kernel, modes=modes, row_devic...  9.94 us
    pallas_call x1, Pallas kernels, body(): pl.pallas_call(functools.partial(column_kernel, modes=modes, planes=plane...  5.94 us
    pallas_call x1, Pallas kernels, body(): pl.pallas_call(functools.partial(finish_kernel, devices=devices, vecs=vec...  4.16 us

profile of v8, /device:TPU:1, one launch (start us, length us, event | category | flops | bytes accessed | tf_op | source)
XLA Modules:
  0.0 175.1 jit_solution(9758545146339245872)
XLA Ops:
  0.6 0.0 copy-start
  0.6 3.0 %fusion = (f32[6,128,768]{2,1,0:T(8,128)S(1)}, f32[6,128,768]{2,1,0:T(8,128)S(1)}) fusion(f32[12,128,768]{2,1,0:T(8,128)} %q_ref.1), kind=kLoop, calls=%fused_computation | loop fusion | bytes 9437184 | tf_op jit(solution)/shard_map/slice | solution.py:451
  3.6 0.0 copy-done
  3.6 0.3 pack.1
  3.9 0.0 copy-start.5
  4.0 0.0 copy-start.6
  4.0 0.0 copy-start.7
  4.0 0.0 copy-start.8
  4.0 0.0 copy-start.9
  4.0 0.0 copy-start.10
  4.0 0.0 slice-start
  4.0 72.1 %all_to_all.15 = f32[128,75,1,128]{3,2,1,0:T(1,128)S(1)} all-to-all(f32[128,75,1,128]{3,2,1,0:T(1,128)S(1)} %bitcast.12), channel_id=1, replica_groups=mesh['row'=16,'col'=8] {'col','row'}, dimensions={0} | all-to-all | bytes 9830400 | tf_op jit(solution)/shard_map/all_to_all | solution.py:452
  76.2 0.0 copy-done.5
  76.2 0.0 copy-done.6
  76.2 0.0 copy-done.7
  76.2 0.0 copy-done.8
  76.2 0.0 copy-done.9
  76.2 0.0 copy-done.10
  76.2 0.0 slice-start.1
  76.2 9.9 %transform.1 = f32[9216,128]{1,0:T(8,128)S(1)} custom-call(f32[9600,128]{1,0:T(8,128)S(1)} %bitcast.13, bf16[576,256]{1,0:T(8,128)(2,1)S(1)} %copy-done.5, bf16[112,336]{1,0:T(8,128)(2,1)S(1)} %copy-done.7, bf16[96,288]{1,0:T(8,128)(2,1)S(1)} %copy-done.10, bf16[104,336]{1,0:T(8,128)(2,1)S(1)} %copy-done.8, bf16[96,288]{1,0:T(8,128)(2,1)S(1)} %copy-done.9, ...), custom_call_target="tpu_custom_call" | custom-call | flops 20000000000 | bytes 9437184 | tf_op jit(solution)/shard_map/transform/pallas_call | solution.py:456
  86.2 0.0 copy-start.1
  86.2 0.0 copy-start.2
  86.2 0.0 copy-start.3
  86.2 0.0 copy-start.4
  86.2 62.8 %all_to_all.16 = f32[128,72,128]{2,1,0:T(8,128)S(1)} all-to-all(f32[128,72,128]{2,1,0:T(8,128)S(1)} %bitcast.16), channel_id=1, replica_groups=mesh['row'=16,'col'=8] {'col','row'}, dimensions={0} | all-to-all | bytes 9437184 | tf_op jit(solution)/shard_map/all_to_all | solution.py:470
  149.0 0.0 slice-done
  149.0 0.0 slice-done.1
  149.1 0.0 copy-done.1
  149.1 0.0 copy-done.2
  149.1 5.9 %column.1 = (f32[1536,768]{1,0:T(8,128)S(1)}, f32[640,128]{1,0:T(8,128)S(1)}) custom-call(f32[9216,128]{1,0:T(8,128)S(1)} %bitcast.17, f32[12,128,768]{2,1,0:T(8,128)S(1)} %bitcast.15, s32[12,24]{1,0:T(8,128)S(1)} %copy-done.3, f32[1,128]{1,0:T(1,128)S(1)} %bitcast.21, f32[128,128]{1,0:T(8,128)S(1)} %copy-done.1, f32[128,128]{1,0:T(8,128)S(1)} %copy-done.2), custom_call_target="tpu_custom_call" | custom-call | flops 10000000000 | bytes 14155776 | tf_op jit(solution)/shard_map/column/pallas_call | solution.py:476
  155.0 15.9 %all_to_all.17 = f32[128,5,1,128]{3,2,1,0:T(1,128)S(1)} all-to-all(f32[128,5,1,128]{3,2,1,0:T(1,128)S(1)} %bitcast.19), channel_id=1, replica_groups=mesh['row'=16,'col'=8] {'col','row'}, dimensions={0} | all-to-all | bytes 655360 | tf_op jit(solution)/shard_map/all_to_all | solution.py:498
  171.0 4.2 %finish.1 = (f32[1536,768]{1,0:T(8,128)}, f32[1,32]{1,0:T(1,128)}) custom-call(f32[640,128]{1,0:T(8,128)S(1)} %bitcast.18, f32[1536,768]{1,0:T(8,128)S(1)} %get-tuple-element.7.stepped_ref), custom_call_target="tpu_custom_call" | custom-call | flops 603979776 | bytes 9437184 | tf_op jit(solution)/shard_map/finish/pallas_call | solution.py:503
  (3 shorter events, 0.0 us)
Async XLA Ops:
  0.6 3.0 %copy-start = (f32[12,128,24]{1,2,0:T(8,128)S(1)}, f32[12,128,24]{1,2,0:T(8,128)}, u32[]{:S(2)}) copy-start(f32[12,128,24]{1,2,0:T(8,128)} %param.13) | copy-start | bytes 442372
  3.9 72.2 %copy-start.5 = (bf16[576,256]{1,0:T(8,128)(2,1)S(1)}, bf16[576,256]{1,0:T(8,128)(2,1)}, u32[]{:S(2)}) copy-start(bf16[576,256]{1,0:T(8,128)(2,1)} %constant.12.clone.sx_ref) | copy-start | bytes 884740
  4.0 72.2 %copy-start.6 = (bf16[384,256]{1,0:T(8,128)(2,1)S(1)}, bf16[384,256]{1,0:T(8,128)(2,1)}, u32[]{:S(2)}) copy-start(bf16[384,256]{1,0:T(8,128)(2,1)} %constant.17.clone.g_ref) | copy-start | bytes 589828
  4.0 72.2 %copy-start.7 = (bf16[112,336]{1,0:T(8,128)(2,1)S(1)}, bf16[112,336]{1,0:T(8,128)(2,1)}, u32[]{:S(2)}) copy-start(bf16[112,336]{1,0:T(8,128)(2,1)} %constant.13.clone.even_p_ref) | copy-start | bytes 225796
  4.0 72.2 %copy-start.8 = (bf16[104,336]{1,0:T(8,128)(2,1)S(1)}, bf16[104,336]{1,0:T(8,128)(2,1)}, u32[]{:S(2)}) copy-start(bf16[104,336]{1,0:T(8,128)(2,1)} %constant.15.clone.even_m_ref) | copy-start | bytes 209668
  4.0 72.2 %copy-start.9 = (bf16[96,288]{1,0:T(8,128)(2,1)S(1)}, bf16[96,288]{1,0:T(8,128)(2,1)}, u32[]{:S(2)}) copy-start(bf16[96,288]{1,0:T(8,128)(2,1)} %constant.16.clone.odd_m_ref) | copy-start | bytes 165892
  4.0 72.2 %copy-start.10 = (bf16[96,288]{1,0:T(8,128)(2,1)S(1)}, bf16[96,288]{1,0:T(8,128)(2,1)}, u32[]{:S(2)}) copy-start(bf16[96,288]{1,0:T(8,128)(2,1)} %constant.14.clone.odd_p_ref) | copy-start | bytes 165892
  4.0 145.0 %slice-start = ((s8[4718592]{0:T(1024)(128)(4,1)}), s8[4194304]{0:T(1024)(128)(4,1)S(1)}, s32[]{:S(2)}) async-start(s8[4718592]{0:T(1024)(128)(4,1)} %bitcast.14), calls=%async_computation.3 | async-start | bytes 8388608
  76.2 72.8 %slice-start.1 = ((s8[4718592]{0:T(1024)(128)(4,1)}), s8[524288]{0:T(1024)(128)(4,1)S(1)}, s32[]{:S(2)}) async-start(s8[4718592]{0:T(1024)(128)(4,1)} %bitcast.14), calls=%async_computation.4 | async-start | bytes 1048576
  86.2 62.9 %copy-start.1 = (f32[128,128]{1,0:T(8,128)S(1)}, f32[128,128]{1,0:T(8,128)}, u32[]{:S(2)}) copy-start(f32[128,128]{1,0:T(8,128)} %to_ref.1) | copy-start | bytes 196612
  86.2 62.9 %copy-start.2 = (f32[128,128]{1,0:T(8,128)S(1)}, f32[128,128]{1,0:T(8,128)}, u32[]{:S(2)}) copy-start(f32[128,128]{1,0:T(8,128)} %from_ref.1) | copy-start | bytes 196612
  86.2 62.9 %copy-start.3 = (s32[12,24]{1,0:T(8,128)S(1)}, s32[12,24]{1,0:T(8,128)}, u32[]{:S(2)}) copy-start(s32[12,24]{1,0:T(8,128)} %mask_ref.1) | copy-start | bytes 3460
  86.2 62.9 %copy-start.4 = (f32[128]{0:T(128)S(1)}, f32[128]{0:T(128)}, u32[]{:S(2)}) copy-start(f32[128]{0:T(128)} %param.15) | copy-start | bytes 1540

commit v9 on v8

--- a/solution.py
+++ b/solution.py
@@ -501,7 +501,7 @@
 
     block = height // 2
     vectors, growth = pl.pallas_call(
-        functools.partial(finish_kernel, devices=devices, vecs=vecs, panel=8),
+        functools.partial(finish_kernel, devices=devices, vecs=vecs, panel=16),
         out_shape=[
             jax.ShapeDtypeStruct((height, width), F32),
             jax.ShapeDtypeStruct((1, vecs), F32),

time: 175 us -> 175 us (level)
  no operation moved by 1% of the time
where the time goes in v9:
time: 175 us
  blocking collectives  151 us (86%)
  Pallas kernels  20.3 us (12%)
  local copies, waits for them, and re-layouts  3.05 us (2%)
    all_to_all x1, blocking collectives, body(): lax.all_to_all(packed.reshape(devices, rows + extra, 1, LANES), both, 0,...  72.1 us
    all_to_all x1, blocking collectives, body(): lax.all_to_all(returned.reshape(devices, rows, LANES), both, 0, 0, tiled=...  62.8 us
    all_to_all x1, blocking collectives, body(): lax.all_to_all(grams.reshape(devices, lines, 1, LANES), both, 0, 0, tiled...  15.9 us
    pallas_call x1, Pallas kernels, body(): pl.pallas_call(functools.partial(transform_kernel, modes=modes, row_devic...  9.94 us
    pallas_call x1, Pallas kernels, body(): pl.pallas_call(functools.partial(column_kernel, modes=modes, planes=plane...  5.94 us
    pallas_call x1, Pallas kernels, body(): pl.pallas_call(functools.partial(finish_kernel, devices=devices, vecs=vec...  4.06 us

profile of v9, /device:TPU:1, one launch (start us, length us, event | category | flops | bytes accessed | tf_op | source)
XLA Modules:
  0.0 175.0 jit_solution(35050026751995580)
XLA Ops:
  0.6 0.0 copy-start
  0.6 3.0 %fusion = (f32[6,128,768]{2,1,0:T(8,128)S(1)}, f32[6,128,768]{2,1,0:T(8,128)S(1)}) fusion(f32[12,128,768]{2,1,0:T(8,128)} %q_ref.1), kind=kLoop, calls=%fused_computation | loop fusion | bytes 9437184 | tf_op jit(solution)/shard_map/slice | solution.py:451
  3.6 0.0 copy-done
  3.6 0.3 pack.1
  3.9 0.0 copy-start.5
  4.0 0.0 copy-start.6
  4.0 0.0 copy-start.7
  4.0 0.0 copy-start.8
  4.0 0.0 copy-start.9
  4.0 0.0 copy-start.10
  4.0 0.0 slice-start
  4.0 72.1 %all_to_all.15 = f32[128,75,1,128]{3,2,1,0:T(1,128)S(1)} all-to-all(f32[128,75,1,128]{3,2,1,0:T(1,128)S(1)} %bitcast.12), channel_id=1, replica_groups=mesh['row'=16,'col'=8] {'col','row'}, dimensions={0} | all-to-all | bytes 9830400 | tf_op jit(solution)/shard_map/all_to_all | solution.py:452
  76.2 0.0 copy-done.5
  76.2 0.0 copy-done.6
  76.2 0.0 copy-done.7
  76.2 0.0 copy-done.8
  76.2 0.0 copy-done.9
  76.2 0.0 copy-done.10
  76.2 0.0 slice-start.1
  76.2 9.9 %transform.1 = f32[9216,128]{1,0:T(8,128)S(1)} custom-call(f32[9600,128]{1,0:T(8,128)S(1)} %bitcast.13, bf16[576,256]{1,0:T(8,128)(2,1)S(1)} %copy-done.5, bf16[112,336]{1,0:T(8,128)(2,1)S(1)} %copy-done.7, bf16[96,288]{1,0:T(8,128)(2,1)S(1)} %copy-done.10, bf16[104,336]{1,0:T(8,128)(2,1)S(1)} %copy-done.8, bf16[96,288]{1,0:T(8,128)(2,1)S(1)} %copy-done.9, ...), custom_call_target="tpu_custom_call" | custom-call | flops 20000000000 | bytes 9437184 | tf_op jit(solution)/shard_map/transform/pallas_call | solution.py:456
  86.2 0.0 copy-start.1
  86.2 0.0 copy-start.2
  86.2 0.0 copy-start.3
  86.2 0.0 copy-start.4
  86.2 62.8 %all_to_all.16 = f32[128,72,128]{2,1,0:T(8,128)S(1)} all-to-all(f32[128,72,128]{2,1,0:T(8,128)S(1)} %bitcast.16), channel_id=1, replica_groups=mesh['row'=16,'col'=8] {'col','row'}, dimensions={0} | all-to-all | bytes 9437184 | tf_op jit(solution)/shard_map/all_to_all | solution.py:470
  149.0 0.0 slice-done
  149.0 0.0 slice-done.1
  149.1 0.0 copy-done.1
  149.1 0.0 copy-done.2
  149.1 5.9 %column.1 = (f32[1536,768]{1,0:T(8,128)S(1)}, f32[640,128]{1,0:T(8,128)S(1)}) custom-call(f32[9216,128]{1,0:T(8,128)S(1)} %bitcast.17, f32[12,128,768]{2,1,0:T(8,128)S(1)} %bitcast.15, s32[12,24]{1,0:T(8,128)S(1)} %copy-done.3, f32[1,128]{1,0:T(1,128)S(1)} %bitcast.21, f32[128,128]{1,0:T(8,128)S(1)} %copy-done.1, f32[128,128]{1,0:T(8,128)S(1)} %copy-done.2), custom_call_target="tpu_custom_call" | custom-call | flops 10000000000 | bytes 14155776 | tf_op jit(solution)/shard_map/column/pallas_call | solution.py:476
  155.0 15.9 %all_to_all.17 = f32[128,5,1,128]{3,2,1,0:T(1,128)S(1)} all-to-all(f32[128,5,1,128]{3,2,1,0:T(1,128)S(1)} %bitcast.19), channel_id=1, replica_groups=mesh['row'=16,'col'=8] {'col','row'}, dimensions={0} | all-to-all | bytes 655360 | tf_op jit(solution)/shard_map/all_to_all | solution.py:498
  171.0 4.1 %finish.1 = (f32[1536,768]{1,0:T(8,128)}, f32[1,32]{1,0:T(1,128)}) custom-call(f32[640,128]{1,0:T(8,128)S(1)} %bitcast.18, f32[1536,768]{1,0:T(8,128)S(1)} %get-tuple-element.7.stepped_ref), custom_call_target="tpu_custom_call" | custom-call | flops 603979776 | bytes 9437184 | tf_op jit(solution)/shard_map/finish/pallas_call | solution.py:503
  (3 shorter events, 0.0 us)
Async XLA Ops:
  0.6 3.0 %copy-start = (f32[12,128,24]{1,2,0:T(8,128)S(1)}, f32[12,128,24]{1,2,0:T(8,128)}, u32[]{:S(2)}) copy-start(f32[12,128,24]{1,2,0:T(8,128)} %param.13) | copy-start | bytes 442372
  3.9 72.2 %copy-start.5 = (bf16[576,256]{1,0:T(8,128)(2,1)S(1)}, bf16[576,256]{1,0:T(8,128)(2,1)}, u32[]{:S(2)}) copy-start(bf16[576,256]{1,0:T(8,128)(2,1)} %constant.12.clone.sx_ref) | copy-start | bytes 884740
  4.0 72.2 %copy-start.6 = (bf16[384,256]{1,0:T(8,128)(2,1)S(1)}, bf16[384,256]{1,0:T(8,128)(2,1)}, u32[]{:S(2)}) copy-start(bf16[384,256]{1,0:T(8,128)(2,1)} %constant.17.clone.g_ref) | copy-start | bytes 589828
  4.0 72.2 %copy-start.7 = (bf16[112,336]{1,0:T(8,128)(2,1)S(1)}, bf16[112,336]{1,0:T(8,128)(2,1)}, u32[]{:S(2)}) copy-start(bf16[112,336]{1,0:T(8,128)(2,1)} %constant.13.clone.even_p_ref) | copy-start | bytes 225796
  4.0 72.2 %copy-start.8 = (bf16[104,336]{1,0:T(8,128)(2,1)S(1)}, bf16[104,336]{1,0:T(8,128)(2,1)}, u32[]{:S(2)}) copy-start(bf16[104,336]{1,0:T(8,128)(2,1)} %constant.15.clone.even_m_ref) | copy-start | bytes 209668
  4.0 72.2 %copy-start.9 = (bf16[96,288]{1,0:T(8,128)(2,1)S(1)}, bf16[96,288]{1,0:T(8,128)(2,1)}, u32[]{:S(2)}) copy-start(bf16[96,288]{1,0:T(8,128)(2,1)} %constant.16.clone.odd_m_ref) | copy-start | bytes 165892
  4.0 72.2 %copy-start.10 = (bf16[96,288]{1,0:T(8,128)(2,1)S(1)}, bf16[96,288]{1,0:T(8,128)(2,1)}, u32[]{:S(2)}) copy-start(bf16[96,288]{1,0:T(8,128)(2,1)} %constant.14.clone.odd_p_ref) | copy-start | bytes 165892
  4.0 145.0 %slice-start = ((s8[4718592]{0:T(1024)(128)(4,1)}), s8[4194304]{0:T(1024)(128)(4,1)S(1)}, s32[]{:S(2)}) async-start(s8[4718592]{0:T(1024)(128)(4,1)} %bitcast.14), calls=%async_computation.3 | async-start | bytes 8388608
  76.2 72.8 %slice-start.1 = ((s8[4718592]{0:T(1024)(128)(4,1)}), s8[524288]{0:T(1024)(128)(4,1)S(1)}, s32[]{:S(2)}) async-start(s8[4718592]{0:T(1024)(128)(4,1)} %bitcast.14), calls=%async_computation.4 | async-start | bytes 1048576
  86.2 62.9 %copy-start.1 = (f32[128,128]{1,0:T(8,128)S(1)}, f32[128,128]{1,0:T(8,128)}, u32[]{:S(2)}) copy-start(f32[128,128]{1,0:T(8,128)} %to_ref.1) | copy-start | bytes 196612
  86.2 62.9 %copy-start.2 = (f32[128,128]{1,0:T(8,128)S(1)}, f32[128,128]{1,0:T(8,128)}, u32[]{:S(2)}) copy-start(f32[128,128]{1,0:T(8,128)} %from_ref.1) | copy-start | bytes 196612
  86.2 62.9 %copy-start.3 = (s32[12,24]{1,0:T(8,128)S(1)}, s32[12,24]{1,0:T(8,128)}, u32[]{:S(2)}) copy-start(s32[12,24]{1,0:T(8,128)} %mask_ref.1) | copy-start | bytes 3460
  86.2 62.9 %copy-start.4 = (f32[128]{0:T(128)S(1)}, f32[128]{0:T(128)}, u32[]{:S(2)}) copy-start(f32[128]{0:T(128)} %param.15) | copy-start | bytes 1540

commit v10 on v8

--- a/solution.py
+++ b/solution.py
@@ -136,6 +136,26 @@
     z_length = z_count // col_devices
     pitch = y_refs[0].shape[0] // vecs
     per_tile = LANES // vecs
+
+    def forward_x(c, carry):
+        parts = []
+        for nb in range(tiles):
+            start = c * (row_devices * stride) + nb * modes
+            block = jnp.concatenate(
+                [d_ref[pl.ds(start + m, row_devices, stride=stride), :] for m in range(modes)],
+                axis=0,
+            )
+            block = jnp.concatenate(split(block), axis=0).T
+            parts.append(jnp.concatenate([block, block[:, :x_count]], axis=1))
+        mixed = dot(jnp.concatenate(parts, axis=0), sx_ref[...], NN)
+        for n in range(z_length):
+            for k, y_ref in enumerate(y_refs):
+                y_ref[pl.ds(c * z_length + n, vecs, stride=pitch), :] = mixed[
+                    n * vecs : (n + 1) * vecs, k * LANES : (k + 1) * LANES
+                ]
+        return carry
+
+    lax.fori_loop(0, col_devices, forward_x, 0, unroll=8)
 
     turned = []
     for k in range(extra):
@@ -158,26 +178,6 @@
     even, odd = to_parity_points(even_p_ref, odd_p_ref, dot3(split(base), sx, NN))
     speed_ref[:wide] = even
     speed_ref[wide:] = odd
-
-    def forward_x(c, carry):
-        parts = []
-        for nb in range(tiles):
-            start = c * (row_devices * stride) + nb * modes
-            block = jnp.concatenate(
-                [d_ref[pl.ds(start + m, row_devices, stride=stride), :] for m in range(modes)],
-                axis=0,
-            )
-            block = jnp.concatenate(split(block), axis=0).T
-            parts.append(jnp.concatenate([block, block[:, :x_count]], axis=1))
-        mixed = dot(jnp.concatenate(parts, axis=0), sx_ref[...], NN)
-        for n in range(z_length):
-            for k, y_ref in enumerate(y_refs):
-                y_ref[pl.ds(c * z_length + n, vecs, stride=pitch), :] = mixed[
-                    n * vecs : (n + 1) * vecs, k * LANES : (k + 1) * LANES
-                ]
-        return carry
-
-    lax.fori_loop(0, col_devices, forward_x, 0, unroll=8)
 
     y_low, y_high = y_refs
     z_low, z_high = z_refs

time: 175 us -> 175 us (level)
  no operation moved by 1% of the time
where the time goes in v10:
time: 175 us
  blocking collectives  151 us (86%)
  Pallas kernels  20.2 us (12%)
  local copies, waits for them, and re-layouts  3.05 us (2%)
    all_to_all x1, blocking collectives, body(): lax.all_to_all(packed.reshape(devices, rows + extra, 1, LANES), both, 0,...  72.1 us
    all_to_all x1, blocking collectives, body(): lax.all_to_all(returned.reshape(devices, rows, LANES), both, 0, 0, tiled=...  62.9 us
    all_to_all x1, blocking collectives, body(): lax.all_to_all(grams.reshape(devices, lines, 1, LANES), both, 0, 0, tiled...  15.9 us
    pallas_call x1, Pallas kernels, body(): pl.pallas_call(functools.partial(transform_kernel, modes=modes, row_devic...  9.76 us
    pallas_call x1, Pallas kernels, body(): pl.pallas_call(functools.partial(column_kernel, modes=modes, planes=plane...  5.95 us
    pallas_call x1, Pallas kernels, body(): pl.pallas_call(functools.partial(finish_kernel, devices=devices, vecs=vec...  4.15 us

profile of v10, /device:TPU:1, one launch (start us, length us, event | category | flops | bytes accessed | tf_op | source)
XLA Modules:
  0.0 175.0 jit_solution(11815762849174225372)
XLA Ops:
  0.6 0.0 copy-start
  0.6 3.0 %fusion = (f32[6,128,768]{2,1,0:T(8,128)S(1)}, f32[6,128,768]{2,1,0:T(8,128)S(1)}) fusion(f32[12,128,768]{2,1,0:T(8,128)} %q_ref.1), kind=kLoop, calls=%fused_computation | loop fusion | bytes 9437184 | tf_op jit(solution)/shard_map/slice | solution.py:451
  3.6 0.0 copy-done
  3.6 0.3 pack.1
  3.9 0.0 copy-start.5
  4.0 0.0 copy-start.6
  4.0 0.0 copy-start.7
  4.0 0.0 copy-start.8
  4.0 0.0 copy-start.9
  4.0 0.0 copy-start.10
  4.0 0.0 slice-start
  4.0 72.1 %all_to_all.15 = f32[128,75,1,128]{3,2,1,0:T(1,128)S(1)} all-to-all(f32[128,75,1,128]{3,2,1,0:T(1,128)S(1)} %bitcast.12), channel_id=1, replica_groups=mesh['row'=16,'col'=8] {'col','row'}, dimensions={0} | all-to-all | bytes 9830400 | tf_op jit(solution)/shard_map/all_to_all | solution.py:452
  76.2 0.0 copy-done.5
  76.2 0.0 copy-done.6
  76.2 0.0 copy-done.7
  76.2 0.0 copy-done.8
  76.2 0.0 copy-done.9
  76.2 0.0 copy-done.10
  76.2 0.0 slice-start.1
  76.2 9.8 %transform.1 = f32[9216,128]{1,0:T(8,128)S(1)} custom-call(f32[9600,128]{1,0:T(8,128)S(1)} %bitcast.13, bf16[576,256]{1,0:T(8,128)(2,1)S(1)} %copy-done.5, bf16[112,336]{1,0:T(8,128)(2,1)S(1)} %copy-done.7, bf16[96,288]{1,0:T(8,128)(2,1)S(1)} %copy-done.10, bf16[104,336]{1,0:T(8,128)(2,1)S(1)} %copy-done.8, bf16[96,288]{1,0:T(8,128)(2,1)S(1)} %copy-done.9, ...), custom_call_target="tpu_custom_call" | custom-call | flops 20000000000 | bytes 9437184 | tf_op jit(solution)/shard_map/transform/pallas_call | solution.py:456
  86.0 0.0 copy-start.1
  86.0 0.0 copy-start.2
  86.0 0.0 copy-start.3
  86.0 0.0 copy-start.4
  86.0 62.9 %all_to_all.16 = f32[128,72,128]{2,1,0:T(8,128)S(1)} all-to-all(f32[128,72,128]{2,1,0:T(8,128)S(1)} %bitcast.16), channel_id=1, replica_groups=mesh['row'=16,'col'=8] {'col','row'}, dimensions={0} | all-to-all | bytes 9437184 | tf_op jit(solution)/shard_map/all_to_all | solution.py:470
  148.9 0.0 copy-done.1
  148.9 0.0 copy-done.2
  148.9 0.0 copy-done.3
  148.9 0.0 copy-done.4
  148.9 5.9 %column.1 = (f32[1536,768]{1,0:T(8,128)S(1)}, f32[640,128]{1,0:T(8,128)S(1)}) custom-call(f32[9216,128]{1,0:T(8,128)S(1)} %bitcast.17, f32[12,128,768]{2,1,0:T(8,128)S(1)} %bitcast.15, s32[12,24]{1,0:T(8,128)S(1)} %copy-done.3, f32[1,128]{1,0:T(1,128)S(1)} %bitcast.21, f32[128,128]{1,0:T(8,128)S(1)} %copy-done.1, f32[128,128]{1,0:T(8,128)S(1)} %copy-done.2), custom_call_target="tpu_custom_call" | custom-call | flops 10000000000 | bytes 14155776 | tf_op jit(solution)/shard_map/column/pallas_call | solution.py:476
  154.9 15.9 %all_to_all.17 = f32[128,5,1,128]{3,2,1,0:T(1,128)S(1)} all-to-all(f32[128,5,1,128]{3,2,1,0:T(1,128)S(1)} %bitcast.19), channel_id=1, replica_groups=mesh['row'=16,'col'=8] {'col','row'}, dimensions={0} | all-to-all | bytes 655360 | tf_op jit(solution)/shard_map/all_to_all | solution.py:498
  170.8 4.2 %finish.1 = (f32[1536,768]{1,0:T(8,128)}, f32[1,32]{1,0:T(1,128)}) custom-call(f32[640,128]{1,0:T(8,128)S(1)} %bitcast.18, f32[1536,768]{1,0:T(8,128)S(1)} %get-tuple-element.7.stepped_ref), custom_call_target="tpu_custom_call" | custom-call | flops 603979776 | bytes 9437184 | tf_op jit(solution)/shard_map/finish/pallas_call | solution.py:503
  (3 shorter events, 0.0 us)
Async XLA Ops:
  0.6 3.0 %copy-start = (f32[12,128,24]{1,2,0:T(8,128)S(1)}, f32[12,128,24]{1,2,0:T(8,128)}, u32[]{:S(2)}) copy-start(f32[12,128,24]{1,2,0:T(8,128)} %param.13) | copy-start | bytes 442372
  3.9 72.2 %copy-start.5 = (bf16[576,256]{1,0:T(8,128)(2,1)S(1)}, bf16[576,256]{1,0:T(8,128)(2,1)}, u32[]{:S(2)}) copy-start(bf16[576,256]{1,0:T(8,128)(2,1)} %constant.12.clone.sx_ref) | copy-start | bytes 884740
  4.0 72.2 %copy-start.6 = (bf16[384,256]{1,0:T(8,128)(2,1)S(1)}, bf16[384,256]{1,0:T(8,128)(2,1)}, u32[]{:S(2)}) copy-start(bf16[384,256]{1,0:T(8,128)(2,1)} %constant.17.clone.g_ref) | copy-start | bytes 589828
  4.0 72.2 %copy-start.7 = (bf16[112,336]{1,0:T(8,128)(2,1)S(1)}, bf16[112,336]{1,0:T(8,128)(2,1)}, u32[]{:S(2)}) copy-start(bf16[112,336]{1,0:T(8,128)(2,1)} %constant.13.clone.even_p_ref) | copy-start | bytes 225796
  4.0 72.2 %copy-start.8 = (bf16[104,336]{1,0:T(8,128)(2,1)S(1)}, bf16[104,336]{1,0:T(8,128)(2,1)}, u32[]{:S(2)}) copy-start(bf16[104,336]{1,0:T(8,128)(2,1)} %constant.15.clone.even_m_ref) | copy-start | bytes 209668
  4.0 72.2 %copy-start.9 = (bf16[96,288]{1,0:T(8,128)(2,1)S(1)}, bf16[96,288]{1,0:T(8,128)(2,1)}, u32[]{:S(2)}) copy-start(bf16[96,288]{1,0:T(8,128)(2,1)} %constant.16.clone.odd_m_ref) | copy-start | bytes 165892
  4.0 72.2 %copy-start.10 = (bf16[96,288]{1,0:T(8,128)(2,1)S(1)}, bf16[96,288]{1,0:T(8,128)(2,1)}, u32[]{:S(2)}) copy-start(bf16[96,288]{1,0:T(8,128)(2,1)} %constant.14.clone.odd_p_ref) | copy-start | bytes 165892
  4.0 144.9 %slice-start = ((s8[4718592]{0:T(1024)(128)(4,1)}), s8[4194304]{0:T(1024)(128)(4,1)S(1)}, s32[]{:S(2)}) async-start(s8[4718592]{0:T(1024)(128)(4,1)} %bitcast.14), calls=%async_computation.3 | async-start | bytes 8388608
  76.2 72.7 %slice-start.1 = ((s8[4718592]{0:T(1024)(128)(4,1)}), s8[524288]{0:T(1024)(128)(4,1)S(1)}, s32[]{:S(2)}) async-start(s8[4718592]{0:T(1024)(128)(4,1)} %bitcast.14), calls=%async_computation.4 | async-start | bytes 1048576
  86.0 62.9 %copy-start.1 = (f32[128,128]{1,0:T(8,128)S(1)}, f32[128,128]{1,0:T(8,128)}, u32[]{:S(2)}) copy-start(f32[128,128]{1,0:T(8,128)} %to_ref.1) | copy-start | bytes 196612
  86.0 62.9 %copy-start.2 = (f32[128,128]{1,0:T(8,128)S(1)}, f32[128,128]{1,0:T(8,128)}, u32[]{:S(2)}) copy-start(f32[128,128]{1,0:T(8,128)} %from_ref.1) | copy-start | bytes 196612
  86.0 62.9 %copy-start.3 = (s32[12,24]{1,0:T(8,128)S(1)}, s32[12,24]{1,0:T(8,128)}, u32[]{:S(2)}) copy-start(s32[12,24]{1,0:T(8,128)} %mask_ref.1) | copy-start | bytes 3460
  86.0 62.9 %copy-start.4 = (f32[128]{0:T(128)S(1)}, f32[128]{0:T(128)}, u32[]{:S(2)}) copy-start(f32[128]{0:T(128)} %param.15) | copy-start | bytes 1540

commit v11 on v10

--- a/solution.py
+++ b/solution.py
@@ -501,7 +501,7 @@
 
     block = height // 2
     vectors, growth = pl.pallas_call(
-        functools.partial(finish_kernel, devices=devices, vecs=vecs, panel=8),
+        functools.partial(finish_kernel, devices=devices, vecs=vecs, panel=16),
         out_shape=[
             jax.ShapeDtypeStruct((height, width), F32),
             jax.ShapeDtypeStruct((1, vecs), F32),

time: 175 us -> 175 us (level)
  no operation moved by 1% of the time
where the time goes in v11:
time: 175 us
  blocking collectives  151 us (86%)
  Pallas kernels  20.1 us (11%)
  local copies, waits for them, and re-layouts  3.05 us (2%)
    all_to_all x1, blocking collectives, body(): lax.all_to_all(packed.reshape(devices, rows + extra, 1, LANES), both, 0,...  72.1 us
    all_to_all x1, blocking collectives, body(): lax.all_to_all(returned.reshape(devices, rows, LANES), both, 0, 0, tiled=...  62.9 us
    all_to_all x1, blocking collectives, body(): lax.all_to_all(grams.reshape(devices, lines, 1, LANES), both, 0, 0, tiled...  15.9 us
    pallas_call x1, Pallas kernels, body(): pl.pallas_call(functools.partial(transform_kernel, modes=modes, row_devic...  9.76 us
    pallas_call x1, Pallas kernels, body(): pl.pallas_call(functools.partial(column_kernel, modes=modes, planes=plane...  5.95 us
    pallas_call x1, Pallas kernels, body(): pl.pallas_call(functools.partial(finish_kernel, devices=devices, vecs=vec...  4.05 us

profile of v11, /device:TPU:1, one launch (start us, length us, event | category | flops | bytes accessed | tf_op | source)
XLA Modules:
  0.0 174.9 jit_solution(14596344053317199594)
XLA Ops:
  0.6 0.0 copy-start
  0.6 3.0 %fusion = (f32[6,128,768]{2,1,0:T(8,128)S(1)}, f32[6,128,768]{2,1,0:T(8,128)S(1)}) fusion(f32[12,128,768]{2,1,0:T(8,128)} %q_ref.1), kind=kLoop, calls=%fused_computation | loop fusion | bytes 9437184 | tf_op jit(solution)/shard_map/slice | solution.py:451
  3.6 0.0 copy-done
  3.6 0.3 pack.1
  3.9 0.0 copy-start.5
  4.0 0.0 copy-start.6
  4.0 0.0 copy-start.7
  4.0 0.0 copy-start.8
  4.0 0.0 copy-start.9
  4.0 0.0 copy-start.10
  4.0 0.0 slice-start
  4.0 72.1 %all_to_all.15 = f32[128,75,1,128]{3,2,1,0:T(1,128)S(1)} all-to-all(f32[128,75,1,128]{3,2,1,0:T(1,128)S(1)} %bitcast.12), channel_id=1, replica_groups=mesh['row'=16,'col'=8] {'col','row'}, dimensions={0} | all-to-all | bytes 9830400 | tf_op jit(solution)/shard_map/all_to_all | solution.py:452
  76.2 0.0 copy-done.5
  76.2 0.0 copy-done.6
  76.2 0.0 copy-done.7
  76.2 0.0 copy-done.8
  76.2 0.0 copy-done.9
  76.2 0.0 copy-done.10
  76.2 0.0 slice-start.1
  76.2 9.8 %transform.1 = f32[9216,128]{1,0:T(8,128)S(1)} custom-call(f32[9600,128]{1,0:T(8,128)S(1)} %bitcast.13, bf16[576,256]{1,0:T(8,128)(2,1)S(1)} %copy-done.5, bf16[112,336]{1,0:T(8,128)(2,1)S(1)} %copy-done.7, bf16[96,288]{1,0:T(8,128)(2,1)S(1)} %copy-done.10, bf16[104,336]{1,0:T(8,128)(2,1)S(1)} %copy-done.8, bf16[96,288]{1,0:T(8,128)(2,1)S(1)} %copy-done.9, ...), custom_call_target="tpu_custom_call" | custom-call | flops 20000000000 | bytes 9437184 | tf_op jit(solution)/shard_map/transform/pallas_call | solution.py:456
  86.0 0.0 copy-start.1
  86.0 0.0 copy-start.2
  86.0 0.0 copy-start.3
  86.0 0.0 copy-start.4
  86.0 62.9 %all_to_all.16 = f32[128,72,128]{2,1,0:T(8,128)S(1)} all-to-all(f32[128,72,128]{2,1,0:T(8,128)S(1)} %bitcast.16), channel_id=1, replica_groups=mesh['row'=16,'col'=8] {'col','row'}, dimensions={0} | all-to-all | bytes 9437184 | tf_op jit(solution)/shard_map/all_to_all | solution.py:470
  148.9 0.0 copy-done.1
  148.9 0.0 copy-done.2
  148.9 0.0 copy-done.3
  148.9 0.0 copy-done.4
  148.9 5.9 %column.1 = (f32[1536,768]{1,0:T(8,128)S(1)}, f32[640,128]{1,0:T(8,128)S(1)}) custom-call(f32[9216,128]{1,0:T(8,128)S(1)} %bitcast.17, f32[12,128,768]{2,1,0:T(8,128)S(1)} %bitcast.15, s32[12,24]{1,0:T(8,128)S(1)} %copy-done.3, f32[1,128]{1,0:T(1,128)S(1)} %bitcast.21, f32[128,128]{1,0:T(8,128)S(1)} %copy-done.1, f32[128,128]{1,0:T(8,128)S(1)} %copy-done.2), custom_call_target="tpu_custom_call" | custom-call | flops 10000000000 | bytes 14155776 | tf_op jit(solution)/shard_map/column/pallas_call | solution.py:476
  154.9 15.9 %all_to_all.17 = f32[128,5,1,128]{3,2,1,0:T(1,128)S(1)} all-to-all(f32[128,5,1,128]{3,2,1,0:T(1,128)S(1)} %bitcast.19), channel_id=1, replica_groups=mesh['row'=16,'col'=8] {'col','row'}, dimensions={0} | all-to-all | bytes 655360 | tf_op jit(solution)/shard_map/all_to_all | solution.py:498
  170.8 4.1 %finish.1 = (f32[1536,768]{1,0:T(8,128)}, f32[1,32]{1,0:T(1,128)}) custom-call(f32[640,128]{1,0:T(8,128)S(1)} %bitcast.18, f32[1536,768]{1,0:T(8,128)S(1)} %get-tuple-element.7.stepped_ref), custom_call_target="tpu_custom_call" | custom-call | flops 603979776 | bytes 9437184 | tf_op jit(solution)/shard_map/finish/pallas_call | solution.py:503
  (3 shorter events, 0.0 us)
Async XLA Ops:
  0.6 3.0 %copy-start = (f32[12,128,24]{1,2,0:T(8,128)S(1)}, f32[12,128,24]{1,2,0:T(8,128)}, u32[]{:S(2)}) copy-start(f32[12,128,24]{1,2,0:T(8,128)} %param.13) | copy-start | bytes 442372
  3.9 72.2 %copy-start.5 = (bf16[576,256]{1,0:T(8,128)(2,1)S(1)}, bf16[576,256]{1,0:T(8,128)(2,1)}, u32[]{:S(2)}) copy-start(bf16[576,256]{1,0:T(8,128)(2,1)} %constant.12.clone.sx_ref) | copy-start | bytes 884740
  4.0 72.2 %copy-start.6 = (bf16[384,256]{1,0:T(8,128)(2,1)S(1)}, bf16[384,256]{1,0:T(8,128)(2,1)}, u32[]{:S(2)}) copy-start(bf16[384,256]{1,0:T(8,128)(2,1)} %constant.17.clone.g_ref) | copy-start | bytes 589828
  4.0 72.2 %copy-start.7 = (bf16[112,336]{1,0:T(8,128)(2,1)S(1)}, bf16[112,336]{1,0:T(8,128)(2,1)}, u32[]{:S(2)}) copy-start(bf16[112,336]{1,0:T(8,128)(2,1)} %constant.13.clone.even_p_ref) | copy-start | bytes 225796
  4.0 72.2 %copy-start.8 = (bf16[104,336]{1,0:T(8,128)(2,1)S(1)}, bf16[104,336]{1,0:T(8,128)(2,1)}, u32[]{:S(2)}) copy-start(bf16[104,336]{1,0:T(8,128)(2,1)} %constant.15.clone.even_m_ref) | copy-start | bytes 209668
  4.0 72.2 %copy-start.9 = (bf16[96,288]{1,0:T(8,128)(2,1)S(1)}, bf16[96,288]{1,0:T(8,128)(2,1)}, u32[]{:S(2)}) copy-start(bf16[96,288]{1,0:T(8,128)(2,1)} %constant.16.clone.odd_m_ref) | copy-start | bytes 165892
  4.0 72.2 %copy-start.10 = (bf16[96,288]{1,0:T(8,128)(2,1)S(1)}, bf16[96,288]{1,0:T(8,128)(2,1)}, u32[]{:S(2)}) copy-start(bf16[96,288]{1,0:T(8,128)(2,1)} %constant.14.clone.odd_p_ref) | copy-start | bytes 165892
  4.0 144.9 %slice-start = ((s8[4718592]{0:T(1024)(128)(4,1)}), s8[4194304]{0:T(1024)(128)(4,1)S(1)}, s32[]{:S(2)}) async-start(s8[4718592]{0:T(1024)(128)(4,1)} %bitcast.14), calls=%async_computation.3 | async-start | bytes 8388608
  76.2 72.7 %slice-start.1 = ((s8[4718592]{0:T(1024)(128)(4,1)}), s8[524288]{0:T(1024)(128)(4,1)S(1)}, s32[]{:S(2)}) async-start(s8[4718592]{0:T(1024)(128)(4,1)} %bitcast.14), calls=%async_computation.4 | async-start | bytes 1048576
  86.0 62.9 %copy-start.1 = (f32[128,128]{1,0:T(8,128)S(1)}, f32[128,128]{1,0:T(8,128)}, u32[]{:S(2)}) copy-start(f32[128,128]{1,0:T(8,128)} %to_ref.1) | copy-start | bytes 196612
  86.0 62.9 %copy-start.2 = (f32[128,128]{1,0:T(8,128)S(1)}, f32[128,128]{1,0:T(8,128)}, u32[]{:S(2)}) copy-start(f32[128,128]{1,0:T(8,128)} %from_ref.1) | copy-start | bytes 196612
  86.0 62.9 %copy-start.3 = (s32[12,24]{1,0:T(8,128)S(1)}, s32[12,24]{1,0:T(8,128)}, u32[]{:S(2)}) copy-start(s32[12,24]{1,0:T(8,128)} %mask_ref.1) | copy-start | bytes 3460
  86.0 62.9 %copy-start.4 = (f32[128]{0:T(128)S(1)}, f32[128]{0:T(128)}, u32[]{:S(2)}) copy-start(f32[128]{0:T(128)} %param.15) | copy-start | bytes 1540
